TPU v7x, 512 devices: a whole 4x4x16 slice. The times are simulated.
512 devices in a mesh: blk: 32 (over y, z_lo, core), replica: 16 (over z_hi, x).
Axes of the slice: x: 4, y: 4, z: 16 (z_hi: 4, z_lo: 4; z = z_hi * 4 + z_lo), core: 2. Of those that a mesh axis runs over, the one named last changes fastest.
Arguments:
- tokens: bfloat16 [640, 4096], P('blk', 'replica'), may hold values from -6 to 6
- cotangent: bfloat16 [640, 4096], P('blk', 'replica'), may hold values from -6 to 6
- gate_weight: bfloat16 [4096, 28672], P('replica', 'blk'), may hold values from -36 to 36, as said below
- up_weight: bfloat16 [4096, 28672], P('replica', 'blk'), may hold values from -36 to 36, as said below
- down_weight: bfloat16 [28672, 4096], P('blk', 'replica'), may hold values from -72 to 72, as said below
- gate_gain: float32 [28672], P('blk'), may hold values from 0.25 to 1.75
- up_gain: float32 [28672], P('blk'), may hold values from 0.25 to 1.75
- down_gain: float32 [4096], P('replica'), may hold values from 0.25 to 1.75
Outputs:
- grad_tokens: float32 [640, 4096], P('blk', 'replica')
- grad_gate: float32 [4096, 28672], P('replica', 'blk')
- grad_up: float32 [4096, 28672], P('replica', 'blk')
- grad_down: float32 [28672, 4096], P('blk', 'replica')
- grad_gate_gain: float32 [28672], P('blk')
- grad_up_gain: float32 [28672], P('blk')
- grad_down_gain: float32 [4096], P('replica')
Inputs may be any that keep to these rules, and one draw needn't show every extreme that they name: `gate_weight`: real-valued raw weights. `up_weight`: real-valued raw weights. `down_weight`: real-valued raw weights.
All inputs are finite; a program needn't handle non-finite values.
Results may differ from a plain program's by a relative error of at most 0.033.
Values may be sent and summed in bfloat16 or wider, within the bound.
No kernel may reach another device: no remote copies, remote signals or barrier semaphores. Data moves between devices by JAX's collectives and lax.ppermute only.
A program may use at most 64 MiB of HBM per device.

v0:
```python
import jax
import jax.numpy as jnp
from jax import lax
from jax.sharding import PartitionSpec as P

epsilon = 0.0001
branch_scale = 0.5


def sent_to_all(x, axis):
    copies = jnp.broadcast_to(x, (lax.axis_size(axis), *x.shape))
    return lax.all_to_all(copies, axis, split_axis=0, concat_axis=0, tiled=True)


def of_everyone(x, axis):
    return sent_to_all(x, axis).sum(axis=0)


def in_one(arrays, axis):
    ends = [0]
    for a in arrays:
        ends.append(ends[-1] + a.size)
    subtotal = of_everyone(jnp.concatenate([a.ravel() for a in arrays]), axis)
    return tuple((subtotal[b:e].reshape(a.shape) for a, b, e in zip(arrays, ends, ends[1:])))


def sent_together(arrays, axis, dim, along):
    both = jnp.concatenate(arrays, axis=along)
    result, at, done = (lax.all_gather(both, axis, axis=dim, tiled=True), 0, [])
    for a in arrays:
        done.append(lax.slice_in_dim(result, at, at + a.shape[along], axis=along))
        at += a.shape[along]
    return tuple(done)


def split_up(x, dim, devices):
    before, after = (x.shape[:dim], x.shape[dim + 1 :])
    return jnp.moveaxis(x.reshape(*before, devices, -1, *after), dim, 0)


def sum_at_owner(x, axis, dim):
    parts = split_up(x, dim, lax.axis_size(axis))
    arrived = lax.all_to_all(parts, axis, split_axis=0, concat_axis=0, tiled=True)
    return arrived.astype(jnp.float32).sum(axis=0)


def contract_first(left, right):
    return lax.dot_general(
        left, right, (((0,), (0,)), ((), ())), preferred_element_type=jnp.float32
    )


def contract_last(left, right):
    return lax.dot_general(
        left, right, (((1,), (1,)), ((), ())), preferred_element_type=jnp.float32
    )


def weight_grad(grad_hat, gain, cent, scale, summed, crossed, count):
    grad = scale * (gain * grad_hat - gain * summed / count) - scale * scale * scale * cent * (
        gain * crossed
    )
    return (grad, scale * crossed)


def gating(gate, up, dhidden):
    act = jax.nn.silu(gate)
    hidden = (act * up).astype(jnp.bfloat16)
    sig = jax.nn.sigmoid(gate)
    d_gate = (dhidden * up * sig * (1.0 + gate * (1.0 - sig))).astype(jnp.bfloat16)
    d_up = (dhidden * act).astype(jnp.bfloat16)
    return (d_gate, d_up, hidden)


def local(tokens, cotangent, gate_weight, up_weight, down_weight, gate_gain, up_gain, down_gain):
    width_all = gate_weight.shape[0] * lax.axis_size("replica")
    hidden_all = down_weight.shape[0] * lax.axis_size("blk")
    gate_raw = gate_weight.astype(jnp.float32)
    up_raw = up_weight.astype(jnp.float32)
    down_raw = down_weight.astype(jnp.float32)
    gate_sum, gate_power, up_sum, up_power = in_one(
        (
            jnp.sum(gate_raw, axis=0),
            jnp.sum(gate_raw * gate_raw, axis=0),
            jnp.sum(up_raw, axis=0),
            jnp.sum(up_raw * up_raw, axis=0),
        ),
        "replica",
    )
    gate_mean = gate_sum / width_all
    up_mean = up_sum / width_all
    gate_cent = gate_raw - gate_mean
    up_cent = up_raw - up_mean
    gate_square = gate_power - gate_sum * gate_mean
    up_square = up_power - up_sum * up_mean
    down_sum, down_power = in_one(
        (jnp.sum(down_raw, axis=0), jnp.sum(down_raw * down_raw, axis=0)), "blk"
    )
    down_mean = down_sum / hidden_all
    down_cent = down_raw - down_mean
    down_square = down_power - down_sum * down_mean
    gate_scale = lax.rsqrt(gate_square + epsilon)
    up_scale = lax.rsqrt(up_square + epsilon)
    down_scale = lax.rsqrt(down_square + epsilon)
    gate_hat = (gate_gain * gate_cent * gate_scale).astype(jnp.bfloat16)
    up_hat = (up_gain * up_cent * up_scale).astype(jnp.bfloat16)
    down_hat = (down_gain * down_cent * down_scale).astype(jnp.bfloat16)
    scaled = (branch_scale * cotangent.astype(jnp.float32)).astype(jnp.bfloat16)
    whole_tokens, whole_scaled = sent_together((tokens, scaled), "blk", 0, 1)
    gate_part = jnp.dot(whole_tokens, gate_hat, preferred_element_type=jnp.float32).astype(
        jnp.bfloat16
    )
    up_part = jnp.dot(whole_tokens, up_hat, preferred_element_type=jnp.float32).astype(jnp.bfloat16)
    down_part = contract_last(whole_scaled, down_hat).astype(jnp.bfloat16)
    gate, up, dhidden = (
        lax.psum(gate_part, "replica").astype(jnp.float32),
        lax.psum(up_part, "replica").astype(jnp.float32),
        lax.psum(down_part, "replica").astype(jnp.float32),
    )
    d_gate, d_up, hidden = gating(gate, up, dhidden)
    share = sum_at_owner(
        (contract_last(d_gate, gate_hat) + contract_last(d_up, up_hat)).astype(jnp.bfloat16),
        "blk",
        0,
    )
    grad_tokens = cotangent.astype(jnp.float32) + share
    p_gate = contract_first(whole_tokens, d_gate)
    p_up = contract_first(whole_tokens, d_up)
    p_down = contract_first(hidden, whole_scaled)
    gate_psum, gate_pcross, up_psum, up_pcross = in_one(
        (
            jnp.sum(p_gate, axis=0),
            jnp.sum(p_gate * gate_cent, axis=0),
            jnp.sum(p_up, axis=0),
            jnp.sum(p_up * up_cent, axis=0),
        ),
        "replica",
    )
    down_psum, down_pcross = in_one(
        (jnp.sum(p_down, axis=0), jnp.sum(p_down * down_cent, axis=0)), "blk"
    )
    grad_gate, grad_gate_gain = weight_grad(
        p_gate, gate_gain, gate_cent, gate_scale, gate_psum, gate_pcross, width_all
    )
    grad_up, grad_up_gain = weight_grad(
        p_up, up_gain, up_cent, up_scale, up_psum, up_pcross, width_all
    )
    grad_down, grad_down_gain = weight_grad(
        p_down, down_gain, down_cent, down_scale, down_psum, down_pcross, hidden_all
    )
    return (
        grad_tokens,
        grad_gate,
        grad_up,
        grad_down,
        grad_gate_gain,
        grad_up_gain,
        grad_down_gain,
    )


def solution(mesh):
    return jax.shard_map(
        local,
        mesh=mesh,
        in_specs=(
            P("blk", "replica"),
            P("blk", "replica"),
            P("replica", "blk"),
            P("replica", "blk"),
            P("blk", "replica"),
            P("blk"),
            P("blk"),
            P("replica"),
        ),
        out_specs=(
            P("blk", "replica"),
            P("replica", "blk"),
            P("replica", "blk"),
            P("blk", "replica"),
            P("blk"),
            P("blk"),
            P("replica"),
        ),
        check_vma=False,
    )
```

profile of v0, /device:TPU:1, one launch (start us, length us, event | category | flops | bytes accessed | tf_op | source)
XLA Modules:
  0.0 533.1 jit_solution(5313933197506070054)
XLA Ops:
  7.2 1.2 convert_reduce_fusion.2
  8.4 0.7 broadcast_in_dim.8
  9.1 10.3 %all-to-all-start = ((f32[32,1,512]{2,1,0:T(1,128)}), f32[32,1,512]{2,1,0:T(1,128)S(1)}, u32[]{:S(2)}, u32[]{:S(2)}) async-start(f32[32,1,512]{2,1,0:T(1,128)} %broadcast_in_dim.8), calls=%async_computation | async-start | bytes 131072 | tf_op jit(solution)/shard_map/all_to_all | solution.py:12
  19.4 1.4 convert_reduce_fusion
  20.9 6.4 %all-to-all-done = f32[32,1,512]{2,1,0:T(1,128)S(1)} async-done(((f32[32,1,512]{2,1,0:T(1,128)}), f32[32,1,512]{2,1,0:T(1,128)S(1)}, u32[]{:S(2)}, u32[]{:S(2)}) %all-to-all-start) | async-done | bytes 65568 | tf_op jit(solution)/shard_map/all_to_all | solution.py:12
  27.3 0.8 broadcast_in_dim.9
  28.1 14.4 %all-to-all-start.1 = ((f32[16,1,3584]{2,1,0:T(1,128)}), f32[16,1,3584]{2,1,0:T(1,128)S(1)}, u32[]{:S(2)}, u32[]{:S(2)}) async-start(f32[16,1,3584]{2,1,0:T(1,128)} %broadcast_in_dim.9), calls=%async_computation.1 | async-start | bytes 458752 | tf_op jit(solution)/shard_map/all_to_all | solution.py:12
  42.6 46.4 %all-gather = bf16[32,20,512]{2,1,0:T(8,128)(2,1)S(1)} all-gather(bf16[1,20,512]{2,1,0:T(8,128)(2,1)S(1)} %maximum_bitcast_fusion), channel_id=1, replica_groups=mesh['blk'=32,'replica'=16] {'blk'}, dimensions={0}, use_global_device_ids=true | all-gather | bytes 675840 | tf_op jit(solution)/shard_map/all_gather | solution.py:29
  89.2 0.7 multiply_multiply_fusion.2
  89.9 1.6 convolution_convert_fusion.2
  92.3 1.6 convolution_convert_fusion
  93.9 1.6 convolution_convert_fusion.1
  95.5 358.5 %all-reduce.3.cloned.1.call-done = (bf16[640,896]{1,0:T(8,128)(2,1)}, bf16[640,896]{1,0:T(8,128)(2,1)}, bf16[640,896]{1,0:T(8,128)(2,1)}) async-done(((bf16[640,896]{1,0:T(8,128)(2,1)}, bf16[640,896]{1,0:T(8,128)(2,1)}, bf16[640,896]{1,0:T(8,128)(2,1)}), (bf16[640,896]{1,0:T(8,128)(2,1)}, bf16[640,896]{1,0:T(8,128)(2,1)}, bf16[640,896]{1,0:T(8,128)(2,1)})) %all-reduce.3.cloned.1.call-update) | async-done | bytes 3440656 | tf_op jit(solution)/shard_map/psum | solution.py:117
  454.1 3.7 fusion.64
  457.7 2.3 fusion
  460.0 0.7 broadcast_in_dim.11
  460.7 6.7 %all-to-all-start.4 = ((f32[32,1,512]{2,1,0:T(1,128)}), f32[32,1,512]{2,1,0:T(1,128)S(1)}, u32[]{:S(2)}, u32[]{:S(2)}) async-start(f32[32,1,512]{2,1,0:T(1,128)} %broadcast_in_dim.11), calls=%async_computation.4 | async-start | bytes 131072 | tf_op jit(solution)/shard_map/all_to_all | solution.py:12
  467.4 1.7 fusion.66
  469.2 1.5 fusion.65
  470.7 4.5 all-to-all-done.4
  475.2 0.8 broadcast_in_dim.10
  476.0 10.2 %all-to-all-start.3 = ((f32[16,1,3584]{2,1,0:T(1,128)}), f32[16,1,3584]{2,1,0:T(1,128)}, u32[]{:S(2)}, u32[]{:S(2)}) async-start(f32[16,1,3584]{2,1,0:T(1,128)} %broadcast_in_dim.10), calls=%async_computation.3 | async-start | bytes 458752 | tf_op jit(solution)/shard_map/all_to_all | solution.py:12
  486.2 1.8 fusion.45
  488.0 1.3 fusion.18
  489.3 1.8 reshape.51
  491.2 11.7 %all-to-all-done.3 = f32[16,1,3584]{2,1,0:T(1,128)} async-done(((f32[16,1,3584]{2,1,0:T(1,128)}), f32[16,1,3584]{2,1,0:T(1,128)}, u32[]{:S(2)}, u32[]{:S(2)}) %all-to-all-start.3) | async-done | bytes 229408 | tf_op jit(solution)/shard_map/all_to_all | solution.py:12
  502.9 8.6 %all-to-all-start.2 = ((bf16[32,20,256]{2,1,0:T(8,128)(2,1)}), bf16[32,20,256]{2,1,0:T(8,128)(2,1)S(1)}, u32[]{:S(2)}, u32[]{:S(2)}) async-start(bf16[32,20,256]{2,1,0:T(8,128)(2,1)} %reshape.51), calls=%async_computation.2 | async-start | bytes 786432 | tf_op jit(solution)/shard_map/all_to_all | solution.py:43
  512.1 2.4 fusion.35
  514.5 1.1 reduce_sum.166
  516.2 2.3 fusion.25
  518.5 1.2 fusion.30
  519.7 5.8 %all-to-all-done.2 = bf16[32,20,256]{2,1,0:T(8,128)(2,1)S(1)} async-done(((bf16[32,20,256]{2,1,0:T(8,128)(2,1)}), bf16[32,20,256]{2,1,0:T(8,128)(2,1)S(1)}, u32[]{:S(2)}, u32[]{:S(2)}) %all-to-all-start.2) | async-done | bytes 327712 | tf_op jit(solution)/shard_map/all_to_all | solution.py:43
  (68 shorter events, 3.1 us)
Async XLA Ops:
  7.2 13.7 %copy-start.9 = (bf16[20,256]{1,0:T(8,128)(2,1)S(1)}, bf16[20,256]{1,0:T(8,128)(2,1)}, u32[]{:S(2)}) copy-start(bf16[20,256]{1,0:T(8,128)(2,1)} %param.9) | copy-start | bytes 30724
  7.2 35.4 %copy-start.17 = (bf16[20,256]{1,0:T(8,128)(2,1)S(1)}, bf16[20,256]{1,0:T(8,128)(2,1)}, u32[]{:S(2)}) copy-start(bf16[20,256]{1,0:T(8,128)(2,1)} %param.8) | copy-start | bytes 30724
  9.1 18.2 %all-to-all-start = ((f32[32,1,512]{2,1,0:T(1,128)}), f32[32,1,512]{2,1,0:T(1,128)S(1)}, u32[]{:S(2)}, u32[]{:S(2)}) async-start(f32[32,1,512]{2,1,0:T(1,128)} %broadcast_in_dim.8), calls=%async_computation | async-start | bytes 131072 | tf_op jit(solution)/shard_map/all_to_all | solution.py:12
  28.1 63.4 %all-to-all-start.1 = ((f32[16,1,3584]{2,1,0:T(1,128)}), f32[16,1,3584]{2,1,0:T(1,128)S(1)}, u32[]{:S(2)}, u32[]{:S(2)}) async-start(f32[16,1,3584]{2,1,0:T(1,128)} %broadcast_in_dim.9), calls=%async_computation.1 | async-start | bytes 458752 | tf_op jit(solution)/shard_map/all_to_all | solution.py:12
  42.5 411.5 %all-reduce.3.cloned.1.call-start = ((), (), s32[]{:S(2)}) async-start(), calls=%async_computation.5 | async-start | bytes 6881280 | tf_op jit(solution)/shard_map/psum | solution.py:117
  42.6 47.3 %copy-start = (bf16[896,256]{1,0:T(8,128)(2,1)S(1)}, bf16[896,256]{1,0:T(8,128)(2,1)}, u32[]{:S(2)}) copy-start(bf16[896,256]{1,0:T(8,128)(2,1)} %param.12) | copy-start | bytes 1376260
  42.6 47.3 %copy-start.20 = (f32[256]{0:T(256)S(1)}, f32[256]{0:T(256)}, u32[]{:S(2)}) copy-start(f32[256]{0:T(256)} %param.15) | copy-start | bytes 3076
  89.1 364.9 %copy-start.7 = (bf16[640,512]{1,0:T(8,128)(2,1)}, bf16[640,512]{1,0:T(8,128)(2,1)S(1)}, u32[]{:S(2)}) copy-start(bf16[640,512]{1,0:T(8,128)(2,1)S(1)} %reshape.53) | copy-start | bytes 1966084
  89.9 1.6 copy-start.18
  89.9 364.2 %copy-start.23 = (f32[256]{0:T(256)}, f32[256]{0:T(256)S(1)}, u32[]{:S(2)}) copy-start(f32[256]{0:T(256)S(1)} %get-tuple-element.46) | copy-start | bytes 3076
  89.9 2.4 copy-start.1
  89.9 2.4 copy-start.10
  91.5 2.4 copy-start.2
  91.5 2.4 copy-start.11
  92.3 375.1 %copy-start.12 = (f32[896]{0:T(1024)}, f32[896]{0:T(1024)S(1)}, u32[]{:S(2)}) copy-start(f32[896]{0:T(1024)S(1)} %get-tuple-element.42) | copy-start | bytes 10756
  92.3 376.9 %copy-start.15 = (f32[896]{0:T(1024)}, f32[896]{0:T(1024)S(1)}, u32[]{:S(2)}) copy-start(f32[896]{0:T(1024)S(1)} %get-tuple-element.39) | copy-start | bytes 10756
  454.0 3.7 copy-start.4
  454.1 3.7 copy-start.5
  454.1 3.7 copy-start.6
  460.7 14.5 %all-to-all-start.4 = ((f32[32,1,512]{2,1,0:T(1,128)}), f32[32,1,512]{2,1,0:T(1,128)S(1)}, u32[]{:S(2)}, u32[]{:S(2)}) async-start(f32[32,1,512]{2,1,0:T(1,128)} %broadcast_in_dim.11), calls=%async_computation.4 | async-start | bytes 131072 | tf_op jit(solution)/shard_map/all_to_all | solution.py:12
  467.4 1.7 copy-start.3
  467.4 1.7 copy-start.8
  476.0 26.9 %all-to-all-start.3 = ((f32[16,1,3584]{2,1,0:T(1,128)}), f32[16,1,3584]{2,1,0:T(1,128)}, u32[]{:S(2)}, u32[]{:S(2)}) async-start(f32[16,1,3584]{2,1,0:T(1,128)} %broadcast_in_dim.10), calls=%async_computation.3 | async-start | bytes 458752 | tf_op jit(solution)/shard_map/all_to_all | solution.py:12
  486.2 1.8 copy-start.13
  489.3 22.2 %copy-start.19 = (f32[256]{0:T(256)S(1)}, f32[256]{0:T(256)}, u32[]{:S(2)}) copy-start(f32[256]{0:T(256)} %copy-done.18) | copy-start | bytes 3076
  489.3 22.2 %copy-start.21 = (f32[256]{0:T(256)S(1)}, f32[256]{0:T(256)}, u32[]{:S(2)}) copy-start(f32[256]{0:T(256)} %param.15) | copy-start | bytes 3076
  489.3 22.8 %copy-start.22 = (f32[256]{0:T(256)S(1)}, f32[256]{0:T(256)}, u32[]{:S(2)}) copy-start(f32[256]{0:T(256)} %get-tuple-element.22) | copy-start | bytes 3076
  489.3 22.8 %copy-start.24 = (f32[256]{0:T(256)S(1)}, f32[256]{0:T(256)}, u32[]{:S(2)}) copy-start(f32[256]{0:T(256)} %copy-done.23) | copy-start | bytes 3076
  502.9 22.7 %all-to-all-start.2 = ((bf16[32,20,256]{2,1,0:T(8,128)(2,1)}), bf16[32,20,256]{2,1,0:T(8,128)(2,1)S(1)}, u32[]{:S(2)}, u32[]{:S(2)}) async-start(bf16[32,20,256]{2,1,0:T(8,128)(2,1)} %reshape.51), calls=%async_computation.2 | async-start | bytes 786432 | tf_op jit(solution)/shard_map/all_to_all | solution.py:43
  512.1 4.1 copy-start.14
  512.1 4.1 copy-start.16
Sparse Core Ops, SparseCore 0:
  95.6 358.3 all-reduce.2
where the time goes:
time: 534 us; the launch traced here: 533 us
  waiting for transfers between devices  387 us (72%)
  starting transfers between devices  50.3 us (9%)
  blocking collectives  46.4 us (9%)
  other arithmetic  15.3 us (3%)
  matrix products  14.7 us (3%)
  between operations  14.3 us (3%)
    psum x1, waiting for transfers between devices, local(): lax.psum(up_part, 'replica').astype(jnp.float32)  359 us
    all_gather x1, blocking collectives, sent_together(): result, at, done = (lax.all_gather(both, axis, axis=dim, tiled=True), 0, [])  46.4 us
    all_to_all x4, starting transfers between devices, sent_to_all(): return lax.all_to_all(copies, axis, split_axis=0, concat_axis=0, tiled=True)  41.6 us
    all_to_all x4, waiting for transfers between devices, sent_to_all(): return lax.all_to_all(copies, axis, split_axis=0, concat_axis=0, tiled=True)  22.6 us
  transfers between devices with their start and end apart: 6, of which 5 were waited for; matrix products, arithmetic and copies ran while one was open for 4% of the time, Pallas kernels for 0%

commit v1 on v0

v1 whole, which is shorter than its diff:
```python
import functools

import jax
import jax.numpy as jnp
from jax import lax
from jax.experimental import pallas as pl
from jax.sharding import Mesh, PartitionSpec as P

epsilon = 0.0001
branch_scale = 0.5
bf16 = jnp.bfloat16
f32 = jnp.float32


def nn(a, b):
    return lax.dot_general(a, b, (((1,), (0,)), ((), ())), preferred_element_type=f32)


def nt(a, b):
    return lax.dot_general(a, b, (((1,), (1,)), ((), ())), preferred_element_type=f32)


def tn(a, b):
    return lax.dot_general(a, b, (((0,), (0,)), ((), ())), preferred_element_type=f32)


def moments(w):
    mean = jnp.sum(w, axis=0, keepdims=True) * (1.0 / w.shape[0])
    off = w - mean
    return mean, jnp.sum(off * off, axis=0, keepdims=True)


def prepare(gate_ref, up_ref, down_ref, packed_ref, wide_ref, narrow_ref):
    share = packed_ref.shape[2]
    for at, ref in enumerate((gate_ref, up_ref)):
        w = ref[...].astype(f32)
        mean, square = moments(w)
        wide_ref[2 * at : 2 * at + 1, :] = mean
        wide_ref[2 * at + 1 : 2 * at + 2, :] = square
        turned = w.T.astype(bf16)
        for j in range(packed_ref.shape[0]):
            packed_ref[j, at] = turned[j * share : (j + 1) * share]
    w = down_ref[...]
    mean, square = moments(w.astype(f32))
    narrow_ref[0:1, :] = mean
    narrow_ref[1:2, :] = square
    for j in range(packed_ref.shape[0]):
        packed_ref[j, 2] = w[j * share : (j + 1) * share]


def whole(own_ref, other_ref, j, at):
    width = own_ref.shape[-1] // 2
    halves = [
        ref[:, j, :, at * width : (at + 1) * width].reshape(-1, width)
        for ref in (own_ref, other_ref)
    ]
    return jnp.concatenate(halves, axis=0)


def hat_of(w_ref, cols_ref, rows_ref, j, at):
    w = w_ref[j, at].astype(f32)
    if at < 2:
        return ((w - cols_ref[:, 2 * at : 2 * at + 1]) * cols_ref[:, 2 * at + 1 : 2 * at + 2]).astype(bf16)
    return ((w - rows_ref[j, 0:1, :]) * rows_ref[j, 1:2, :]).astype(bf16)


def forward(w_ref, own_ref, other_ref, cols_ref, rows_ref, out_ref):
    blocks = w_ref.shape[0]
    parts = out_ref.shape[0]
    tall = w_ref.shape[2] // parts
    for at in range(3):
        total = None
        for j in range(blocks):
            hat = hat_of(w_ref, cols_ref, rows_ref, j, at)
            term = nt(hat, whole(own_ref, other_ref, j, 0 if at < 2 else 1))
            total = term if total is None else total + term
        total = total.astype(bf16)
        for q in range(parts):
            out_ref[q, at * tall : (at + 1) * tall, :] = total[q * tall : (q + 1) * tall]
    ones = jnp.ones((8, own_ref.shape[-1] // 2), bf16)
    row = None
    for j in range(blocks):
        term = nt(ones, whole(own_ref, other_ref, j, 0))
        row = term if row is None else row + term
    high = row.astype(bf16)
    low = (row - high.astype(f32)).astype(bf16)
    index = lax.broadcasted_iota(jnp.int32, row.shape, 0)
    both = jnp.where(index == 0, high.astype(f32), jnp.where(index == 1, low.astype(f32), 0.0)).astype(bf16)
    for q in range(parts):
        out_ref[q, 3 * tall : 3 * tall + 8, :] = both


def gating(z_ref, d_ref, dots_ref, row_ref):
    tall = dots_ref.shape[0]

    def summed(a, b):
        total = z_ref[0, a:b, :].astype(f32)
        for q in range(1, z_ref.shape[0]):
            total = total + z_ref[q, a:b, :].astype(f32)
        return total

    gate = summed(0, tall)
    up = summed(tall, 2 * tall)
    dhidden = summed(2 * tall, 3 * tall)
    row = summed(3 * tall, 3 * tall + 8)
    row_ref[...] = jnp.broadcast_to(row[0:1] + row[1:2], row_ref.shape)
    sig = 1.0 / (1.0 + jnp.exp(-gate))
    act = gate * sig
    d_gate = (dhidden * up * sig * (1.0 + gate * (1.0 - sig))).astype(bf16)
    d_up = (dhidden * act).astype(bf16)
    d_ref[0:tall, :] = d_gate
    d_ref[tall : 2 * tall, :] = d_up
    d_ref[2 * tall : 3 * tall, :] = (act * up).astype(bf16)
    gate_dot = jnp.sum(d_gate.astype(f32) * gate, axis=1, keepdims=True)
    up_dot = jnp.sum(d_up.astype(f32) * up, axis=1, keepdims=True)
    lane = lax.broadcasted_iota(jnp.int32, dots_ref.shape, 1)
    dots_ref[...] = jnp.where(lane == 0, gate_dot, jnp.where(lane == 1, up_dot, 0.0))


def backward(
    width_all, d_ref, w_ref, own_ref, other_ref, cols_ref, rows_ref, dots_ref, row_ref,
    grad_ref, sums_ref, mine_ref, theirs_ref,
):
    blocks = w_ref.shape[0]
    parts = d_ref.shape[0]
    tall = w_ref.shape[2] // parts
    streams = [
        jnp.concatenate([d_ref[q, at * tall : (at + 1) * tall, :] for q in range(parts)], axis=0)
        for at in range(3)
    ]
    row = row_ref[0:1, :]
    means = [
        jnp.sum(streams[at].astype(f32) * row, axis=1, keepdims=True) * (1.0 / width_all) for at in range(2)
    ]
    half = mine_ref.shape[0] * mine_ref.shape[2]
    for j in range(blocks):
        left = whole(own_ref, other_ref, j, 0)
        back = None
        for at in range(2):
            p = nn(streams[at], left)
            gs = cols_ref[:, 2 * at + 1 : 2 * at + 2]
            s = cols_ref[:, 4 + at : 5 + at]
            cent = w_ref[j, at].astype(f32) - cols_ref[:, 2 * at : 2 * at + 1]
            grad = gs * (p - means[at]) - cent * (s * s * dots_ref[:, at : at + 1])
            grad_ref[j, at] = grad.astype(bf16)
            term = tn(streams[at], (cent * gs).astype(bf16))
            back = term if back is None else back + term
        mine_ref[:, j] = back[:half].reshape(mine_ref.shape[0], mine_ref.shape[2], mine_ref.shape[3])
        theirs_ref[:, j] = (
            back[half:].astype(bf16).reshape(mine_ref.shape[0], mine_ref.shape[2], mine_ref.shape[3])
        )
        p = nn(streams[2], whole(own_ref, other_ref, j, 1))
        cent = w_ref[j, 2].astype(f32) - rows_ref[j, 0:1, :]
        sums_ref[j, 0:1, :] = jnp.sum(p, axis=0, keepdims=True)
        sums_ref[j, 1:2, :] = jnp.sum(p * cent, axis=0, keepdims=True)
        grad_ref[j, 2] = p.astype(bf16)


def finish(hidden_all, g_ref, down_ref, stat_ref, gate_ref, up_ref, grad_ref):
    for at, ref in enumerate((gate_ref, up_ref)):
        tall = jnp.concatenate([g_ref[j, at].astype(f32) for j in range(g_ref.shape[0])], axis=0)
        ref[...] = tall.T
    mean, s, gain = stat_ref[0:1, :], stat_ref[1:2, :], stat_ref[2:3, :]
    summed, crossed = stat_ref[3:4, :], stat_ref[4:5, :]
    share = g_ref.shape[2]
    for j in range(g_ref.shape[0]):
        p = g_ref[j, 2].astype(f32)
        cent = down_ref[j * share : (j + 1) * share, :].astype(f32) - mean
        grad_ref[j * share : (j + 1) * share, :] = s * gain * (p - summed * (1.0 / hidden_all)) - (
            s * s * s * gain * crossed
        ) * cent


def call(body, outs, *args):
    return pl.pallas_call(body, out_shape=[jax.ShapeDtypeStruct(s, t) for s, t in outs])(*args)


def exchange(x, axis):
    return lax.all_to_all(x, axis, split_axis=0, concat_axis=0, tiled=True)


def to_all(x, axis):
    size = 1
    for a in (axis,) if isinstance(axis, str) else axis:
        size *= lax.axis_size(a)
    return exchange(jnp.broadcast_to(x, (size, *x.shape)), axis)


def combined(means, squares, count):
    mean = jnp.mean(means, axis=0)
    off = means - mean
    return mean, lax.rsqrt(jnp.sum(squares, axis=0) + count * jnp.sum(off * off, axis=0) + epsilon)


BLK = ("y", "zl", "core")
REP = ("zh", "x")


def local(tokens, cotangent, gate_weight, up_weight, down_weight, gate_gain, up_gain, down_gain):
    rows, width = tokens.shape
    hidden = gate_weight.shape[1]
    nx, nz, ny = lax.axis_size("x"), lax.axis_size("zh"), lax.axis_size("y")
    nl = lax.axis_size("zl")
    width_all = width * nx * nz
    hidden_all = hidden * ny * nl * lax.axis_size("core")
    share = hidden // nx
    tall = share // nz
    count = rows * ny * nl * lax.axis_size("core")
    me = lax.axis_index("x")

    scaled = (branch_scale * cotangent.astype(f32)).astype(bf16)
    both = jnp.concatenate([tokens, scaled], axis=1)
    along = to_all(both, "x")
    packed, wide, narrow = call(
        prepare,
        [((nx, 3, share, width), bf16), ((4, hidden), f32), ((2, width), f32)],
        gate_weight, up_weight, down_weight,
    )
    along = to_all(along, "zl")
    along = jnp.moveaxis(along, 0, 1).reshape(nx, nl * rows, 2 * width)
    weights = exchange(packed, "x")

    own = to_all(along, "y")
    other = lax.ppermute(own, "core", [(0, 1), (1, 0)])

    wide = jnp.moveaxis(wide.reshape(4, nx, share), 1, 0)
    wide = exchange(jnp.broadcast_to(wide[None], (nz, nx, 4, share)).reshape(nz * nx, 4, share), REP)
    gate_mean, gate_scale = combined(wide[:, 0], wide[:, 1], width)
    up_mean, up_scale = combined(wide[:, 2], wide[:, 3], width)
    my_gate_gain = gate_gain.reshape(nx, share)[me]
    my_up_gain = up_gain.reshape(nx, share)[me]
    cols = jnp.stack(
        [
            gate_mean, my_gate_gain * gate_scale, up_mean, my_up_gain * up_scale,
            gate_scale, up_scale, gate_scale, up_scale,
        ],
        axis=1,
    )
    narrow = to_all(narrow, BLK)
    down_mean, down_scale = combined(narrow[:, 0], narrow[:, 1], hidden)
    rows_of = to_all(jnp.stack([down_mean, down_gain * down_scale]), "x")

    (parts,) = call(
        forward, [((nz, 3 * tall + 8, count), bf16)], weights, own, other, cols, rows_of
    )
    parts = exchange(parts, "zh")
    d, dots, row = call(
        gating, [((3 * tall, count), bf16), ((tall, 128), f32), ((8, count), f32)], parts
    )
    dots = to_all(dots, "zh").reshape(share, 128)
    d = to_all(d, "zh")
    shape = (ny, nx, nl * rows, width)
    grads, sums, mine, theirs = call(
        functools.partial(backward, width_all),
        [((nx, 3, share, width), bf16), ((nx, 2, width), f32), (shape, f32), (shape, bf16)],
        d, weights, own, other, cols, rows_of, dots, row,
    )
    theirs = lax.ppermute(theirs, "core", [(0, 1), (1, 0)])
    sums = exchange(sums, "x").sum(axis=0)
    sums = to_all(sums, BLK).sum(axis=0)
    gains = to_all(dots[:, :2].T, "x")
    gains = jnp.moveaxis(gains, 0, 1).reshape(2, hidden)
    grads = exchange(grads, "x")
    back = exchange((mine + theirs.astype(f32)).astype(bf16), "y")
    back = back.astype(f32).sum(axis=0).astype(bf16)
    back = jnp.moveaxis(back.reshape(nx, nl, rows, width), 1, 0)
    back = exchange(back, "zl").astype(f32).sum(axis=0).astype(bf16)
    back = exchange(back, "x").astype(f32).sum(axis=0)
    grad_tokens = cotangent.astype(f32) + back
    zero = jnp.zeros_like(down_mean)
    stat = jnp.stack([down_mean, down_scale, down_gain, sums[0], sums[1], zero, zero, zero])
    grad_gate, grad_up, grad_down = call(
        functools.partial(finish, hidden_all),
        [((width, hidden), f32), ((width, hidden), f32), ((hidden, width), f32)],
        grads, down_weight, stat,
    )
    return (
        grad_tokens,
        grad_gate,
        grad_up,
        grad_down,
        gains[0] / gate_gain,
        gains[1] / up_gain,
        down_scale * sums[1],
    )


def solution(mesh):
    fine = Mesh(mesh.devices.reshape(4, 4, 2, 4, 4), (*BLK, *REP))
    return jax.shard_map(
        local,
        mesh=fine,
        in_specs=(
            P(BLK, REP), P(BLK, REP), P(REP, BLK), P(REP, BLK), P(BLK, REP), P(BLK), P(BLK), P(REP),
        ),
        out_specs=(
            P(BLK, REP), P(REP, BLK), P(REP, BLK), P(BLK, REP), P(BLK), P(BLK), P(REP),
        ),
        check_vma=False,
    )
```

time: 534 us -> 340 us (0.64)
  waiting for transfers between devices: 387 us -> 89.8 us
  blocking collectives: 46.4 us -> 139 us
  Pallas kernels: 0 us -> 19.4 us
  starting transfers between devices: 50.3 us -> 69.5 us
  matrix products: 14.7 us -> 0 us
  between operations: 14.3 us -> 0.91 us
  other arithmetic: 15.3 us -> 6.72 us
  local copies, waits for them, and re-layouts: 5.02 us -> 11.5 us
    psum x1 -> x0, waiting for transfers between devices: 359 us -> none  [local(): lax.psum(up_part, 'replica').astype(jnp.float32)]
    all_to_all x0 -> x6, blocking collectives: none -> 139 us  [exchange(): return lax.all_to_all(x, axis, split_axis=0, concat_axis=0, tiled=True)]
    all_to_all x5 -> x11, waiting for transfers between devices: 28.4 us -> 89.8 us  [exchange(): return lax.all_to_all(x, axis, split_axis=0, concat_axis=0, tiled=True)]
    all_gather x1 -> x0, blocking collectives: 46.4 us -> none  [sent_together(): result, at, done = (lax.all_gather(both, axis, axis=dim, tiled=True), 0, [])]
    pallas_call x0 -> x5, Pallas kernels: none -> 19.4 us  [call(): pl.pallas_call(body, out_shape=[jax.ShapeDtypeStruct(s, t) for s, t in ou...]
    dot_general x8 -> x0, matrix products: 14.7 us -> none  [the longest x3 6.88 us: contract_first(): lax.dot_general(left, right, (((0,), (0,)), ((), ())), preferred_element_...]
    all_to_all x5 -> x11, starting transfers between devices: 50.3 us -> 62.5 us  [exchange(): return lax.all_to_all(x, axis, split_axis=0, concat_axis=0, tiled=True)]
    ppermute x0 -> x2, starting transfers between devices: none -> 7.03 us  [the longest x1 3.8 us: local(): theirs = lax.ppermute(theirs, 'core', [(0, 1), (1, 0)])]
  transfers between devices with their start and end apart: 6 -> 13, of which waited for: 5 -> 10; matrix products, arithmetic and copies ran while one was open for 4% -> 2% of each run, Pallas kernels for 0% -> 2%
where the time goes in v1:
time: 340 us; the launch traced here: 337 us
  blocking collectives  139 us (41%)
  waiting for transfers between devices  89.8 us (26%)
  starting transfers between devices  69.5 us (20%)
  Pallas kernels  19.4 us (6%)
  local copies, waits for them, and re-layouts  11.5 us (3%)
  other arithmetic  6.72 us (2%)
    all_to_all x6, blocking collectives, exchange(): return lax.all_to_all(x, axis, split_axis=0, concat_axis=0, tiled=True)  139 us
    all_to_all x11, waiting for transfers between devices, exchange(): return lax.all_to_all(x, axis, split_axis=0, concat_axis=0, tiled=True)  89.8 us
    all_to_all x11, starting transfers between devices, exchange(): return lax.all_to_all(x, axis, split_axis=0, concat_axis=0, tiled=True)  62.5 us
    pallas_call x5, Pallas kernels, call(): pl.pallas_call(body, out_shape=[jax.ShapeDtypeStruct(s, t) for s, t in ou...  19.4 us
  transfers between devices with their start and end apart: 13, of which 10 were waited for; matrix products, arithmetic and copies ran while one was open for 2% of the time, Pallas kernels for 2%

profile of v1, /device:TPU:1, one launch (start us, length us, event | category | flops | bytes accessed | tf_op | source)
XLA Modules:
  0.0 336.6 jit_solution(13049338583984402291)
XLA Ops:
  2.7 4.8 %all-to-all-start.1 = ((bf16[4,20,512]{2,1,0:T(8,128)(2,1)}), bf16[4,20,512]{2,1,0:T(8,128)(2,1)S(1)}, u32[]{:S(2)}, u32[]{:S(2)}) async-start(bf16[4,20,512]{2,1,0:T(8,128)(2,1)} %broadcast_in_dim.36), calls=%async_computation.1 | async-start | bytes 196608 | tf_op jit(solution)/shard_map/all_to_all | solution.py:179
  7.5 2.9 shard_map.135
  12.8 16.7 %all-to-all-start.4 = ((f32[16,4,224]{2,1,0:T(4,128)}), f32[16,4,224]{2,1,0:T(4,128)S(1)}, u32[]{:S(2)}, u32[]{:S(2)}) async-start(f32[16,4,224]{2,1,0:T(4,128)} %bitcast.3), calls=%async_computation.4 | async-start | bytes 131072 | tf_op jit(solution)/shard_map/all_to_all | solution.py:179
  29.6 13.7 %all-to-all-done.4 = f32[16,4,224]{2,1,0:T(4,128)S(1)} async-done(((f32[16,4,224]{2,1,0:T(4,128)}), f32[16,4,224]{2,1,0:T(4,128)S(1)}, u32[]{:S(2)}, u32[]{:S(2)}) %all-to-all-start.4) | async-done | bytes 57376 | tf_op jit(solution)/shard_map/all_to_all | solution.py:179
  43.4 9.5 %all_to_all.85 = bf16[4,4,20,512]{3,1,2,0:T(4,128)(2,1)S(1)} all-to-all(bf16[4,4,20,512]{3,1,2,0:T(4,128)(2,1)S(1)} %broadcast_in_dim.37), channel_id=1, replica_groups=mesh['y'=4,'zl'=4,'core'=2,'zh'=4,'x'=4] {'zl'}, dimensions={0} | all-to-all | bytes 655360 | tf_op jit(solution)/shard_map/all_to_all | solution.py:179
  53.6 9.9 %all-to-all-start.5 = ((f32[32,2,256]{2,1,0:T(2,128)}), f32[32,2,256]{2,1,0:T(2,128)S(1)}, u32[]{:S(2)}, u32[]{:S(2)}) async-start(f32[32,2,256]{2,1,0:T(2,128)} %broadcast_in_dim.40), calls=%async_computation.5 | async-start | bytes 131072 | tf_op jit(solution)/shard_map/all_to_all | solution.py:179
  63.7 7.5 %all-to-all-done.5 = f32[32,2,256]{2,1,0:T(2,128)S(1)} async-done(((f32[32,2,256]{2,1,0:T(2,128)}), f32[32,2,256]{2,1,0:T(2,128)S(1)}, u32[]{:S(2)}, u32[]{:S(2)}) %all-to-all-start.5) | async-done | bytes 65568 | tf_op jit(solution)/shard_map/all_to_all | solution.py:179
  72.5 3.7 %all-to-all-start.3 = ((bf16[4,4,80,512]{3,2,1,0:T(8,128)(2,1)}), bf16[4,4,80,512]{3,2,1,0:T(8,128)(2,1)S(1)}, u32[]{:S(2)}, u32[]{:S(2)}) async-start(bf16[4,4,80,512]{3,2,1,0:T(8,128)(2,1)} %broadcast_in_dim.38), calls=%async_computation.3 | async-start | bytes 2621440 | tf_op jit(solution)/shard_map/all_to_all | solution.py:179
  76.4 17.3 %all-to-all-done.3.own_ref = bf16[4,4,80,512]{3,2,1,0:T(8,128)(2,1)S(1)} async-done(((bf16[4,4,80,512]{3,2,1,0:T(8,128)(2,1)}), bf16[4,4,80,512]{3,2,1,0:T(8,128)(2,1)S(1)}, u32[]{:S(2)}, u32[]{:S(2)}) %all-to-all-start.3) | async-done | bytes 1310752 | tf_op jit(solution)/shard_map/all_to_all | solution.py:179
  94.3 3.2 all-to-all-start.6
  97.6 3.2 collective-permute-start
  102.3 3.6 %all-to-all-start = ((bf16[4,3,224,256]{3,2,1,0:T(8,128)(2,1)}), bf16[4,3,224,256]{3,2,1,0:T(8,128)(2,1)S(1)}, u32[]{:S(2)}, u32[]{:S(2)}) async-start(bf16[4,3,224,256]{3,2,1,0:T(8,128)(2,1)} %get-tuple-element.20), calls=%async_computation | async-start | bytes 2752512 | tf_op jit(solution)/shard_map/all_to_all | solution.py:179
  106.8 15.4 %all-to-all-done.w_ref = bf16[4,3,224,256]{3,2,1,0:T(8,128)(2,1)S(1)} async-done(((bf16[4,3,224,256]{3,2,1,0:T(8,128)(2,1)}), bf16[4,3,224,256]{3,2,1,0:T(8,128)(2,1)S(1)}, u32[]{:S(2)}, u32[]{:S(2)}) %all-to-all-start) | async-done | bytes 1376288 | tf_op jit(solution)/shard_map/all_to_all | solution.py:179
  123.3 4.8 %shard_map.136 = bf16[4,176,640]{2,1,0:T(8,128)(2,1)} custom-call(bf16[4,3,224,256]{3,2,1,0:T(8,128)(2,1)} %copy-done, bf16[4,4,80,512]{3,2,1,0:T(8,128)(2,1)} %copy-done.1, bf16[4,4,80,512]{3,2,1,0:T(8,128)(2,1)} %collective-permute-done.other_ref, f32[224,8]{1,0:T(8,128)} %copy.61.cols_ref, f32[4,2,256]{2,1,0:T(2,128)} %copy-done.4), custom_call_target="tpu_custom_call" | custom-call | tf_op jit(solution)/shard_map/pallas_call | solution.py:175
  128.1 48.8 %all_to_all.86.z_ref = bf16[4,176,640]{2,1,0:T(8,128)(2,1)} all-to-all(bf16[4,176,640]{2,1,0:T(8,128)(2,1)} %shard_map.136), channel_id=1, replica_groups=mesh['y'=4,'zl'=4,'core'=2,'zh'=4,'x'=4] {'zh'}, dimensions={0} | all-to-all | bytes 1802240 | tf_op jit(solution)/shard_map/all_to_all | solution.py:179
  176.9 2.1 shard_map.137
  179.7 19.1 %all_to_all.87 = f32[4,56,128]{2,1,0:T(8,128)} all-to-all(f32[4,56,128]{2,1,0:T(8,128)S(1)} %broadcast_in_dim.43), channel_id=1, replica_groups=mesh['y'=4,'zl'=4,'core'=2,'zh'=4,'x'=4] {'zh'}, dimensions={0} | all-to-all | bytes 229376 | tf_op jit(solution)/shard_map/all_to_all | solution.py:179
  199.8 46.3 %all_to_all.88.d_ref = bf16[4,168,640]{2,1,0:T(8,128)(2,1)} all-to-all(bf16[4,168,640]{2,1,0:T(8,128)(2,1)S(1)} %broadcast_in_dim.42), channel_id=1, replica_groups=mesh['y'=4,'zl'=4,'core'=2,'zh'=4,'x'=4] {'zh'}, dimensions={0} | all-to-all | bytes 1720320 | tf_op jit(solution)/shard_map/all_to_all | solution.py:179
  246.2 6.4 %shard_map.138 = (bf16[4,3,224,256]{3,2,1,0:T(8,128)(2,1)}, f32[4,2,256]{2,1,0:T(2,128)}, f32[4,4,80,256]{3,2,1,0:T(8,128)}, bf16[4,4,80,256]{3,2,1,0:T(8,128)(2,1)}) custom-call(bf16[4,168,640]{2,1,0:T(8,128)(2,1)} %all_to_all.88.d_ref, bf16[4,3,224,256]{3,2,1,0:T(8,128)(2,1)} %copy-done, bf16[4,4,80,512]{3,2,1,0:T(8,128)(2,1)} %copy-done.1, ...), custom_call_target="tpu_custom_call" | custom-call | tf_op jit(solution)/shard_map/pallas_call | solution.py:175
  252.6 3.8 %collective-permute-start.1 = (bf16[4,4,80,256]{3,2,1,0:T(8,128)(2,1)}, bf16[4,4,80,256]{3,2,1,0:T(8,128)(2,1)S(1)}, u32[]{:S(2)}, u32[]{:S(2)}) collective-permute-start(bf16[4,4,80,256]{3,2,1,0:T(8,128)(2,1)} %get-tuple-element.27), channel_id=1, source_target_pairs={{0,16},{16,0},{1,17},{17,1},{2,18},{18,2},{3,19},{19,3},{4,20},{20... | collective-permute-start | bytes 1966088 | tf_op jit(solution)/shard_map/ppermute | solution.py:258
  256.5 6.5 %all_to_all.89 = f32[4,2,224]{2,1,0:T(2,128)S(1)} all-to-all(f32[4,2,224]{2,1,0:T(2,128)S(1)} %broadcast_in_dim.45), channel_id=1, replica_groups=mesh['y'=4,'zl'=4,'core'=2,'zh'=4,'x'=4] {'x'}, dimensions={0} | all-to-all | bytes 14336 | tf_op jit(solution)/shard_map/all_to_all | solution.py:179
  263.0 3.2 all-to-all-start.14
  266.2 2.3 add_convert_fusion
  270.4 3.5 %all-to-all-start.10 = ((bf16[4,4,80,256]{3,2,1,0:T(8,128)(2,1)}), bf16[4,4,80,256]{3,2,1,0:T(8,128)(2,1)S(1)}, u32[]{:S(2)}, u32[]{:S(2)}) async-start(bf16[4,4,80,256]{3,2,1,0:T(8,128)(2,1)} %add_convert_fusion), calls=%async_computation.10 | async-start | bytes 1310720 | tf_op jit(solution)/shard_map/all_to_all | solution.py:179
  273.9 8.3 %all-to-all-done.10 = bf16[4,4,80,256]{3,2,1,0:T(8,128)(2,1)S(1)} async-done(((bf16[4,4,80,256]{3,2,1,0:T(8,128)(2,1)}), bf16[4,4,80,256]{3,2,1,0:T(8,128)(2,1)S(1)}, u32[]{:S(2)}, u32[]{:S(2)}) %all-to-all-start.10) | async-done | bytes 655392 | tf_op jit(solution)/shard_map/all_to_all | solution.py:179
  282.8 7.0 %all-to-all-start.15 = ((f32[32,2,256]{2,1,0:T(2,128)}), f32[32,2,256]{2,1,0:T(2,128)S(1)}, u32[]{:S(2)}, u32[]{:S(2)}) async-start(f32[32,2,256]{2,1,0:T(2,128)} %broadcast_in_dim.44), calls=%async_computation.15 | async-start | bytes 131072 | tf_op jit(solution)/shard_map/all_to_all | solution.py:179
  290.0 7.7 %all-to-all-done.15 = f32[32,2,256]{2,1,0:T(2,128)S(1)} async-done(((f32[32,2,256]{2,1,0:T(2,128)}), f32[32,2,256]{2,1,0:T(2,128)S(1)}, u32[]{:S(2)}, u32[]{:S(2)}) %all-to-all-start.15) | async-done | bytes 65568 | tf_op jit(solution)/shard_map/all_to_all | solution.py:179
  297.7 8.4 %all_to_all.90 = bf16[4,4,20,256]{3,1,2,0:T(4,128)(2,1)S(1)} all-to-all(bf16[4,4,20,256]{3,1,2,0:T(4,128)(2,1)S(1)} %bitcast.46), channel_id=1, replica_groups=mesh['y'=4,'zl'=4,'core'=2,'zh'=4,'x'=4] {'zl'}, dimensions={0} | all-to-all | bytes 327680 | tf_op jit(solution)/shard_map/all_to_all | solution.py:179
  306.1 3.5 %all-to-all-start.13 = ((bf16[4,3,224,256]{3,2,1,0:T(8,128)(2,1)}), bf16[4,3,224,256]{3,2,1,0:T(8,128)(2,1)S(1)}, u32[]{:S(2)}, u32[]{:S(2)}) async-start(bf16[4,3,224,256]{3,2,1,0:T(8,128)(2,1)} %get-tuple-element.28), calls=%async_computation.13 | async-start | bytes 2752512 | tf_op jit(solution)/shard_map/all_to_all | solution.py:179
  310.4 16.4 %all-to-all-done.13.g_ref = bf16[4,3,224,256]{3,2,1,0:T(8,128)(2,1)S(1)} async-done(((bf16[4,3,224,256]{3,2,1,0:T(8,128)(2,1)}), bf16[4,3,224,256]{3,2,1,0:T(8,128)(2,1)S(1)}, u32[]{:S(2)}, u32[]{:S(2)}) %all-to-all-start.13) | async-done | bytes 1376288 | tf_op jit(solution)/shard_map/all_to_all | solution.py:179
  326.8 3.3 all-to-all-start.12
  332.7 3.2 shard_map.139
  (79 shorter events, 19.4 us)
Async XLA Ops:
  2.7 9.5 %all-to-all-start.1 = ((bf16[4,20,512]{2,1,0:T(8,128)(2,1)}), bf16[4,20,512]{2,1,0:T(8,128)(2,1)S(1)}, u32[]{:S(2)}, u32[]{:S(2)}) async-start(bf16[4,20,512]{2,1,0:T(8,128)(2,1)} %broadcast_in_dim.36), calls=%async_computation.1 | async-start | bytes 196608 | tf_op jit(solution)/shard_map/all_to_all | solution.py:179
  7.5 55.9 %copy-start.7 = (f32[896]{0:T(1024)S(1)}, f32[896]{0:T(1024)}, u32[]{:S(2)}) copy-start(f32[896]{0:T(1024)} %param.14) | copy-start | bytes 10756
  7.5 56.0 %copy-start.6 = (f32[896]{0:T(1024)S(1)}, f32[896]{0:T(1024)}, u32[]{:S(2)}) copy-start(f32[896]{0:T(1024)} %param.13) | copy-start | bytes 10756
  10.5 42.4 %copy-start.9 = (f32[2,256]{1,0:T(2,128)S(1)}, f32[2,256]{1,0:T(2,128)}, u32[]{:S(2)}) copy-start(f32[2,256]{1,0:T(2,128)} %get-tuple-element.22) | copy-start | bytes 6148
  12.8 30.5 %all-to-all-start.4 = ((f32[16,4,224]{2,1,0:T(4,128)}), f32[16,4,224]{2,1,0:T(4,128)S(1)}, u32[]{:S(2)}, u32[]{:S(2)}) async-start(f32[16,4,224]{2,1,0:T(4,128)} %bitcast.3), calls=%async_computation.4 | async-start | bytes 131072 | tf_op jit(solution)/shard_map/all_to_all | solution.py:179
  53.6 17.7 %all-to-all-start.5 = ((f32[32,2,256]{2,1,0:T(2,128)}), f32[32,2,256]{2,1,0:T(2,128)S(1)}, u32[]{:S(2)}, u32[]{:S(2)}) async-start(f32[32,2,256]{2,1,0:T(2,128)} %broadcast_in_dim.40), calls=%async_computation.5 | async-start | bytes 131072 | tf_op jit(solution)/shard_map/all_to_all | solution.py:179
  72.5 3.9 %copy-start.8 = (f32[256]{0:T(256)S(1)}, f32[256]{0:T(256)}, u32[]{:S(2)}) copy-start(f32[256]{0:T(256)} %param.15) | copy-start | bytes 3076
  72.5 21.2 %all-to-all-start.3 = ((bf16[4,4,80,512]{3,2,1,0:T(8,128)(2,1)}), bf16[4,4,80,512]{3,2,1,0:T(8,128)(2,1)S(1)}, u32[]{:S(2)}, u32[]{:S(2)}) async-start(bf16[4,4,80,512]{3,2,1,0:T(8,128)(2,1)} %broadcast_in_dim.38), calls=%async_computation.3 | async-start | bytes 2621440 | tf_op jit(solution)/shard_map/all_to_all | solution.py:179
  93.6 8.0 %copy-start.1 = (bf16[4,4,80,512]{3,2,1,0:T(8,128)(2,1)}, bf16[4,4,80,512]{3,2,1,0:T(8,128)(2,1)S(1)}, u32[]{:S(2)}) copy-start(bf16[4,4,80,512]{3,2,1,0:T(8,128)(2,1)S(1)} %all-to-all-done.3.own_ref) | copy-start | bytes 3932164
  94.3 7.4 %all-to-all-start.6 = ((f32[4,2,256]{2,1,0:T(2,128)}), f32[4,2,256]{2,1,0:T(2,128)S(1)}, u32[]{:S(2)}, u32[]{:S(2)}) async-start(f32[4,2,256]{2,1,0:T(2,128)} %broadcast_in_dim.41), calls=%async_computation.6 | async-start | bytes 16384 | tf_op jit(solution)/shard_map/all_to_all | solution.py:179
  97.6 24.6 %collective-permute-start = (bf16[4,4,80,512]{3,2,1,0:T(8,128)(2,1)S(1)}, bf16[4,4,80,512]{3,2,1,0:T(8,128)(2,1)}, u32[]{:S(2)}, u32[]{:S(2)}) collective-permute-start(bf16[4,4,80,512]{3,2,1,0:T(8,128)(2,1)S(1)} %all-to-all-done.3.own_ref), channel_id=1, source_target_pairs={{0,16},{16,0},{1,17},{17,1},{2,18},{18,2},{3,19},{19,3},{4,20},{20... | collective-permute-start | bytes 3932168 | tf_op jit(solution)/shard_map/ppermute | solution.py:224
  101.7 0.6 copy-start.4
  102.3 19.9 %all-to-all-start = ((bf16[4,3,224,256]{3,2,1,0:T(8,128)(2,1)}), bf16[4,3,224,256]{3,2,1,0:T(8,128)(2,1)S(1)}, u32[]{:S(2)}, u32[]{:S(2)}) async-start(bf16[4,3,224,256]{3,2,1,0:T(8,128)(2,1)} %get-tuple-element.20), calls=%async_computation | async-start | bytes 2752512 | tf_op jit(solution)/shard_map/all_to_all | solution.py:179
  122.2 1.1 copy-start
  246.2 10.2 %copy-start.3 = (f32[4,56,128]{2,1,0:T(8,128)S(1)}, f32[4,56,128]{2,1,0:T(8,128)}, u32[]{:S(2)}) copy-start(f32[4,56,128]{2,1,0:T(8,128)} %all_to_all.87) | copy-start | bytes 344068
  252.6 13.7 %collective-permute-start.1 = (bf16[4,4,80,256]{3,2,1,0:T(8,128)(2,1)}, bf16[4,4,80,256]{3,2,1,0:T(8,128)(2,1)S(1)}, u32[]{:S(2)}, u32[]{:S(2)}) collective-permute-start(bf16[4,4,80,256]{3,2,1,0:T(8,128)(2,1)} %get-tuple-element.27), channel_id=1, source_target_pairs={{0,16},{16,0},{1,17},{17,1},{2,18},{18,2},{3,19},{19,3},{4,20},{20... | collective-permute-start | bytes 1966088 | tf_op jit(solution)/shard_map/ppermute | solution.py:258
  263.0 7.4 %all-to-all-start.14 = ((f32[4,2,256]{2,1,0:T(2,128)}), f32[4,2,256]{2,1,0:T(2,128)S(1)}, u32[]{:S(2)}, u32[]{:S(2)}) async-start(f32[4,2,256]{2,1,0:T(2,128)} %get-tuple-element.29), calls=%async_computation.14 | async-start | bytes 16384 | tf_op jit(solution)/shard_map/all_to_all | solution.py:179
  270.4 11.8 %all-to-all-start.10 = ((bf16[4,4,80,256]{3,2,1,0:T(8,128)(2,1)}), bf16[4,4,80,256]{3,2,1,0:T(8,128)(2,1)S(1)}, u32[]{:S(2)}, u32[]{:S(2)}) async-start(bf16[4,4,80,256]{3,2,1,0:T(8,128)(2,1)} %add_convert_fusion), calls=%async_computation.10 | async-start | bytes 1310720 | tf_op jit(solution)/shard_map/all_to_all | solution.py:179
  282.8 14.9 %all-to-all-start.15 = ((f32[32,2,256]{2,1,0:T(2,128)}), f32[32,2,256]{2,1,0:T(2,128)S(1)}, u32[]{:S(2)}, u32[]{:S(2)}) async-start(f32[32,2,256]{2,1,0:T(2,128)} %broadcast_in_dim.44), calls=%async_computation.15 | async-start | bytes 131072 | tf_op jit(solution)/shard_map/all_to_all | solution.py:179
  306.1 20.6 %all-to-all-start.13 = ((bf16[4,3,224,256]{3,2,1,0:T(8,128)(2,1)}), bf16[4,3,224,256]{3,2,1,0:T(8,128)(2,1)S(1)}, u32[]{:S(2)}, u32[]{:S(2)}) async-start(bf16[4,3,224,256]{3,2,1,0:T(8,128)(2,1)} %get-tuple-element.28), calls=%async_computation.13 | async-start | bytes 2752512 | tf_op jit(solution)/shard_map/all_to_all | solution.py:179
  309.7 26.3 %copy-start.5 = (bf16[20,256]{1,0:T(8,128)(2,1)S(1)}, bf16[20,256]{1,0:T(8,128)(2,1)}, u32[]{:S(2)}) copy-start(bf16[20,256]{1,0:T(8,128)(2,1)} %param.9) | copy-start | bytes 30724
  326.8 5.9 %copy-start.2 = (bf16[4,3,224,256]{3,2,1,0:T(8,128)(2,1)}, bf16[4,3,224,256]{3,2,1,0:T(8,128)(2,1)S(1)}, u32[]{:S(2)}) copy-start(bf16[4,3,224,256]{3,2,1,0:T(8,128)(2,1)S(1)} %all-to-all-done.13.g_ref) | copy-start | bytes 4128772
  326.8 9.2 %all-to-all-start.12 = ((bf16[4,20,256]{2,1,0:T(8,128)(2,1)}), bf16[4,20,256]{2,1,0:T(8,128)(2,1)S(1)}, u32[]{:S(2)}, u32[]{:S(2)}) async-start(bf16[4,20,256]{2,1,0:T(8,128)(2,1)} %copy.64), calls=%async_computation.12 | async-start | bytes 98304 | tf_op jit(solution)/shard_map/all_to_all | solution.py:179

commit v2 on v0

v2 whole, which is shorter than its diff:
```python
import functools

import jax
import jax.numpy as jnp
from jax import lax
from jax.experimental import pallas as pl
from jax.experimental.pallas import tpu as pltpu
from jax.sharding import Mesh, PartitionSpec as P


epsilon = 0.0001
branch_scale = 0.5
bf16 = jnp.bfloat16
f32 = jnp.float32

BLK = ("y", "zl", "core")
REP = ("zh", "x")


def nn(a, b):
    return lax.dot_general(a, b, (((1,), (0,)), ((), ())), preferred_element_type=f32)


def nt(a, b):
    return lax.dot_general(a, b, (((1,), (1,)), ((), ())), preferred_element_type=f32)


def tn(a, b):
    return lax.dot_general(a, b, (((0,), (0,)), ((), ())), preferred_element_type=f32)


def pieces(x):
    high = x.astype(bf16)
    rest = x - high.astype(f32)
    middle = rest.astype(bf16)
    return high, middle, (rest - middle.astype(f32)).astype(bf16)


def joined(rows):
    return rows[0:1].astype(f32) + rows[1:2].astype(f32) + rows[2:3].astype(f32)


def merged(moments, count):
    mean = sum(m for m, _ in moments) * (1.0 / len(moments))
    square = sum(s for _, s in moments)
    for m, _ in moments:
        square = square + count * ((m - mean) * (m - mean))
    return mean, square


def upright(row, tall):
    shape = (tall, row.shape[1])
    same = lax.broadcasted_iota(jnp.int32, shape, 0) == lax.broadcasted_iota(jnp.int32, shape, 1)
    return jnp.sum(jnp.where(same, row, 0.0), axis=1, keepdims=True)


def level(col, wide):
    shape = (col.shape[0], wide)
    same = lax.broadcasted_iota(jnp.int32, shape, 0) == lax.broadcasted_iota(jnp.int32, shape, 1)
    return jnp.sum(jnp.where(same, col, 0.0), axis=0, keepdims=True)


def pack_tokens(tokens_ref, cotangent_ref, gate_ref, up_ref, down_ref, gain_ref, out_ref):
    rows, width = tokens_ref.shape
    scaled = (branch_scale * cotangent_ref[...].astype(f32)).astype(bf16)

    def moments(ref):
        w = ref[...].astype(f32)
        mean = jnp.sum(w, axis=0, keepdims=True) * (1.0 / w.shape[0])
        off = w - mean
        return mean, jnp.sum(off * off, axis=0, keepdims=True)

    def single(x):
        return [p.astype(f32) for p in pieces(x)]

    mean, square = moments(down_ref)
    gain = single(gain_ref[...])
    left = jnp.concatenate([tokens_ref[...].astype(f32), *single(mean), gain[0]], axis=0).astype(bf16)
    right = jnp.concatenate([scaled.astype(f32), *single(square), gain[1]], axis=0).astype(bf16)
    wide = [moments(ref) for ref in (gate_ref, up_ref)]
    blocks, lines = out_ref.shape[0], out_ref.shape[1]
    share = gate_ref.shape[1] // blocks
    for j in range(blocks):
        sides = []
        for side in range(2):
            parts = []
            for pair in wide:
                row = pair[side][:, j * share : (j + 1) * share]
                parts += single(jnp.concatenate([row, jnp.zeros((1, width - share), f32)], axis=1))
            sides.append(jnp.concatenate([*parts, jnp.zeros((2, width), f32)], axis=0).astype(bf16))
        for l in range(lines):
            out_ref[j, l, 0 : rows + 4, 0:width] = left
            out_ref[j, l, 0 : rows + 4, width : 2 * width] = right
            out_ref[j, l, rows + 4 : rows + 12, 0:width] = sides[0]
            out_ref[j, l, rows + 4 : rows + 12, width : 2 * width] = sides[1]


def pack_weights(place_ref, gate_ref, up_ref, down_ref, *refs):
    *outs, store_ref = refs
    blocks, _, share, _ = store_ref.shape
    for at, ref in enumerate((gate_ref, up_ref)):
        turned = ref[...].astype(f32).T.astype(bf16)
        for j in range(blocks):
            store_ref[j, at] = turned[j * share : (j + 1) * share]
    for j in range(blocks):
        store_ref[j, 2] = down_ref[j * share : (j + 1) * share]
    for k in range(blocks):
        outs[k][...] = store_ref[lax.rem(place_ref[1] + k, blocks)]


def repack_tokens(wide_count, tall_count, place_ref, in_ref, out_ref, moment_ref):
    blocks, lines, high, wide = in_ref.shape
    rows = high - 12
    width = wide // 2
    for j in range(blocks):
        source = lax.rem(place_ref[1] + blocks - j, blocks)
        lots = [in_ref[source, l, 0 : rows + 4, :].astype(f32) for l in range(lines)]
        moments = [
            (joined(lot[rows : rows + 3, 0:width]), joined(lot[rows : rows + 3, width:])) for lot in lots
        ]
        mean, square = merged(moments, tall_count)
        zero = jnp.zeros((4, width), f32)
        for extra, a in ((mean, 0), (square, width)):
            parts = [lot[0:rows, a : a + width] for lot in lots]
            parts += [p.astype(f32) for p in pieces(extra)]
            parts += [lots[0][rows + 3 : rows + 4, a : a + width], zero]
            block = jnp.concatenate(parts, axis=0).astype(bf16)
            for y in range(out_ref.shape[0]):
                out_ref[y, j, :, a : a + width] = block
    line = place_ref[2]
    own = [in_ref[j, line, rows + 4 : rows + 12, :].astype(f32) for j in range(blocks)]
    found = []
    for at in range(2):
        moments = [
            (joined(o[3 * at : 3 * at + 3, 0:width]), joined(o[3 * at : 3 * at + 3, width:])) for o in own
        ]
        found += merged(moments, wide_count)
    block = jnp.concatenate([*found, jnp.zeros((4, width), f32)], axis=0)
    moment_ref[...] = block


def whole(own_ref, other_ref, j, at):
    rows = own_ref.shape[2] - 8
    width = own_ref.shape[3] // 2
    halves = [
        ref[:, j, 0:rows, at * width : (at + 1) * width].reshape(-1, width) for ref in (own_ref, other_ref)
    ]
    return jnp.concatenate(halves, axis=0)


def forward(
    wide_count, tall_count, place_ref, w0_ref, w1_ref, w2_ref, w3_ref, own_ref, other_ref,
    moment0_ref, moment1_ref, moment2_ref, moment3_ref, gain_ref,
    kept_ref, near_a_ref, near_b_ref, back_a_ref, back_b_ref, far_a_ref, far_b_ref,
    cols_ref, rows_ref, row_ref, store_ref,
):
    w_ref = (w0_ref, w1_ref, w2_ref, w3_ref)
    blocks = len(w_ref)
    _, share, width = w0_ref.shape
    parts = store_ref.shape[0]
    tall = share // parts
    lane = lax.broadcasted_iota(jnp.int32, cols_ref.shape, 1)
    cols = jnp.zeros(cols_ref.shape, f32)
    row = 0.0
    lefts = [whole(own_ref, other_ref, j, 0) for j in range(blocks)]
    ones = jnp.ones((8, width), bf16)
    for j in range(blocks):
        row = row + nt(ones, lefts[j])
    row_ref[...] = row
    for at in range(2):
        moments = [
            (ref[2 * at : 2 * at + 1, :], ref[2 * at + 1 : 2 * at + 2, :])
            for ref in (moment0_ref, moment1_ref, moment2_ref, moment3_ref)
        ]
        mean, square = merged(moments, wide_count)
        mean = upright(mean, share)
        scale = upright(lax.rsqrt(square + epsilon), share)
        gs = gain_ref[:, at : at + 1] * scale
        for k, v in ((3 * at, mean), (3 * at + 1, gs), (3 * at + 2, scale)):
            cols = jnp.where(lane == k, v, cols)
        total = 0.0
        for j in range(blocks):
            total = total + nt(w_ref[j][at], lefts[j])
        total = ((total - mean * row[0:1]) * gs).astype(bf16)
        for q in range(parts):
            store_ref[q, at * tall : (at + 1) * tall, :] = total[q * tall : (q + 1) * tall]
    cols_ref[...] = cols
    total = 0.0
    rows = own_ref.shape[2] - 8
    for j in range(blocks):
        lots = [
            ref[y, j, rows : rows + 8, :].astype(f32) for ref in (own_ref, other_ref) for y in range(own_ref.shape[0])
        ]
        mean, square = merged([(joined(lot[:, 0:width]), joined(lot[:, width:])) for lot in lots], tall_count)
        scale = lax.rsqrt(square + epsilon)
        gain = lots[0][3:4, 0:width] + lots[0][3:4, width:]
        gs = gain * scale
        rows_ref[j] = jnp.concatenate([mean, gs, scale, jnp.zeros((5, width), f32)], axis=0)
        hat = ((w_ref[j][2].astype(f32) - mean) * gs).astype(bf16)
        total = total + nt(hat, whole(own_ref, other_ref, j, 1))
    total = total.astype(bf16)
    for q in range(parts):
        store_ref[q, 2 * tall : 3 * tall, :] = total[q * tall : (q + 1) * tall]
    at = place_ref[0]
    cut = near_a_ref.shape[0]
    kept_ref[...] = store_ref[at]
    for k, a_ref, b_ref in ((1, near_a_ref, near_b_ref), (2, far_a_ref, far_b_ref), (3, back_a_ref, back_b_ref)):
        q = lax.rem(at + k, parts)
        a_ref[...] = store_ref[q, 0:cut, :]
        b_ref[...] = store_ref[q, cut:, :]


def add_pair(a_ref, b_ref, c_ref, d_ref, left_ref, right_ref):
    left_ref[...] = (a_ref[...].astype(f32) + b_ref[...].astype(f32)).astype(bf16)
    right_ref[...] = (c_ref[...].astype(f32) + d_ref[...].astype(f32)).astype(bf16)


def gating(kept_ref, near_a_ref, near_b_ref, back_a_ref, back_b_ref, row_ref, d_ref):
    tall = (d_ref.shape[0] - 8) // 3
    cut = near_a_ref.shape[0]
    top = kept_ref[0:cut, :].astype(f32) + near_a_ref[...].astype(f32) + back_a_ref[...].astype(f32)
    low = kept_ref[cut:, :].astype(f32) + near_b_ref[...].astype(f32) + back_b_ref[...].astype(f32)
    total = jnp.concatenate([top, low], axis=0)
    gate, up, dhidden = total[0:tall], total[tall : 2 * tall], total[2 * tall : 3 * tall]
    sig = 1.0 / (1.0 + jnp.exp(-gate))
    act = gate * sig
    d_gate = (dhidden * up * sig * (1.0 + gate * (1.0 - sig))).astype(bf16)
    d_up = (dhidden * act).astype(bf16)
    d_ref[2 * tall : 3 * tall, :] = (act * up).astype(bf16)
    d_ref[0:tall, :] = d_gate
    d_ref[tall : 2 * tall, :] = d_up
    dots = [
        level(jnp.sum(d.astype(f32) * v, axis=1, keepdims=True), 128)
        for d, v in ((d_gate, gate), (d_up, up))
    ]
    wide = d_ref.shape[1]
    dots = jnp.concatenate([*dots, jnp.zeros((1, wide - 256), f32)], axis=1)
    extra = [*pieces(dots), *pieces(row_ref[0:1, :])]
    extra = [p.astype(f32) for p in extra] + [jnp.zeros((2, wide), f32)]
    d_ref[3 * tall : 3 * tall + 8, :] = jnp.concatenate(extra, axis=0).astype(bf16)


def stacked(d_ref, at, tall):
    return jnp.concatenate(
        [d_ref[q, at * tall : (at + 1) * tall, :] for q in range(d_ref.shape[0])], axis=0
    )


def token_back(d_ref, w0_ref, w1_ref, w2_ref, w3_ref, cols_ref, mine_ref, theirs_ref):
    w_ref = (w0_ref, w1_ref, w2_ref, w3_ref)
    blocks = len(w_ref)
    _, share, width = w0_ref.shape
    tall = share // d_ref.shape[0]
    streams = [stacked(d_ref, at, tall) for at in range(2)]
    lines, _, rows, _ = mine_ref.shape
    half = lines * rows
    for j in range(blocks):
        back = 0.0
        for at in range(2):
            cent = w_ref[j][at].astype(f32) - cols_ref[:, 3 * at : 3 * at + 1]
            back = back + tn(streams[at], (cent * cols_ref[:, 3 * at + 1 : 3 * at + 2]).astype(bf16))
        mine_ref[:, j] = back[:half].reshape(lines, rows, width)
        theirs_ref[:, j] = back[half:].astype(bf16).reshape(lines, rows, width)


def tall_grads(d_ref, w0_ref, w1_ref, w2_ref, w3_ref, own_ref, other_ref, rows_ref, grad_ref, sums_ref):
    w_ref = (w0_ref, w1_ref, w2_ref, w3_ref)
    blocks = len(w_ref)
    _, share, width = w0_ref.shape
    stream = stacked(d_ref, 2, share // d_ref.shape[0])
    for j in range(blocks):
        p = nn(stream, whole(own_ref, other_ref, j, 1))
        cent = w_ref[j][2].astype(f32) - rows_ref[j, 0:1, :]
        summed = jnp.sum(p, axis=0, keepdims=True)
        crossed = jnp.sum(p * cent, axis=0, keepdims=True)
        sums_ref[j] = jnp.concatenate([summed, crossed, jnp.zeros((6, width), f32)], axis=0)
        grad_ref[j] = p.astype(bf16)


def wide_grads(width_all, d_ref, w0_ref, w1_ref, w2_ref, w3_ref, own_ref, other_ref, cols_ref, down_ref, g0_ref, g1_ref, g2_ref, g3_ref, dots_ref):
    w_ref = (w0_ref, w1_ref, w2_ref, w3_ref)
    grad_ref = (g0_ref, g1_ref, g2_ref, g3_ref)
    blocks = len(w_ref)
    _, share, _ = w0_ref.shape
    parts = d_ref.shape[0]
    tall = share // parts
    streams = [stacked(d_ref, at, tall) for at in range(2)]
    extra = [d_ref[q, 3 * tall : 3 * tall + 8, :].astype(f32) for q in range(parts)]
    row = sum(joined(e[3:6]) for e in extra)
    dots_ref[...] = jnp.zeros(dots_ref.shape, f32)
    means, pulls = [], []
    for at in range(2):
        means.append(jnp.sum(streams[at].astype(f32) * row, axis=1, keepdims=True) * (1.0 / width_all))
        dot = jnp.concatenate(
            [upright(joined(e[0:3, 128 * at : 128 * (at + 1)]), tall) for e in extra], axis=0
        )
        dots_ref[at : at + 1, :] = level(dot, dots_ref.shape[1])
        s = cols_ref[:, 3 * at + 2 : 3 * at + 3]
        pulls.append(s * s * dot)
    for j in range(blocks):
        left = whole(own_ref, other_ref, j, 0)
        for at in range(2):
            p = nn(streams[at], left)
            cent = w_ref[j][at].astype(f32) - cols_ref[:, 3 * at : 3 * at + 1]
            grad = cols_ref[:, 3 * at + 1 : 3 * at + 2] * (p - means[at]) - cent * pulls[at]
            grad_ref[j][at] = grad.astype(bf16)
        grad_ref[j][2] = down_ref[j]


def both_cores(mine_ref, theirs_ref, sums_ref, other_ref, out_ref):
    lines, blocks, rows, _ = mine_ref.shape
    for j in range(blocks):
        total = sums_ref[j] + other_ref[j]
        extra = [p.astype(f32) for k in range(2) for p in pieces(total[k : k + 1, :])]
        extra = jnp.concatenate([*extra, total[2:4, :]], axis=0).astype(bf16)
        for y in range(lines):
            out_ref[y, j, 0:rows, :] = (mine_ref[y, j] + theirs_ref[y, j].astype(f32)).astype(bf16)
            out_ref[y, j, rows : rows + 8, :] = extra


def whole_column(place_ref, in_ref, dots_ref, out_ref):
    lines, blocks, high, _ = in_ref.shape
    dots = [p.astype(f32) for k in range(2) for p in pieces(dots_ref[k : k + 1, :])]
    cuts = out_ref.shape[0]
    rows = (high - 8) // cuts
    for j in range(blocks):
        lots = [in_ref[y, j].astype(f32) for y in range(lines)]
        back = sum(lot[0 : high - 8] for lot in lots)
        extra = []
        for k in range(2):
            total = sum(joined(lot[high - 8 + 3 * k : high - 5 + 3 * k]) for lot in lots)
            extra += [p.astype(f32) for p in pieces(total)]
        for l in range(cuts):
            out_ref[l, lax.rem(place_ref[1] + blocks - j, blocks)] = jnp.concatenate([back[l * rows : (l + 1) * rows], *extra, *dots], axis=0).astype(bf16)


def finish_wide(place_ref, g0_ref, g1_ref, g2_ref, g3_ref, gate_ref, up_ref, store_ref):
    g_ref = (g0_ref, g1_ref, g2_ref, g3_ref)
    for at, ref in enumerate((gate_ref, up_ref)):
        for k, g in enumerate(g_ref):
            store_ref[lax.rem(place_ref[1] + k, len(g_ref))] = g[at].astype(f32)
        ref[...] = store_ref[...].reshape(-1, store_ref.shape[2]).T


def finish_tall(
    hidden_all, place_ref, in_ref, cotangent_ref, g0_ref, g1_ref, g2_ref, g3_ref, down_ref, rows_ref, gain_ref,
    tokens_ref, grad_ref, dgain_ref, dots_ref,
):
    lines, blocks, _, _ = in_ref.shape
    rows = tokens_ref.shape[0]
    lots = [in_ref[l, j].astype(f32) for l in range(lines) for j in range(blocks)]
    total = sum(lots)
    tokens_ref[...] = cotangent_ref[...].astype(f32) + total[0:rows]
    summed, crossed = (sum(joined(lot[rows + 3 * k : rows + 3 * k + 3]) for lot in lots) for k in range(2))
    line = place_ref[2]
    for j in range(blocks):
        own = in_ref[line, j].astype(f32)
        dots_ref[0:1, j, :] = joined(own[rows + 6 : rows + 9])
        dots_ref[1:2, j, :] = joined(own[rows + 9 : rows + 12])
    mine = rows_ref[0]
    mean, scale = mine[0:1, :], mine[2:3, :]
    gain = gain_ref[...]
    dgain_ref[...] = scale * crossed
    g_ref = (g0_ref, g1_ref, g2_ref, g3_ref)
    for k, g in enumerate(g_ref):
        j = lax.rem(place_ref[1] + k, len(g_ref))
        cent = down_ref[j].astype(f32) - mean
        grad_ref[j] = scale * gain * (g[2].astype(f32) - summed * (1.0 / hidden_all)) - (
            scale * scale * scale * gain * crossed
        ) * cent


def call(body, outs, *args, place=None, scratch=()):
    specs = [pl.BlockSpec(memory_space=pltpu.VMEM)] * len(args)
    if place is not None:
        args = (place, *args)
        specs = [pl.BlockSpec(memory_space=pltpu.SMEM), *specs]
    return pl.pallas_call(
        body,
        out_shape=[jax.ShapeDtypeStruct(s, t) for s, t in outs],
        in_specs=specs,
        scratch_shapes=scratch,
    )(*args)


def exchange(x, axis):
    return lax.all_to_all(x, axis, split_axis=0, concat_axis=0, tiled=True)


def shift(x, axis, by):
    size = lax.axis_size(axis)
    return lax.ppermute(x, axis, [(i, (i + by) % size) for i in range(size)])


def block(tokens, cotangent, gate_weight, up_weight, down_weight, gate_gain, up_gain, down_gain):
    rows, width = tokens.shape
    hidden = gate_weight.shape[1]
    nx, nz, ny = lax.axis_size("x"), lax.axis_size("zh"), lax.axis_size("y")
    nl, nc = lax.axis_size("zl"), lax.axis_size("core")
    width_all = width * nx * nz
    hidden_all = hidden * ny * nl * nc
    share = hidden // nx
    tall = share // nz
    count = rows * ny * nl * nc
    place = jnp.stack([lax.axis_index("zh"), lax.axis_index("x"), lax.axis_index("zl")]).astype(jnp.int32)
    swap = [(0, 1), (1, 0)]

    def grid_exchange(x, axes):
        flat = exchange(x.reshape(x.shape[0] * x.shape[1], *x.shape[2:]), axes)
        return flat.reshape(x.shape)

    (both,) = call(
        pack_tokens, [((nx, nl, rows + 12, 2 * width), bf16)],
        tokens, cotangent, gate_weight, up_weight, down_weight, down_gain.reshape(1, width),
    )
    both = grid_exchange(both, ("x", "zl"))
    cut_weights = call(
        pack_weights, [((3, share, width), bf16)] * nx, gate_weight, up_weight, down_weight,
        place=place, scratch=[pltpu.VMEM((nx, 3, share, width), bf16)],
    )
    weights = [cut_weights[0], *(shift(cut_weights[k], "x", k) for k in (1, 2, 3))]
    both, moments = call(
        functools.partial(repack_tokens, width, hidden),
        [((ny, nx, nl * rows + 8, 2 * width), bf16), ((8, width), f32)], both, place=place,
    )
    own = exchange(both, "y")
    moments = [moments, *(shift(moments, "zh", k) for k in (1, 2, 3))]
    other = lax.ppermute(own, "core", swap)
    gains = jnp.stack([gate_gain.reshape(nx, share)[place[1]], up_gain.reshape(nx, share)[place[1]]], axis=1)

    cut = 88
    a, b = ((cut, count), bf16), ((3 * tall - cut, count), bf16)
    kept, near_a, near_b, back_a, back_b, far_a, far_b, cols, rows_of, row = call(
        functools.partial(forward, width * nx, hidden * nl),
        [
            ((3 * tall, count), bf16), a, b, a, b, a, b,
            ((share, 128), f32), ((nx, 8, width), f32), ((8, count), f32),
        ],
        *weights, own, other, *moments, gains,
        place=place,
        scratch=[pltpu.VMEM((nz, 3 * tall, count), bf16)],
    )
    far_a = shift(far_a, "zh", 1)
    far_b = shift(far_b, "zh", -1)
    near_b = shift(near_b, "zh", 1)
    back_a = shift(back_a, "zh", -1)
    near_a, back_b = call(add_pair, [a, b], near_a, far_a, back_b, far_b)
    near_a = shift(near_a, "zh", 1)
    back_b = shift(back_b, "zh", -1)
    (d,) = call(gating, [((3 * tall + 8, count), bf16)], kept, near_a, near_b, back_a, back_b, row)
    d = lax.all_gather(d, "zh")

    shape = (ny, nx, nl * rows, width)
    mine, theirs = call(token_back, [(shape, f32), (shape, bf16)], d, *weights, cols)
    theirs = lax.ppermute(theirs, "core", swap)
    down_grads, sums = call(
        tall_grads, [((nx, share, width), bf16), ((nx, 8, width), f32)], d, *weights, own, other, rows_of
    )
    other_sums = lax.ppermute(sums, "core", swap)
    (back,) = call(both_cores, [((ny, nx, nl * rows + 8, width), bf16)], mine, theirs, sums, other_sums)
    back = exchange(back, "y")
    *grads, dots = call(
        functools.partial(wide_grads, width_all), [((3, share, width), bf16)] * nx + [((8, width), f32)],
        d, *weights, own, other, cols, down_grads,
    )
    grads = [grads[0], *(shift(grads[k], "x", -k) for k in (1, 2, 3))]
    (back,) = call(whole_column, [((nl, nx, rows + 12, width), bf16)], back, dots, place=place)
    back = grid_exchange(back, ("zl", "x"))
    grad_gate, grad_up = call(
        finish_wide, [((width, hidden), f32), ((width, hidden), f32)], *grads,
        place=place, scratch=[pltpu.VMEM((nx, share, width), f32)],
    )
    grad_tokens, grad_down, down_dgain, dots = call(
        functools.partial(finish_tall, hidden_all),
        [((rows, width), f32), ((nx, share, width), f32), ((1, width), f32), ((2, nx, width), f32)],
        back, cotangent, *grads, down_weight.reshape(nx, share, width), rows_of, down_gain.reshape(1, width),
        place=place,
    )
    dots = dots[:, :, :share].reshape(2, hidden)
    return (
        grad_tokens,
        grad_gate,
        grad_up,
        grad_down.reshape(hidden, width),
        dots[0] / gate_gain,
        dots[1] / up_gain,
        down_dgain.reshape(width),
    )


def solution(mesh):
    fine = Mesh(mesh.devices.reshape(4, 4, 2, 4, 4), (*BLK, *REP))
    return jax.shard_map(
        block,
        mesh=fine,
        in_specs=(
            P(BLK, REP), P(BLK, REP), P(REP, BLK), P(REP, BLK), P(BLK, REP), P(BLK), P(BLK), P(REP),
        ),
        out_specs=(
            P(BLK, REP), P(REP, BLK), P(REP, BLK), P(BLK, REP), P(BLK), P(BLK), P(REP),
        ),
        check_vma=False,
    )
```

time: 534 us -> 263 us (0.49)
  waiting for transfers between devices: 387 us -> 60.7 us
  starting transfers between devices: 50.3 us -> 96.3 us
  Pallas kernels: 0 us -> 39.9 us
  matrix products: 14.7 us -> 0 us
  other arithmetic: 15.3 us -> 1.83 us
  between operations: 14.3 us -> 0.97 us
  blocking collectives: 46.4 us -> 53.2 us
    psum x1 -> x0, waiting for transfers between devices: 359 us -> none  [local(): lax.psum(up_part, 'replica').astype(jnp.float32)]
    ppermute x0 -> x18, starting transfers between devices: none -> 79.6 us  [the longest x15 70 us: shift(): return lax.ppermute(x, axis, [(i, (i + by) % size) for i in range(size)])]
    pallas_call x0 -> x13, Pallas kernels: none -> 39.9 us  [call(): pl.pallas_call(body, out_shape=[jax.ShapeDtypeStruct(s, t) for s, t in ou...]
    ppermute x0 -> x18, waiting for transfers between devices: none -> 38.9 us  [the longest x15 37.5 us: shift(): return lax.ppermute(x, axis, [(i, (i + by) % size) for i in range(size)])]
    all_to_all x5 -> x3, starting transfers between devices: 50.3 us -> 16.8 us  [exchange(): return lax.all_to_all(x, axis, split_axis=0, concat_axis=0, tiled=True)]
    all_to_all x0 -> x1, blocking collectives: none -> 21.8 us  [exchange(): return lax.all_to_all(x, axis, split_axis=0, concat_axis=0, tiled=True)]
    all_gather x1, blocking collectives: 46.4 us -> 31.4 us  [block(): d = lax.all_gather(d, 'zh')]
    dot_general x8 -> x0, matrix products: 14.7 us -> none  [the longest x3 6.88 us: contract_first(): lax.dot_general(left, right, (((0,), (0,)), ((), ())), preferred_element_...]
  transfers between devices with their start and end apart: 6 -> 21, of which waited for: 5 -> 11; matrix products, arithmetic and copies ran while one was open for 4% -> 1% of each run, Pallas kernels for 0% -> 6%
where the time goes in v2:
time: 263 us; the launch traced here: 261 us
  starting transfers between devices  96.3 us (37%)
  waiting for transfers between devices  60.7 us (23%)
  blocking collectives  53.2 us (20%)
  Pallas kernels  39.9 us (15%)
  local copies, waits for them, and re-layouts  8.19 us (3%)
    ppermute x15, starting transfers between devices, shift(): return lax.ppermute(x, axis, [(i, (i + by) % size) for i in range(size)])  70 us
    pallas_call x13, Pallas kernels, call(): pl.pallas_call(body, out_shape=[jax.ShapeDtypeStruct(s, t) for s, t in ou...  39.9 us
    ppermute x15, waiting for transfers between devices, shift(): return lax.ppermute(x, axis, [(i, (i + by) % size) for i in range(size)])  37.5 us
    all_gather x1, blocking collectives, block(): d = lax.all_gather(d, 'zh')  31.4 us
    all_to_all x3, waiting for transfers between devices, exchange(): return lax.all_to_all(x, axis, split_axis=0, concat_axis=0, tiled=True)  21.8 us
    all_to_all x1, blocking collectives, exchange(): return lax.all_to_all(x, axis, split_axis=0, concat_axis=0, tiled=True)  21.8 us
    all_to_all x3, starting transfers between devices, exchange(): return lax.all_to_all(x, axis, split_axis=0, concat_axis=0, tiled=True)  16.8 us
    unnamed x52, local copies, waits for them, and re-layouts  6.4 us
  transfers between devices with their start and end apart: 21, of which 11 were waited for; matrix products, arithmetic and copies ran while one was open for 1% of the time, Pallas kernels for 6%

profile of v2, /device:TPU:1, one launch (start us, length us, event | category | flops | bytes accessed | tf_op | source)
XLA Modules:
  0.0 261.2 jit_solution(17099623778689786306)
XLA Ops:
  0.6 3.0 %shard_map.136 = bf16[4,4,32,512]{3,2,1,0:T(8,128)(2,1)} custom-call(bf16[20,256]{1,0:T(8,128)(2,1)} %tokens_ref.1, bf16[20,256]{1,0:T(8,128)(2,1)} %cotangent_ref.3, bf16[256,896]{1,0:T(8,128)(2,1)} %gate_ref.3, bf16[256,896]{1,0:T(8,128)(2,1)} %up_ref.3, bf16[896,256]{1,0:T(8,128)(2,1)} %down_ref.3, f32[1,256]{1,0:T(1,128)} %bitcast.24), custom_call_target="tpu_custom_call" | custom-call | tf_op jit(solution)/shard_map/pallas_call | solution.py:378
  3.6 9.0 %all-to-all-start = ((bf16[16,32,512]{2,1,0:T(8,128)(2,1)}), bf16[16,32,512]{2,1,0:T(8,128)(2,1)S(1)}, u32[]{:S(2)}, u32[]{:S(2)}) async-start(bf16[16,32,512]{2,1,0:T(8,128)(2,1)} %bitcast.20), calls=%async_computation | async-start | bytes 1048576 | tf_op jit(solution)/shard_map/all_to_all | solution.py:387
  13.2 15.1 %all-to-all-done = bf16[16,32,512]{2,1,0:T(8,128)(2,1)S(1)} async-done(((bf16[16,32,512]{2,1,0:T(8,128)(2,1)}), bf16[16,32,512]{2,1,0:T(8,128)(2,1)S(1)}, u32[]{:S(2)}, u32[]{:S(2)}) %all-to-all-start) | async-done | bytes 524320 | tf_op jit(solution)/shard_map/all_to_all | solution.py:387
  31.5 21.8 %all_to_all.20.own_ref = bf16[4,4,88,512]{3,2,1,0:T(8,128)(2,1)S(1)} all-to-all(bf16[4,4,88,512]{3,2,1,0:T(8,128)(2,1)} %get-tuple-element.44), channel_id=1, replica_groups=mesh['y'=4,'zl'=4,'core'=2,'zh'=4,'x'=4] {'y'}, dimensions={0} | all-to-all | bytes 2883584 | tf_op jit(solution)/shard_map/all_to_all | solution.py:387
  53.3 4.7 %collective-permute-start.3 = (bf16[4,4,88,512]{3,2,1,0:T(8,128)(2,1)S(1)}, bf16[4,4,88,512]{3,2,1,0:T(8,128)(2,1)S(1)}, u32[]{:S(2)}, u32[]{:S(2)}) collective-permute-start(bf16[4,4,88,512]{3,2,1,0:T(8,128)(2,1)S(1)} %all_to_all.20.own_ref), channel_id=1, source_target_pairs={{0,16},{16,0},{1,17},{17,1},{2,18},{18,2},{3,19},{19,3},{4,20},{20... | collective-permute-start | bytes 4325384 | tf_op jit(solution)/shard_map/ppermute | solution.py:428
  62.8 3.7 %collective-permute-start.1 = (bf16[3,224,256]{2,1,0:T(8,128)(2,1)}, bf16[3,224,256]{2,1,0:T(8,128)(2,1)}, u32[]{:S(2)}, u32[]{:S(2)}) collective-permute-start(bf16[3,224,256]{2,1,0:T(8,128)(2,1)} %get-tuple-element.42), channel_id=1, source_target_pairs={{0,2},{1,3},{2,0},{3,1},{4,6},{5,7},{6,4},{7,5},{8,10},{9,11},{10,... | collective-permute-start | bytes 1032200 | tf_op jit(solution)/shard_map/ppermute | solution.py:392
  69.5 9.8 %collective-permute-start.6 = (f32[8,256]{1,0:T(8,128)S(1)}, f32[8,256]{1,0:T(8,128)S(1)}, u32[]{:S(2)}, u32[]{:S(2)}) collective-permute-start(f32[8,256]{1,0:T(8,128)S(1)} %copy-done.19), channel_id=1, source_target_pairs={{0,12},{4,0},{8,4},{12,8},{1,13},{5,1},{9,5},{13,9},{2,14},{6,2},{... | collective-permute-start | bytes 24584 | tf_op jit(solution)/shard_map/ppermute | solution.py:392
  81.2 12.7 %collective-permute-start.5 = (f32[8,256]{1,0:T(8,128)S(1)}, f32[8,256]{1,0:T(8,128)S(1)}, u32[]{:S(2)}, u32[]{:S(2)}) collective-permute-start(f32[8,256]{1,0:T(8,128)S(1)} %copy-done.19), channel_id=1, source_target_pairs={{0,8},{4,12},{8,0},{12,4},{1,9},{5,13},{9,1},{13,5},{2,10},{6,14},... | collective-permute-start | bytes 24584 | tf_op jit(solution)/shard_map/ppermute | solution.py:392
  93.9 4.0 %collective-permute-start.4 = (f32[8,256]{1,0:T(8,128)S(1)}, f32[8,256]{1,0:T(8,128)S(1)}, u32[]{:S(2)}, u32[]{:S(2)}) collective-permute-start(f32[8,256]{1,0:T(8,128)S(1)} %copy-done.19), channel_id=1, source_target_pairs={{0,4},{4,8},{8,12},{12,0},{1,5},{5,9},{9,13},{13,1},{2,6},{6,10},{... | collective-permute-start | bytes 24584 | tf_op jit(solution)/shard_map/ppermute | solution.py:392
  98.8 3.5 %collective-permute-done.4.moment1_ref = f32[8,256]{1,0:T(8,128)S(1)} collective-permute-done((f32[8,256]{1,0:T(8,128)S(1)}, f32[8,256]{1,0:T(8,128)S(1)}, u32[]{:S(2)}, u32[]{:S(2)}) %collective-permute-start.4) | collective-permute-done | bytes 8224 | tf_op jit(solution)/shard_map/ppermute | solution.py:392
  103.4 4.9 %shard_map.138 = (bf16[168,640]{1,0:T(8,128)(2,1)}, bf16[88,640]{1,0:T(8,128)(2,1)}, bf16[80,640]{1,0:T(8,128)(2,1)}, bf16[88,640]{1,0:T(8,128)(2,1)}, bf16[80,6...) custom-call(s32[3]{0:T(128)} %pad_add_fusion.place_ref, ...), custom_call_target="tpu_custom_call" | custom-call | tf_op jit(solution)/shard_map/pallas_call | solution.py:378
  108.3 4.0 %collective-permute-start.7 = (bf16[88,640]{1,0:T(8,128)(2,1)}, bf16[88,640]{1,0:T(8,128)(2,1)S(1)}, u32[]{:S(2)}, u32[]{:S(2)}) collective-permute-start(bf16[88,640]{1,0:T(8,128)(2,1)} %get-tuple-element.48), channel_id=1, source_target_pairs={{0,4},{4,8},{8,12},{12,0},{1,5},{5,9},{9,13},{13,1},{2,6},{6,10},{... | collective-permute-start | bytes 337928 | tf_op jit(solution)/shard_map/ppermute | solution.py:392
  112.3 5.2 %collective-permute-start.8 = (bf16[80,640]{1,0:T(8,128)(2,1)}, bf16[80,640]{1,0:T(8,128)(2,1)S(1)}, u32[]{:S(2)}, u32[]{:S(2)}) collective-permute-start(bf16[80,640]{1,0:T(8,128)(2,1)} %get-tuple-element.50), channel_id=1, source_target_pairs={{0,12},{4,0},{8,4},{12,8},{1,13},{5,1},{9,5},{13,9},{2,14},{6,2},{... | collective-permute-start | bytes 307208 | tf_op jit(solution)/shard_map/ppermute | solution.py:392
  117.5 3.4 %collective-permute-start.11 = (bf16[88,640]{1,0:T(8,128)(2,1)}, bf16[88,640]{1,0:T(8,128)(2,1)S(1)}, u32[]{:S(2)}, u32[]{:S(2)}) collective-permute-start(bf16[88,640]{1,0:T(8,128)(2,1)} %get-tuple-element.53), channel_id=1, source_target_pairs={{0,12},{4,0},{8,4},{12,8},{1,13},{5,1},{9,5},{13,9},{2,14},{6,2},{... | collective-permute-start | bytes 337928 | tf_op jit(solution)/shard_map/ppermute | solution.py:392
  120.9 8.6 %collective-permute-done.8.d_ref = bf16[80,640]{1,0:T(8,128)(2,1)S(1)} collective-permute-done((bf16[80,640]{1,0:T(8,128)(2,1)}, bf16[80,640]{1,0:T(8,128)(2,1)S(1)}, u32[]{:S(2)}, u32[]{:S(2)}) %collective-permute-start.8) | collective-permute-done | bytes 102432 | tf_op jit(solution)/shard_map/ppermute | solution.py:392
  131.9 3.9 %collective-permute-start.9 = (bf16[88,640]{1,0:T(8,128)(2,1)}, bf16[88,640]{1,0:T(8,128)(2,1)S(1)}, u32[]{:S(2)}, u32[]{:S(2)}) collective-permute-start(bf16[88,640]{1,0:T(8,128)(2,1)} %get-tuple-element.51), channel_id=1, source_target_pairs={{0,4},{4,8},{8,12},{12,0},{1,5},{5,9},{9,13},{13,1},{2,6},{6,10},{... | collective-permute-start | bytes 337928 | tf_op jit(solution)/shard_map/ppermute | solution.py:392
  135.8 4.5 %collective-permute-start.10 = (bf16[80,640]{1,0:T(8,128)(2,1)}, bf16[80,640]{1,0:T(8,128)(2,1)S(1)}, u32[]{:S(2)}, u32[]{:S(2)}) collective-permute-start(bf16[80,640]{1,0:T(8,128)(2,1)} %get-tuple-element.52), channel_id=1, source_target_pairs={{0,4},{4,8},{8,12},{12,0},{1,5},{5,9},{9,13},{13,1},{2,6},{6,10},{... | collective-permute-start | bytes 307208 | tf_op jit(solution)/shard_map/ppermute | solution.py:392
  140.3 4.7 %collective-permute-start.12 = (bf16[80,640]{1,0:T(8,128)(2,1)}, bf16[80,640]{1,0:T(8,128)(2,1)S(1)}, u32[]{:S(2)}, u32[]{:S(2)}) collective-permute-start(bf16[80,640]{1,0:T(8,128)(2,1)} %get-tuple-element.54), channel_id=1, source_target_pairs={{0,12},{4,0},{8,4},{12,8},{1,13},{5,1},{9,5},{13,9},{2,14},{6,2},{... | collective-permute-start | bytes 307208 | tf_op jit(solution)/shard_map/ppermute | solution.py:392
  145.0 4.9 %collective-permute-done.10.near_b_ref = bf16[80,640]{1,0:T(8,128)(2,1)S(1)} collective-permute-done((bf16[80,640]{1,0:T(8,128)(2,1)}, bf16[80,640]{1,0:T(8,128)(2,1)S(1)}, u32[]{:S(2)}, u32[]{:S(2)}) %collective-permute-start.10) | collective-permute-done | bytes 102432 | tf_op jit(solution)/shard_map/ppermute | solution.py:392
  155.3 31.4 %all-gather = bf16[704,640]{1,0:T(8,128)(2,1)} all-gather(bf16[176,640]{1,0:T(8,128)(2,1)} %shard_map.140), channel_id=2, replica_groups=mesh['y'=4,'zl'=4,'core'=2,'zh'=4,'x'=4] {'zh'}, dimensions={0}, use_global_device_ids=true | all-gather | bytes 1126400 | tf_op jit(solution)/shard_map/all_gather | solution.py:451
  186.8 4.0 %shard_map.141 = (f32[4,4,80,256]{3,2,1,0:T(8,128)}, bf16[4,4,80,256]{3,2,1,0:T(8,128)(2,1)}) custom-call(bf16[4,176,640]{2,1,0:T(8,128)(2,1)} %bitcast.16, bf16[3,224,256]{2,1,0:T(8,128)(2,1)} %get-tuple-element.40.w0_ref, bf16[3,224,256]{2,1,0:T(8,128)(2,1)} %copy-done.2, bf16[3,224,256]{2,1,0:T(8,128)(2,1)} %collective-permute-done.1.w2_ref, ...), custom_call_target="tpu_custom_call" | custom-call | tf_op jit(solution)/shard_map/pallas_call | solution.py:378
  190.8 3.0 %collective-permute-start.13 = (bf16[4,4,80,256]{3,2,1,0:T(8,128)(2,1)}, bf16[4,4,80,256]{3,2,1,0:T(8,128)(2,1)S(1)}, u32[]{:S(2)}, u32[]{:S(2)}) collective-permute-start(bf16[4,4,80,256]{3,2,1,0:T(8,128)(2,1)} %get-tuple-element.58), channel_id=1, source_target_pairs={{0,16},{16,0},{1,17},{17,1},{2,18},{18,2},{3,19},{19,3},{4,20},{20... | collective-permute-start | bytes 1966088 | tf_op jit(solution)/shard_map/ppermute | solution.py:455
  193.7 3.8 %shard_map.142 = (bf16[4,224,256]{2,1,0:T(8,128)(2,1)}, f32[4,8,256]{2,1,0:T(8,128)}) custom-call(bf16[4,176,640]{2,1,0:T(8,128)(2,1)} %bitcast.17, bf16[3,224,256]{2,1,0:T(8,128)(2,1)} %get-tuple-element.40.w0_ref, bf16[3,224,256]{2,1,0:T(8,128)(2,1)} %copy-done.2, bf16[3,224,256]{2,1,0:T(8,128)(2,1)} %collective-permute-done.1.w2_ref, ...), custom_call_target="tpu_custom_call" | custom-call | tf_op jit(solution)/shard_map/pallas_call | solution.py:378
  204.2 3.5 %all-to-all-start.2 = ((bf16[4,4,88,256]{3,2,1,0:T(8,128)(2,1)}), bf16[4,4,88,256]{3,2,1,0:T(8,128)(2,1)S(1)}, u32[]{:S(2)}, u32[]{:S(2)}) async-start(bf16[4,4,88,256]{3,2,1,0:T(8,128)(2,1)} %shard_map.143), calls=%async_computation.2 | async-start | bytes 1441792 | tf_op jit(solution)/shard_map/all_to_all | solution.py:387
  207.7 4.8 %shard_map.144 = (bf16[3,224,256]{2,1,0:T(8,128)(2,1)}, bf16[3,224,256]{2,1,0:T(8,128)(2,1)}, bf16[3,224,256]{2,1,0:T(8,128)(2,1)}, bf16[3,224,256]{2,1,0:T(8,128)(2,1)}, f32[8,256]{1,0:T(8,128)}) custom-call(bf16[4,176,640]{2,1,0:T(8,128)(2,1)} %bitcast.18, bf16[3,224,256]{2,1,0:T(8,128)(2,1)} %get-tuple-element.40.w0_ref, bf16[3,224,256]{2,1,0:T(8,128)(2,1)} %copy-done.2, ...), custom_call_target="tpu_custom_call" | custom-call | tf_op jit(solution)/shard_map/pallas_call | solution.py:378
  212.5 6.7 %all-to-all-done.2.in_ref = bf16[4,4,88,256]{3,2,1,0:T(8,128)(2,1)S(1)} async-done(((bf16[4,4,88,256]{3,2,1,0:T(8,128)(2,1)}), bf16[4,4,88,256]{3,2,1,0:T(8,128)(2,1)S(1)}, u32[]{:S(2)}, u32[]{:S(2)}) %all-to-all-start.2) | async-done | bytes 720928 | tf_op jit(solution)/shard_map/all_to_all | solution.py:387
  222.0 4.3 %all-to-all-start.3 = ((bf16[16,32,256]{2,1,0:T(8,128)(2,1)}), bf16[16,32,256]{2,1,0:T(8,128)(2,1)S(1)}, u32[]{:S(2)}, u32[]{:S(2)}) async-start(bf16[16,32,256]{2,1,0:T(8,128)(2,1)} %bitcast.23), calls=%async_computation.3 | async-start | bytes 524288 | tf_op jit(solution)/shard_map/all_to_all | solution.py:387
  226.3 4.5 %collective-permute-start.15 = (bf16[3,224,256]{2,1,0:T(8,128)(2,1)S(1)}, bf16[3,224,256]{2,1,0:T(8,128)(2,1)S(1)}, u32[]{:S(2)}, u32[]{:S(2)}) collective-permute-start(bf16[3,224,256]{2,1,0:T(8,128)(2,1)S(1)} %copy-done.25), channel_id=1, source_target_pairs={{0,3},{1,0},{2,1},{3,2},{4,7},{5,4},{6,5},{7,6},{8,11},{9,8},{10,9... | collective-permute-start | bytes 1032200 | tf_op jit(solution)/shard_map/ppermute | solution.py:392
  235.8 3.8 %collective-permute-done.15.g1_ref = bf16[3,224,256]{2,1,0:T(8,128)(2,1)S(1)} collective-permute-done((bf16[3,224,256]{2,1,0:T(8,128)(2,1)S(1)}, bf16[3,224,256]{2,1,0:T(8,128)(2,1)S(1)}, u32[]{:S(2)}, u32[]{:S(2)}) %collective-permute-start.15) | collective-permute-done | bytes 344096 | tf_op jit(solution)/shard_map/ppermute | solution.py:392
  239.6 3.1 %collective-permute-done.16.g2_ref = bf16[3,224,256]{2,1,0:T(8,128)(2,1)S(1)} collective-permute-done((bf16[3,224,256]{2,1,0:T(8,128)(2,1)S(1)}, bf16[3,224,256]{2,1,0:T(8,128)(2,1)S(1)}, u32[]{:S(2)}, u32[]{:S(2)}) %collective-permute-start.16) | collective-permute-done | bytes 344096 | tf_op jit(solution)/shard_map/ppermute | solution.py:392
  242.7 9.2 %collective-permute-done.17.g3_ref = bf16[3,224,256]{2,1,0:T(8,128)(2,1)S(1)} collective-permute-done((bf16[3,224,256]{2,1,0:T(8,128)(2,1)S(1)}, bf16[3,224,256]{2,1,0:T(8,128)(2,1)S(1)}, u32[]{:S(2)}, u32[]{:S(2)}) %collective-permute-start.17) | collective-permute-done | bytes 344096 | tf_op jit(solution)/shard_map/ppermute | solution.py:392
  252.6 3.1 %shard_map.147 = (f32[256,896]{1,0:T(8,128)}, f32[256,896]{1,0:T(8,128)}) custom-call(s32[3]{0:T(128)} %pad_add_fusion.place_ref, bf16[3,224,256]{2,1,0:T(8,128)(2,1)} %get-tuple-element.63.g0_ref, bf16[3,224,256]{2,1,0:T(8,128)(2,1)} %copy-done.5, bf16[3,224,256]{2,1,0:T(8,128)(2,1)} %copy-done.6, bf16[3,224,256]{2,1,0:T(8,128)(2,1)} %copy-done.7), custom_call_target="tpu_custom_call" | custom-call | tf_op jit(solution)/shard_map/pallas_call | solution.py:378
  (88 shorter events, 44.0 us)
Async XLA Ops:
  3.6 24.8 %all-to-all-start = ((bf16[16,32,512]{2,1,0:T(8,128)(2,1)}), bf16[16,32,512]{2,1,0:T(8,128)(2,1)S(1)}, u32[]{:S(2)}, u32[]{:S(2)}) async-start(bf16[16,32,512]{2,1,0:T(8,128)(2,1)} %bitcast.20), calls=%async_computation | async-start | bytes 1048576 | tf_op jit(solution)/shard_map/all_to_all | solution.py:387
  31.5 37.8 %copy-start.18 = (f32[896]{0:T(1024)S(1)}, f32[896]{0:T(1024)}, u32[]{:S(2)}) copy-start(f32[896]{0:T(1024)} %param.13) | copy-start | bytes 10756
  31.5 37.9 %copy-start.17 = (f32[896]{0:T(1024)S(1)}, f32[896]{0:T(1024)}, u32[]{:S(2)}) copy-start(f32[896]{0:T(1024)} %param.14) | copy-start | bytes 10756
  31.5 38.0 %copy-start.19 = (f32[8,256]{1,0:T(8,128)S(1)}, f32[8,256]{1,0:T(8,128)}, u32[]{:S(2)}) copy-start(f32[8,256]{1,0:T(8,128)} %get-tuple-element.45.moment0_ref) | copy-start | bytes 24580
  53.3 48.9 %copy-start = (bf16[4,4,88,512]{3,2,1,0:T(8,128)(2,1)}, bf16[4,4,88,512]{3,2,1,0:T(8,128)(2,1)S(1)}, u32[]{:S(2)}) copy-start(bf16[4,4,88,512]{3,2,1,0:T(8,128)(2,1)S(1)} %all_to_all.20.own_ref) | copy-start | bytes 4325380
  53.3 48.9 %collective-permute-start.3 = (bf16[4,4,88,512]{3,2,1,0:T(8,128)(2,1)S(1)}, bf16[4,4,88,512]{3,2,1,0:T(8,128)(2,1)S(1)}, u32[]{:S(2)}, u32[]{:S(2)}) collective-permute-start(bf16[4,4,88,512]{3,2,1,0:T(8,128)(2,1)S(1)} %all_to_all.20.own_ref), channel_id=1, source_target_pairs={{0,16},{16,0},{1,17},{17,1},{2,18},{18,2},{3,19},{19,3},{4,20},{20... | collective-permute-start | bytes 4325384 | tf_op jit(solution)/shard_map/ppermute | solution.py:428
  60.9 20.3 %collective-permute-start = (bf16[3,224,256]{2,1,0:T(8,128)(2,1)}, bf16[3,224,256]{2,1,0:T(8,128)(2,1)S(1)}, u32[]{:S(2)}, u32[]{:S(2)}) collective-permute-start(bf16[3,224,256]{2,1,0:T(8,128)(2,1)} %get-tuple-element.41), channel_id=1, source_target_pairs={{0,1},{1,2},{2,3},{3,0},{4,5},{5,6},{6,7},{7,4},{8,9},{9,10},{10,1... | collective-permute-start | bytes 1032200 | tf_op jit(solution)/shard_map/ppermute | solution.py:392
  62.8 31.1 %collective-permute-start.1 = (bf16[3,224,256]{2,1,0:T(8,128)(2,1)}, bf16[3,224,256]{2,1,0:T(8,128)(2,1)}, u32[]{:S(2)}, u32[]{:S(2)}) collective-permute-start(bf16[3,224,256]{2,1,0:T(8,128)(2,1)} %get-tuple-element.42), channel_id=1, source_target_pairs={{0,2},{1,3},{2,0},{3,1},{4,6},{5,7},{6,4},{7,5},{8,10},{9,11},{10,... | collective-permute-start | bytes 1032200 | tf_op jit(solution)/shard_map/ppermute | solution.py:392
  66.5 32.3 %collective-permute-start.2 = (bf16[3,224,256]{2,1,0:T(8,128)(2,1)}, bf16[3,224,256]{2,1,0:T(8,128)(2,1)}, u32[]{:S(2)}, u32[]{:S(2)}) collective-permute-start(bf16[3,224,256]{2,1,0:T(8,128)(2,1)} %get-tuple-element.43), channel_id=1, source_target_pairs={{0,3},{1,0},{2,1},{3,2},{4,7},{5,4},{6,5},{7,6},{8,11},{9,8},{10,9... | collective-permute-start | bytes 1032200 | tf_op jit(solution)/shard_map/ppermute | solution.py:392
  69.5 29.2 %collective-permute-start.6 = (f32[8,256]{1,0:T(8,128)S(1)}, f32[8,256]{1,0:T(8,128)S(1)}, u32[]{:S(2)}, u32[]{:S(2)}) collective-permute-start(f32[8,256]{1,0:T(8,128)S(1)} %copy-done.19), channel_id=1, source_target_pairs={{0,12},{4,0},{8,4},{12,8},{1,13},{5,1},{9,5},{13,9},{2,14},{6,2},{... | collective-permute-start | bytes 24584 | tf_op jit(solution)/shard_map/ppermute | solution.py:392
  81.2 21.1 %copy-start.2 = (bf16[3,224,256]{2,1,0:T(8,128)(2,1)}, bf16[3,224,256]{2,1,0:T(8,128)(2,1)S(1)}, u32[]{:S(2)}) copy-start(bf16[3,224,256]{2,1,0:T(8,128)(2,1)S(1)} %collective-permute-done.w1_ref) | copy-start | bytes 1032196
  81.2 17.6 %collective-permute-start.5 = (f32[8,256]{1,0:T(8,128)S(1)}, f32[8,256]{1,0:T(8,128)S(1)}, u32[]{:S(2)}, u32[]{:S(2)}) collective-permute-start(f32[8,256]{1,0:T(8,128)S(1)} %copy-done.19), channel_id=1, source_target_pairs={{0,8},{4,12},{8,0},{12,4},{1,9},{5,13},{9,1},{13,5},{2,10},{6,14},... | collective-permute-start | bytes 24584 | tf_op jit(solution)/shard_map/ppermute | solution.py:392
  93.9 8.3 %collective-permute-start.4 = (f32[8,256]{1,0:T(8,128)S(1)}, f32[8,256]{1,0:T(8,128)S(1)}, u32[]{:S(2)}, u32[]{:S(2)}) collective-permute-start(f32[8,256]{1,0:T(8,128)S(1)} %copy-done.19), channel_id=1, source_target_pairs={{0,4},{4,8},{8,12},{12,0},{1,5},{5,9},{9,13},{13,1},{2,6},{6,10},{... | collective-permute-start | bytes 24584 | tf_op jit(solution)/shard_map/ppermute | solution.py:392
  98.8 3.5 %copy-start.20 = (f32[8,256]{1,0:T(8,128)}, f32[8,256]{1,0:T(8,128)S(1)}, u32[]{:S(2)}) copy-start(f32[8,256]{1,0:T(8,128)S(1)} %collective-permute-done.6.moment3_ref) | copy-start | bytes 24580
  108.3 21.2 %collective-permute-start.7 = (bf16[88,640]{1,0:T(8,128)(2,1)}, bf16[88,640]{1,0:T(8,128)(2,1)S(1)}, u32[]{:S(2)}, u32[]{:S(2)}) collective-permute-start(bf16[88,640]{1,0:T(8,128)(2,1)} %get-tuple-element.48), channel_id=1, source_target_pairs={{0,4},{4,8},{8,12},{12,0},{1,5},{5,9},{9,13},{13,1},{2,6},{6,10},{... | collective-permute-start | bytes 337928 | tf_op jit(solution)/shard_map/ppermute | solution.py:392
  112.3 17.1 %collective-permute-start.8 = (bf16[80,640]{1,0:T(8,128)(2,1)}, bf16[80,640]{1,0:T(8,128)(2,1)S(1)}, u32[]{:S(2)}, u32[]{:S(2)}) collective-permute-start(bf16[80,640]{1,0:T(8,128)(2,1)} %get-tuple-element.50), channel_id=1, source_target_pairs={{0,12},{4,0},{8,4},{12,8},{1,13},{5,1},{9,5},{13,9},{2,14},{6,2},{... | collective-permute-start | bytes 307208 | tf_op jit(solution)/shard_map/ppermute | solution.py:392
  117.5 32.4 %collective-permute-start.11 = (bf16[88,640]{1,0:T(8,128)(2,1)}, bf16[88,640]{1,0:T(8,128)(2,1)S(1)}, u32[]{:S(2)}, u32[]{:S(2)}) collective-permute-start(bf16[88,640]{1,0:T(8,128)(2,1)} %get-tuple-element.53), channel_id=1, source_target_pairs={{0,12},{4,0},{8,4},{12,8},{1,13},{5,1},{9,5},{13,9},{2,14},{6,2},{... | collective-permute-start | bytes 337928 | tf_op jit(solution)/shard_map/ppermute | solution.py:392
  131.9 20.6 %collective-permute-start.9 = (bf16[88,640]{1,0:T(8,128)(2,1)}, bf16[88,640]{1,0:T(8,128)(2,1)S(1)}, u32[]{:S(2)}, u32[]{:S(2)}) collective-permute-start(bf16[88,640]{1,0:T(8,128)(2,1)} %get-tuple-element.51), channel_id=1, source_target_pairs={{0,4},{4,8},{8,12},{12,0},{1,5},{5,9},{9,13},{13,1},{2,6},{6,10},{... | collective-permute-start | bytes 337928 | tf_op jit(solution)/shard_map/ppermute | solution.py:392
  135.8 14.1 %collective-permute-start.10 = (bf16[80,640]{1,0:T(8,128)(2,1)}, bf16[80,640]{1,0:T(8,128)(2,1)S(1)}, u32[]{:S(2)}, u32[]{:S(2)}) collective-permute-start(bf16[80,640]{1,0:T(8,128)(2,1)} %get-tuple-element.52), channel_id=1, source_target_pairs={{0,4},{4,8},{8,12},{12,0},{1,5},{5,9},{9,13},{13,1},{2,6},{6,10},{... | collective-permute-start | bytes 307208 | tf_op jit(solution)/shard_map/ppermute | solution.py:392
  140.3 12.2 %collective-permute-start.12 = (bf16[80,640]{1,0:T(8,128)(2,1)}, bf16[80,640]{1,0:T(8,128)(2,1)S(1)}, u32[]{:S(2)}, u32[]{:S(2)}) collective-permute-start(bf16[80,640]{1,0:T(8,128)(2,1)} %get-tuple-element.54), channel_id=1, source_target_pairs={{0,12},{4,0},{8,4},{12,8},{1,13},{5,1},{9,5},{13,9},{2,14},{6,2},{... | collective-permute-start | bytes 307208 | tf_op jit(solution)/shard_map/ppermute | solution.py:392
  190.8 10.1 %collective-permute-start.13 = (bf16[4,4,80,256]{3,2,1,0:T(8,128)(2,1)}, bf16[4,4,80,256]{3,2,1,0:T(8,128)(2,1)S(1)}, u32[]{:S(2)}, u32[]{:S(2)}) collective-permute-start(bf16[4,4,80,256]{3,2,1,0:T(8,128)(2,1)} %get-tuple-element.58), channel_id=1, source_target_pairs={{0,16},{16,0},{1,17},{17,1},{2,18},{18,2},{3,19},{19,3},{4,20},{20... | collective-permute-start | bytes 1966088 | tf_op jit(solution)/shard_map/ppermute | solution.py:455
  197.5 3.3 %collective-permute-start.14 = (f32[4,8,256]{2,1,0:T(8,128)}, f32[4,8,256]{2,1,0:T(8,128)S(1)}, u32[]{:S(2)}, u32[]{:S(2)}) collective-permute-start(f32[4,8,256]{2,1,0:T(8,128)} %get-tuple-element.60.sums_ref), channel_id=1, source_target_pairs={{0,16},{16,0},{1,17},{17,1},{2,18},{18,2},{3,19},{19,3},{4,20},{20... | collective-permute-start | bytes 98312 | tf_op jit(solution)/shard_map/ppermute | solution.py:459
  204.2 15.0 %all-to-all-start.2 = ((bf16[4,4,88,256]{3,2,1,0:T(8,128)(2,1)}), bf16[4,4,88,256]{3,2,1,0:T(8,128)(2,1)S(1)}, u32[]{:S(2)}, u32[]{:S(2)}) async-start(bf16[4,4,88,256]{3,2,1,0:T(8,128)(2,1)} %shard_map.143), calls=%async_computation.2 | async-start | bytes 1441792 | tf_op jit(solution)/shard_map/all_to_all | solution.py:387
  212.5 13.8 %copy-start.25 = (bf16[3,224,256]{2,1,0:T(8,128)(2,1)S(1)}, bf16[3,224,256]{2,1,0:T(8,128)(2,1)}, u32[]{:S(2)}) copy-start(bf16[3,224,256]{2,1,0:T(8,128)(2,1)} %get-tuple-element.64) | copy-start | bytes 1032196
  212.5 18.3 %copy-start.24 = (bf16[3,224,256]{2,1,0:T(8,128)(2,1)S(1)}, bf16[3,224,256]{2,1,0:T(8,128)(2,1)}, u32[]{:S(2)}) copy-start(bf16[3,224,256]{2,1,0:T(8,128)(2,1)} %get-tuple-element.65) | copy-start | bytes 1032196
  212.5 20.8 %copy-start.23 = (bf16[3,224,256]{2,1,0:T(8,128)(2,1)S(1)}, bf16[3,224,256]{2,1,0:T(8,128)(2,1)}, u32[]{:S(2)}) copy-start(bf16[3,224,256]{2,1,0:T(8,128)(2,1)} %get-tuple-element.66) | copy-start | bytes 1032196
  222.0 33.7 %all-to-all-start.3 = ((bf16[16,32,256]{2,1,0:T(8,128)(2,1)}), bf16[16,32,256]{2,1,0:T(8,128)(2,1)S(1)}, u32[]{:S(2)}, u32[]{:S(2)}) async-start(bf16[16,32,256]{2,1,0:T(8,128)(2,1)} %bitcast.23), calls=%async_computation.3 | async-start | bytes 524288 | tf_op jit(solution)/shard_map/all_to_all | solution.py:387
  226.3 13.3 %collective-permute-start.15 = (bf16[3,224,256]{2,1,0:T(8,128)(2,1)S(1)}, bf16[3,224,256]{2,1,0:T(8,128)(2,1)S(1)}, u32[]{:S(2)}, u32[]{:S(2)}) collective-permute-start(bf16[3,224,256]{2,1,0:T(8,128)(2,1)S(1)} %copy-done.25), channel_id=1, source_target_pairs={{0,3},{1,0},{2,1},{3,2},{4,7},{5,4},{6,5},{7,6},{8,11},{9,8},{10,9... | collective-permute-start | bytes 1032200 | tf_op jit(solution)/shard_map/ppermute | solution.py:392
  230.8 11.9 %collective-permute-start.16 = (bf16[3,224,256]{2,1,0:T(8,128)(2,1)S(1)}, bf16[3,224,256]{2,1,0:T(8,128)(2,1)S(1)}, u32[]{:S(2)}, u32[]{:S(2)}) collective-permute-start(bf16[3,224,256]{2,1,0:T(8,128)(2,1)S(1)} %copy-done.24), channel_id=1, source_target_pairs={{0,2},{1,3},{2,0},{3,1},{4,6},{5,7},{6,4},{7,5},{8,10},{9,11},{10,... | collective-permute-start | bytes 1032200 | tf_op jit(solution)/shard_map/ppermute | solution.py:392
  233.3 18.6 %collective-permute-start.17 = (bf16[3,224,256]{2,1,0:T(8,128)(2,1)S(1)}, bf16[3,224,256]{2,1,0:T(8,128)(2,1)S(1)}, u32[]{:S(2)}, u32[]{:S(2)}) collective-permute-start(bf16[3,224,256]{2,1,0:T(8,128)(2,1)S(1)} %copy-done.23), channel_id=1, source_target_pairs={{0,1},{1,2},{2,3},{3,0},{4,5},{5,6},{6,7},{7,4},{8,9},{9,10},{10,1... | collective-permute-start | bytes 1032200 | tf_op jit(solution)/shard_map/ppermute | solution.py:392
  239.6 12.3 %copy-start.5 = (bf16[3,224,256]{2,1,0:T(8,128)(2,1)}, bf16[3,224,256]{2,1,0:T(8,128)(2,1)S(1)}, u32[]{:S(2)}) copy-start(bf16[3,224,256]{2,1,0:T(8,128)(2,1)S(1)} %collective-permute-done.15.g1_ref) | copy-start | bytes 1032196
  242.7 9.2 %copy-start.6 = (bf16[3,224,256]{2,1,0:T(8,128)(2,1)}, bf16[3,224,256]{2,1,0:T(8,128)(2,1)S(1)}, u32[]{:S(2)}) copy-start(bf16[3,224,256]{2,1,0:T(8,128)(2,1)S(1)} %collective-permute-done.16.g2_ref) | copy-start | bytes 1032196
  (15 other events, 17.7 us)

commit v3 on v2

--- a/solution.py
+++ b/solution.py
@@ -25,10 +25,6 @@
     return lax.dot_general(a, b, (((1,), (1,)), ((), ())), preferred_element_type=f32)
 
 
-def tn(a, b):
-    return lax.dot_general(a, b, (((0,), (0,)), ((), ())), preferred_element_type=f32)
-
-
 def pieces(x):
     high = x.astype(bf16)
     rest = x - high.astype(f32)
@@ -60,9 +56,25 @@
     return jnp.sum(jnp.where(same, col, 0.0), axis=0, keepdims=True)
 
 
-def pack_tokens(tokens_ref, cotangent_ref, gate_ref, up_ref, down_ref, gain_ref, out_ref):
+def fetched(pairs, sems):
+    copies = [pltpu.make_async_copy(a, b, sems.at[i]) for i, (a, b) in enumerate(pairs)]
+    for c in copies:
+        c.start()
+    return copies
+
+
+def pack_tokens(
+    down_hbm, gain_hbm, tokens_hbm, cotangent_hbm, gate_hbm, up_hbm, out_ref,
+    down_ref, gain_ref, tokens_ref, cotangent_ref, gate_ref, up_ref, sems,
+):
+    copies = fetched(
+        (
+            (down_hbm, down_ref), (gain_hbm, gain_ref), (tokens_hbm, tokens_ref), (cotangent_hbm, cotangent_ref),
+            (gate_hbm, gate_ref), (up_hbm, up_ref),
+        ),
+        sems,
+    )
     rows, width = tokens_ref.shape
-    scaled = (branch_scale * cotangent_ref[...].astype(f32)).astype(bf16)
 
     def moments(ref):
         w = ref[...].astype(f32)
@@ -73,11 +85,18 @@
     def single(x):
         return [p.astype(f32) for p in pieces(x)]
 
+    copies[0].wait()
     mean, square = moments(down_ref)
+    for c in copies[1:4]:
+        c.wait()
+    scaled = (branch_scale * cotangent_ref[...].astype(f32)).astype(bf16)
     gain = single(gain_ref[...])
     left = jnp.concatenate([tokens_ref[...].astype(f32), *single(mean), gain[0]], axis=0).astype(bf16)
     right = jnp.concatenate([scaled.astype(f32), *single(square), gain[1]], axis=0).astype(bf16)
-    wide = [moments(ref) for ref in (gate_ref, up_ref)]
+    wide = []
+    for c, ref in zip(copies[4:], (gate_ref, up_ref)):
+        c.wait()
+        wide.append(moments(ref))
     blocks, lines = out_ref.shape[0], out_ref.shape[1]
     share = gate_ref.shape[1] // blocks
     for j in range(blocks):
@@ -95,13 +114,16 @@
             out_ref[j, l, rows + 4 : rows + 12, width : 2 * width] = sides[1]
 
 
-def pack_weights(place_ref, gate_ref, up_ref, down_ref, *refs):
-    *outs, store_ref = refs
+def pack_weights(place_ref, gate_hbm, up_hbm, down_hbm, *refs):
+    *outs, store_ref, gate_ref, up_ref, down_ref, sems = refs
+    copies = fetched(((gate_hbm, gate_ref), (up_hbm, up_ref), (down_hbm, down_ref)), sems)
     blocks, _, share, _ = store_ref.shape
     for at, ref in enumerate((gate_ref, up_ref)):
+        copies[at].wait()
         turned = ref[...].astype(f32).T.astype(bf16)
         for j in range(blocks):
             store_ref[j, at] = turned[j * share : (j + 1) * share]
+    copies[2].wait()
     for j in range(blocks):
         store_ref[j, 2] = down_ref[j * share : (j + 1) * share]
     for k in range(blocks):
@@ -150,8 +172,8 @@
 
 def forward(
     wide_count, tall_count, place_ref, w0_ref, w1_ref, w2_ref, w3_ref, own_ref, other_ref,
-    moment0_ref, moment1_ref, moment2_ref, moment3_ref, gain_ref,
-    kept_ref, near_a_ref, near_b_ref, back_a_ref, back_b_ref, far_a_ref, far_b_ref,
+    moment0_ref, moment1_ref, moment2_ref, moment3_ref, gate_gain_ref, up_gain_ref,
+    kept_ref, first_ref, second_ref, third_ref,
     cols_ref, rows_ref, row_ref, store_ref,
 ):
     w_ref = (w0_ref, w1_ref, w2_ref, w3_ref)
@@ -175,8 +197,13 @@
         mean, square = merged(moments, wide_count)
         mean = upright(mean, share)
         scale = upright(lax.rsqrt(square + epsilon), share)
-        gs = gain_ref[:, at : at + 1] * scale
-        for k, v in ((3 * at, mean), (3 * at + 1, gs), (3 * at + 2, scale)):
+        row_of = (gate_gain_ref, up_gain_ref)[at]
+        gain = sum(
+            jnp.where(place_ref[1] == j, row_of[:, j * share : (j + 1) * share], 0.0) for j in range(blocks)
+        )
+        gain = upright(gain, share)
+        gs = gain * scale
+        for k, v in ((3 * at, mean), (3 * at + 1, gs), (3 * at + 2, scale), (6 + at, gain)):
             cols = jnp.where(lane == k, v, cols)
         total = 0.0
         for j in range(blocks):
@@ -201,26 +228,18 @@
     total = total.astype(bf16)
     for q in range(parts):
         store_ref[q, 2 * tall : 3 * tall, :] = total[q * tall : (q + 1) * tall]
-    at = place_ref[0]
-    cut = near_a_ref.shape[0]
-    kept_ref[...] = store_ref[at]
-    for k, a_ref, b_ref in ((1, near_a_ref, near_b_ref), (2, far_a_ref, far_b_ref), (3, back_a_ref, back_b_ref)):
-        q = lax.rem(at + k, parts)
-        a_ref[...] = store_ref[q, 0:cut, :]
-        b_ref[...] = store_ref[q, cut:, :]
-
-
-def add_pair(a_ref, b_ref, c_ref, d_ref, left_ref, right_ref):
-    left_ref[...] = (a_ref[...].astype(f32) + b_ref[...].astype(f32)).astype(bf16)
-    right_ref[...] = (c_ref[...].astype(f32) + d_ref[...].astype(f32)).astype(bf16)
-
-
-def gating(kept_ref, near_a_ref, near_b_ref, back_a_ref, back_b_ref, row_ref, d_ref):
+    at, core = place_ref[0], place_ref[4]
+    for ref, k in ((kept_ref, 0), (first_ref, 2), (second_ref, 3 - 2 * core), (third_ref, 1 + 2 * core)):
+        ref[...] = store_ref[lax.rem(at + k, parts)]
+
+
+def add_pair(a_ref, b_ref, out_ref):
+    out_ref[...] = (a_ref[...].astype(f32) + b_ref[...].astype(f32)).astype(bf16)
+
+
+def gating(kept_ref, second_ref, third_ref, row_ref, d_ref):
     tall = (d_ref.shape[0] - 8) // 3
-    cut = near_a_ref.shape[0]
-    top = kept_ref[0:cut, :].astype(f32) + near_a_ref[...].astype(f32) + back_a_ref[...].astype(f32)
-    low = kept_ref[cut:, :].astype(f32) + near_b_ref[...].astype(f32) + back_b_ref[...].astype(f32)
-    total = jnp.concatenate([top, low], axis=0)
+    total = kept_ref[...].astype(f32) + second_ref[...].astype(f32) + third_ref[...].astype(f32)
     gate, up, dhidden = total[0:tall], total[tall : 2 * tall], total[2 * tall : 3 * tall]
     sig = 1.0 / (1.0 + jnp.exp(-gate))
     act = gate * sig
@@ -246,45 +265,17 @@
     )
 
 
-def token_back(d_ref, w0_ref, w1_ref, w2_ref, w3_ref, cols_ref, mine_ref, theirs_ref):
+def weight_grads(
+    width_all, d_ref, w0_ref, w1_ref, w2_ref, w3_ref, own_ref, other_ref, cols_ref,
+    g0_ref, g1_ref, g2_ref, g3_ref, dots_ref,
+):
     w_ref = (w0_ref, w1_ref, w2_ref, w3_ref)
     blocks = len(w_ref)
-    _, share, width = w0_ref.shape
-    tall = share // d_ref.shape[0]
-    streams = [stacked(d_ref, at, tall) for at in range(2)]
-    lines, _, rows, _ = mine_ref.shape
-    half = lines * rows
-    for j in range(blocks):
-        back = 0.0
-        for at in range(2):
-            cent = w_ref[j][at].astype(f32) - cols_ref[:, 3 * at : 3 * at + 1]
-            back = back + tn(streams[at], (cent * cols_ref[:, 3 * at + 1 : 3 * at + 2]).astype(bf16))
-        mine_ref[:, j] = back[:half].reshape(lines, rows, width)
-        theirs_ref[:, j] = back[half:].astype(bf16).reshape(lines, rows, width)
-
-
-def tall_grads(d_ref, w0_ref, w1_ref, w2_ref, w3_ref, own_ref, other_ref, rows_ref, grad_ref, sums_ref):
-    w_ref = (w0_ref, w1_ref, w2_ref, w3_ref)
-    blocks = len(w_ref)
-    _, share, width = w0_ref.shape
-    stream = stacked(d_ref, 2, share // d_ref.shape[0])
-    for j in range(blocks):
-        p = nn(stream, whole(own_ref, other_ref, j, 1))
-        cent = w_ref[j][2].astype(f32) - rows_ref[j, 0:1, :]
-        summed = jnp.sum(p, axis=0, keepdims=True)
-        crossed = jnp.sum(p * cent, axis=0, keepdims=True)
-        sums_ref[j] = jnp.concatenate([summed, crossed, jnp.zeros((6, width), f32)], axis=0)
-        grad_ref[j] = p.astype(bf16)
-
-
-def wide_grads(width_all, d_ref, w0_ref, w1_ref, w2_ref, w3_ref, own_ref, other_ref, cols_ref, down_ref, g0_ref, g1_ref, g2_ref, g3_ref, dots_ref):
-    w_ref = (w0_ref, w1_ref, w2_ref, w3_ref)
+    _, share, _ = w0_ref.shape
     grad_ref = (g0_ref, g1_ref, g2_ref, g3_ref)
-    blocks = len(w_ref)
-    _, share, _ = w0_ref.shape
     parts = d_ref.shape[0]
     tall = share // parts
-    streams = [stacked(d_ref, at, tall) for at in range(2)]
+    streams = [stacked(d_ref, at, tall) for at in range(3)]
     extra = [d_ref[q, 3 * tall : 3 * tall + 8, :].astype(f32) for q in range(parts)]
     row = sum(joined(e[3:6]) for e in extra)
     dots_ref[...] = jnp.zeros(dots_ref.shape, f32)
@@ -294,7 +285,7 @@
         dot = jnp.concatenate(
             [upright(joined(e[0:3, 128 * at : 128 * (at + 1)]), tall) for e in extra], axis=0
         )
-        dots_ref[at : at + 1, :] = level(dot, dots_ref.shape[1])
+        dots_ref[at : at + 1, :] = level(dot / cols_ref[:, 6 + at : 7 + at], dots_ref.shape[1])
         s = cols_ref[:, 3 * at + 2 : 3 * at + 3]
         pulls.append(s * s * dot)
     for j in range(blocks):
@@ -304,34 +295,68 @@
             cent = w_ref[j][at].astype(f32) - cols_ref[:, 3 * at : 3 * at + 1]
             grad = cols_ref[:, 3 * at + 1 : 3 * at + 2] * (p - means[at]) - cent * pulls[at]
             grad_ref[j][at] = grad.astype(bf16)
-        grad_ref[j][2] = down_ref[j]
-
-
-def both_cores(mine_ref, theirs_ref, sums_ref, other_ref, out_ref):
-    lines, blocks, rows, _ = mine_ref.shape
-    for j in range(blocks):
-        total = sums_ref[j] + other_ref[j]
-        extra = [p.astype(f32) for k in range(2) for p in pieces(total[k : k + 1, :])]
-        extra = jnp.concatenate([*extra, total[2:4, :]], axis=0).astype(bf16)
-        for y in range(lines):
-            out_ref[y, j, 0:rows, :] = (mine_ref[y, j] + theirs_ref[y, j].astype(f32)).astype(bf16)
-            out_ref[y, j, rows : rows + 8, :] = extra
+        grad_ref[j][2] = nn(streams[2], whole(own_ref, other_ref, j, 1)).astype(bf16)
+
+
+def spread(sums):
+    return [p.astype(f32) for k in range(2) for p in pieces(sums[k : k + 1, :])]
+
+
+def token_back(
+    d_ref, w0_ref, w1_ref, w2_ref, w3_ref, own_ref, other_ref, cols_ref, rows_ref, mine_ref, theirs_ref, sums_ref
+):
+    w_ref = (w0_ref, w1_ref, w2_ref, w3_ref)
+    blocks = len(w_ref)
+    _, share, width = w0_ref.shape
+    tall = share // d_ref.shape[0]
+    streams = [stacked(d_ref, at, tall).T for at in range(2)]
+    hidden = stacked(d_ref, 2, tall)
+    half = mine_ref.shape[1]
+    for j in range(blocks):
+        back = 0.0
+        for at in range(2):
+            cent = w_ref[j][at].astype(f32) - cols_ref[:, 3 * at : 3 * at + 1]
+            back = back + nn(streams[at], (cent * cols_ref[:, 3 * at + 1 : 3 * at + 2]).astype(bf16))
+        mine_ref[j] = back[:half]
+        p = nn(hidden, whole(own_ref, other_ref, j, 1))
+        cent = w_ref[j][2].astype(f32) - rows_ref[j, 0:1, :]
+        summed = jnp.sum(p, axis=0, keepdims=True)
+        crossed = jnp.sum(p * cent, axis=0, keepdims=True)
+        zero = jnp.zeros((6, width), f32)
+        sums = jnp.concatenate([summed, crossed, zero], axis=0)
+        sums_ref[j] = sums
+        sums = jnp.concatenate([*spread(sums), zero[0:2]], axis=0)
+        theirs_ref[j] = jnp.concatenate([back[half:], sums], axis=0).astype(bf16)
+
+
+def both_cores(mine_ref, theirs_ref, sums_ref, out_ref):
+    blocks, half, _ = mine_ref.shape
+    lines = out_ref.shape[0]
+    rows = half // lines
+    for j in range(blocks):
+        other = theirs_ref[j, half : half + 8, :].astype(f32)
+        total = sums_ref[j, 0:2, :] + jnp.concatenate([joined(other[0:3]), joined(other[3:6])], axis=0)
+        extra = jnp.concatenate([*spread(total), other[6:8]], axis=0).astype(bf16)
+        for k in range(lines):
+            at = slice(k * rows, (k + 1) * rows)
+            out_ref[k, j, 0:rows, :] = (mine_ref[j, at, :] + theirs_ref[j, at, :].astype(f32)).astype(bf16)
+            out_ref[k, j, rows : rows + 8, :] = extra
 
 
 def whole_column(place_ref, in_ref, dots_ref, out_ref):
     lines, blocks, high, _ = in_ref.shape
-    dots = [p.astype(f32) for k in range(2) for p in pieces(dots_ref[k : k + 1, :])]
+    dots = spread(dots_ref[...])
     cuts = out_ref.shape[0]
     rows = (high - 8) // cuts
     for j in range(blocks):
         lots = [in_ref[y, j].astype(f32) for y in range(lines)]
         back = sum(lot[0 : high - 8] for lot in lots)
-        extra = []
-        for k in range(2):
-            total = sum(joined(lot[high - 8 + 3 * k : high - 5 + 3 * k]) for lot in lots)
-            extra += [p.astype(f32) for p in pieces(total)]
+        total = [sum(joined(lot[high - 8 + 3 * k : high - 5 + 3 * k]) for lot in lots) for k in range(2)]
+        extra = spread(jnp.concatenate(total, axis=0))
         for l in range(cuts):
-            out_ref[l, lax.rem(place_ref[1] + blocks - j, blocks)] = jnp.concatenate([back[l * rows : (l + 1) * rows], *extra, *dots], axis=0).astype(bf16)
+            out_ref[l, lax.rem(place_ref[1] + blocks - j, blocks)] = jnp.concatenate(
+                [back[l * rows : (l + 1) * rows], *extra, *dots], axis=0
+            ).astype(bf16)
 
 
 def finish_wide(place_ref, g0_ref, g1_ref, g2_ref, g3_ref, gate_ref, up_ref, store_ref):
@@ -370,8 +395,8 @@
         ) * cent
 
 
-def call(body, outs, *args, place=None, scratch=()):
-    specs = [pl.BlockSpec(memory_space=pltpu.VMEM)] * len(args)
+def call(body, outs, *args, place=None, scratch=(), far=0, grant=20):
+    specs = [pl.BlockSpec(memory_space=pltpu.HBM if i < far else pltpu.VMEM) for i in range(len(args))]
     if place is not None:
         args = (place, *args)
         specs = [pl.BlockSpec(memory_space=pltpu.SMEM), *specs]
@@ -380,6 +405,7 @@
         out_shape=[jax.ShapeDtypeStruct(s, t) for s, t in outs],
         in_specs=specs,
         scratch_shapes=scratch,
+        compiler_params=pltpu.CompilerParams(vmem_limit_bytes=grant << 20),
     )(*args)
 
 
@@ -390,6 +416,14 @@
 def shift(x, axis, by):
     size = lax.axis_size(axis)
     return lax.ppermute(x, axis, [(i, (i + by) % size) for i in range(size)])
+
+
+def apart(x, axis, by):
+    size = lax.axis_size(axis)
+    pairs = [
+        (core * size + i, core * size + (i + (by if core == 0 else -by)) % size) for core in (0, 1) for i in range(size)
+    ]
+    return lax.ppermute(x, ("core", axis), pairs)
 
 
 def block(tokens, cotangent, gate_weight, up_weight, down_weight, gate_gain, up_gain, down_gain):
@@ -402,7 +436,9 @@
     share = hidden // nx
     tall = share // nz
     count = rows * ny * nl * nc
-    place = jnp.stack([lax.axis_index("zh"), lax.axis_index("x"), lax.axis_index("zl")]).astype(jnp.int32)
+    place = jnp.stack(
+        [lax.axis_index("zh"), lax.axis_index("x"), lax.axis_index("zl"), lax.axis_index("y"), lax.axis_index("core")]
+    ).astype(jnp.int32)
     swap = [(0, 1), (1, 0)]
 
     def grid_exchange(x, axes):
@@ -411,14 +447,29 @@
 
     (both,) = call(
         pack_tokens, [((nx, nl, rows + 12, 2 * width), bf16)],
-        tokens, cotangent, gate_weight, up_weight, down_weight, down_gain.reshape(1, width),
+        down_weight, down_gain.reshape(1, width), tokens, cotangent, gate_weight, up_weight,
+        far=6,
+        grant=60,
+        scratch=[
+            pltpu.VMEM((hidden, width), bf16), pltpu.VMEM((1, width), f32),
+            pltpu.VMEM((rows, width), bf16), pltpu.VMEM((rows, width), bf16),
+            pltpu.VMEM((width, hidden), bf16), pltpu.VMEM((width, hidden), bf16), pltpu.SemaphoreType.DMA((6,)),
+        ],
     )
     both = grid_exchange(both, ("x", "zl"))
     cut_weights = call(
         pack_weights, [((3, share, width), bf16)] * nx, gate_weight, up_weight, down_weight,
-        place=place, scratch=[pltpu.VMEM((nx, 3, share, width), bf16)],
-    )
-    weights = [cut_weights[0], *(shift(cut_weights[k], "x", k) for k in (1, 2, 3))]
+        place=place,
+        far=3,
+        scratch=[
+            pltpu.VMEM((nx, 3, share, width), bf16),
+            pltpu.VMEM((width, hidden), bf16), pltpu.VMEM((width, hidden), bf16), pltpu.VMEM((hidden, width), bf16),
+            pltpu.SemaphoreType.DMA((3,)),
+        ],
+    )
+    weights = [cut_weights[0]]
+    for k in (1, 2, 3):
+        weights.append(shift(cut_weights[k], "x", k))
     both, moments = call(
         functools.partial(repack_tokens, width, hidden),
         [((ny, nx, nl * rows + 8, 2 * width), bf16), ((8, width), f32)], both, place=place,
@@ -426,54 +477,45 @@
     own = exchange(both, "y")
     moments = [moments, *(shift(moments, "zh", k) for k in (1, 2, 3))]
     other = lax.ppermute(own, "core", swap)
-    gains = jnp.stack([gate_gain.reshape(nx, share)[place[1]], up_gain.reshape(nx, share)[place[1]]], axis=1)
-
-    cut = 88
-    a, b = ((cut, count), bf16), ((3 * tall - cut, count), bf16)
-    kept, near_a, near_b, back_a, back_b, far_a, far_b, cols, rows_of, row = call(
+    piece = ((3 * tall, count), bf16)
+    kept, first, second, third, cols, rows_of, row = call(
         functools.partial(forward, width * nx, hidden * nl),
-        [
-            ((3 * tall, count), bf16), a, b, a, b, a, b,
-            ((share, 128), f32), ((nx, 8, width), f32), ((8, count), f32),
-        ],
-        *weights, own, other, *moments, gains,
+        [piece, piece, piece, piece, ((share, 128), f32), ((nx, 8, width), f32), ((8, count), f32)],
+        *weights, own, other, *moments, gate_gain.reshape(1, hidden), up_gain.reshape(1, hidden),
         place=place,
         scratch=[pltpu.VMEM((nz, 3 * tall, count), bf16)],
     )
-    far_a = shift(far_a, "zh", 1)
-    far_b = shift(far_b, "zh", -1)
-    near_b = shift(near_b, "zh", 1)
-    back_a = shift(back_a, "zh", -1)
-    near_a, back_b = call(add_pair, [a, b], near_a, far_a, back_b, far_b)
-    near_a = shift(near_a, "zh", 1)
-    back_b = shift(back_b, "zh", -1)
-    (d,) = call(gating, [((3 * tall + 8, count), bf16)], kept, near_a, near_b, back_a, back_b, row)
+    first = apart(first, "zh", 1)
+    second = apart(second, "zh", -1)
+    (third,) = call(add_pair, [piece], third, first)
+    third = apart(third, "zh", 1)
+    (d,) = call(gating, [((3 * tall + 8, count), bf16)], kept, second, third, row)
     d = lax.all_gather(d, "zh")
 
-    shape = (ny, nx, nl * rows, width)
-    mine, theirs = call(token_back, [(shape, f32), (shape, bf16)], d, *weights, cols)
+    half = count // nc
+    mine, theirs, sums = call(
+        token_back, [((nx, half, width), f32), ((nx, half + 8, width), bf16), ((nx, 8, width), f32)],
+        d, *weights, own, other, cols, rows_of,
+    )
     theirs = lax.ppermute(theirs, "core", swap)
-    down_grads, sums = call(
-        tall_grads, [((nx, share, width), bf16), ((nx, 8, width), f32)], d, *weights, own, other, rows_of
-    )
-    other_sums = lax.ppermute(sums, "core", swap)
-    (back,) = call(both_cores, [((ny, nx, nl * rows + 8, width), bf16)], mine, theirs, sums, other_sums)
+    *grads, dots = call(
+        functools.partial(weight_grads, width_all), [((3, share, width), bf16)] * nx + [((8, width), f32)],
+        d, *weights, own, other, cols,
+    )
+    (back,) = call(both_cores, [((ny, nx, nl * rows + 8, width), bf16)], mine, theirs, sums)
     back = exchange(back, "y")
-    *grads, dots = call(
-        functools.partial(wide_grads, width_all), [((3, share, width), bf16)] * nx + [((8, width), f32)],
-        d, *weights, own, other, cols, down_grads,
-    )
-    grads = [grads[0], *(shift(grads[k], "x", -k) for k in (1, 2, 3))]
+    sent = [grads[0], None, None, None]
+    for k in (2, 1, 3):
+        sent[k] = shift(grads[k], "x", -k)
     (back,) = call(whole_column, [((nl, nx, rows + 12, width), bf16)], back, dots, place=place)
     back = grid_exchange(back, ("zl", "x"))
-    grad_gate, grad_up = call(
-        finish_wide, [((width, hidden), f32), ((width, hidden), f32)], *grads,
+    grad_gate, grad_up = call(finish_wide, [((width, hidden), f32), ((width, hidden), f32)], *sent,
         place=place, scratch=[pltpu.VMEM((nx, share, width), f32)],
     )
     grad_tokens, grad_down, down_dgain, dots = call(
         functools.partial(finish_tall, hidden_all),
         [((rows, width), f32), ((nx, share, width), f32), ((1, width), f32), ((2, nx, width), f32)],
-        back, cotangent, *grads, down_weight.reshape(nx, share, width), rows_of, down_gain.reshape(1, width),
+        back, cotangent, *sent, down_weight.reshape(nx, share, width), rows_of, down_gain.reshape(1, width),
         place=place,
     )
     dots = dots[:, :, :share].reshape(2, hidden)
@@ -482,8 +524,8 @@
         grad_gate,
         grad_up,
         grad_down.reshape(hidden, width),
-        dots[0] / gate_gain,
-        dots[1] / up_gain,
+        dots[0],
+        dots[1],
         down_dgain.reshape(width),
     )
 

time: 263 us -> 231 us (0.88)
  Pallas kernels: 39.9 us -> 17.5 us
  starting transfers between devices: 96.3 us -> 84.4 us
  blocking collectives: 53.2 us -> 55.9 us
    ppermute x15 -> x9, starting transfers between devices: 70 us -> 42.5 us  [shift(): return lax.ppermute(x, axis, [(i, (i + by) % size) for i in range(size)])]
    pallas_call x13 -> x12, Pallas kernels: 39.9 us -> 17.5 us  [call(): pl.pallas_call(body, out_shape=[jax.ShapeDtypeStruct(s, t) for s, t in ou...]
    ppermute x1 -> x3, waiting for transfers between devices: 1.38 us -> 17.2 us  [apart(): return lax.ppermute(x, ('core', axis), pairs)]
    ppermute x1 -> x3, starting transfers between devices: 1.91 us -> 15.3 us  [apart(): return lax.ppermute(x, ('core', axis), pairs)]
    ppermute x15 -> x9, waiting for transfers between devices: 37.5 us -> 24.1 us  [shift(): return lax.ppermute(x, axis, [(i, (i + by) % size) for i in range(size)])]
    all_to_all x3, waiting for transfers between devices: 21.8 us -> 17.4 us  [exchange(): return lax.all_to_all(x, axis, split_axis=0, concat_axis=0, tiled=True)]
    all_gather x1, blocking collectives: 31.4 us -> 34.3 us  [block(): d = lax.all_gather(d, 'zh')]
  transfers between devices with their start and end apart: 21 -> 17, of which waited for: 11 -> 10; matrix products, arithmetic and copies ran while one was open for 1% -> 0% of each run, Pallas kernels for 6% -> 3%
where the time goes in v3:
time: 231 us; the launch traced here: 230 us
  starting transfers between devices  84.4 us (37%)
  waiting for transfers between devices  60.5 us (26%)
  blocking collectives  55.9 us (24%)
  Pallas kernels  17.5 us (8%)
  local copies, waits for them, and re-layouts  10.4 us (5%)
    ppermute x9, starting transfers between devices, shift(): return lax.ppermute(x, axis, [(i, (i + by) % size) for i in range(size)])  42.5 us
    all_gather x1, blocking collectives, block(): d = lax.all_gather(d, 'zh')  34.3 us
    ppermute x9, waiting for transfers between devices, shift(): return lax.ppermute(x, axis, [(i, (i + by) % size) for i in range(size)])  24.1 us
    all_to_all x1, blocking collectives, exchange(): return lax.all_to_all(x, axis, split_axis=0, concat_axis=0, tiled=True)  21.6 us
    pallas_call x12, Pallas kernels, call(): pl.pallas_call(body, out_shape=[jax.ShapeDtypeStruct(s, t) for s, t in ou...  17.5 us
    all_to_all x3, waiting for transfers between devices, exchange(): return lax.all_to_all(x, axis, split_axis=0, concat_axis=0, tiled=True)  17.4 us
    all_to_all x3, starting transfers between devices, exchange(): return lax.all_to_all(x, axis, split_axis=0, concat_axis=0, tiled=True)  17.4 us
    ppermute x3, waiting for transfers between devices, apart(): return lax.ppermute(x, ('core', axis), pairs)  17.2 us
  transfers between devices with their start and end apart: 17, of which 10 were waited for; matrix products, arithmetic and copies ran while one was open for 0% of the time, Pallas kernels for 3%

profile of v3, /device:TPU:1, one launch (start us, length us, event | category | flops | bytes accessed | tf_op | source)
XLA Modules:
  0.0 229.7 jit_solution(16910340588079929925)
XLA Ops:
  0.6 2.7 %shard_map.136 = bf16[4,4,32,512]{3,2,1,0:T(8,128)(2,1)} custom-call(bf16[896,256]{1,0:T(8,128)(2,1)} %down_hbm.3, f32[1,256]{1,0:T(1,128)} %bitcast.19, bf16[20,256]{1,0:T(8,128)(2,1)} %tokens_hbm.1, bf16[20,256]{1,0:T(8,128)(2,1)} %cotangent_ref.1, bf16[256,896]{1,0:T(8,128)(2,1)} %gate_hbm.3, bf16[256,896]{1,0:T(8,128)(2,1)} %up_hbm.3), custom_call_target="tpu_custom_call" | custom-call | tf_op jit(solution)/shard_map/pallas_call | solution.py:403
  3.3 9.0 %all-to-all-start = ((bf16[16,32,512]{2,1,0:T(8,128)(2,1)}), bf16[16,32,512]{2,1,0:T(8,128)(2,1)S(1)}, u32[]{:S(2)}, u32[]{:S(2)}) async-start(bf16[16,32,512]{2,1,0:T(8,128)(2,1)} %bitcast.21), calls=%async_computation | async-start | bytes 1048576 | tf_op jit(solution)/shard_map/all_to_all | solution.py:413
  12.4 15.7 %all-to-all-done = bf16[16,32,512]{2,1,0:T(8,128)(2,1)S(1)} async-done(((bf16[16,32,512]{2,1,0:T(8,128)(2,1)}), bf16[16,32,512]{2,1,0:T(8,128)(2,1)S(1)}, u32[]{:S(2)}, u32[]{:S(2)}) %all-to-all-start) | async-done | bytes 524320 | tf_op jit(solution)/shard_map/all_to_all | solution.py:413
  28.9 21.6 %all_to_all.20.own_ref = bf16[4,4,88,512]{3,2,1,0:T(8,128)(2,1)S(1)} all-to-all(bf16[4,4,88,512]{3,2,1,0:T(8,128)(2,1)S(1)} %get-tuple-element.38), channel_id=1, replica_groups=mesh['y'=4,'zl'=4,'core'=2,'zh'=4,'x'=4] {'y'}, dimensions={0} | all-to-all | bytes 2883584 | tf_op jit(solution)/shard_map/all_to_all | solution.py:413
  50.4 4.7 %collective-permute-start.3 = (bf16[4,4,88,512]{3,2,1,0:T(8,128)(2,1)S(1)}, bf16[4,4,88,512]{3,2,1,0:T(8,128)(2,1)S(1)}, u32[]{:S(2)}, u32[]{:S(2)}) collective-permute-start(bf16[4,4,88,512]{3,2,1,0:T(8,128)(2,1)S(1)} %all_to_all.20.own_ref), channel_id=1, source_target_pairs={{0,16},{16,0},{1,17},{17,1},{2,18},{18,2},{3,19},{19,3},{4,20},{20... | collective-permute-start | bytes 4325384 | tf_op jit(solution)/shard_map/ppermute | solution.py:479
  55.2 1.9 shard_map.135
  57.1 1.9 collective-permute-start
  59.1 3.7 %collective-permute-start.1 = (bf16[3,224,256]{2,1,0:T(8,128)(2,1)S(1)}, bf16[3,224,256]{2,1,0:T(8,128)(2,1)S(1)}, u32[]{:S(2)}, u32[]{:S(2)}) collective-permute-start(bf16[3,224,256]{2,1,0:T(8,128)(2,1)S(1)} %get-tuple-element.36), channel_id=1, source_target_pairs={{0,2},{1,3},{2,0},{3,1},{4,6},{5,7},{6,4},{7,5},{8,10},{9,11},{10,... | collective-permute-start | bytes 1032200 | tf_op jit(solution)/shard_map/ppermute | solution.py:418
  62.7 2.8 %collective-permute-start.2 = (bf16[3,224,256]{2,1,0:T(8,128)(2,1)S(1)}, bf16[3,224,256]{2,1,0:T(8,128)(2,1)S(1)}, u32[]{:S(2)}, u32[]{:S(2)}) collective-permute-start(bf16[3,224,256]{2,1,0:T(8,128)(2,1)S(1)} %get-tuple-element.37), channel_id=1, source_target_pairs={{0,3},{1,0},{2,1},{3,2},{4,7},{5,4},{6,5},{7,6},{8,11},{9,8},{10,9... | collective-permute-start | bytes 1032200 | tf_op jit(solution)/shard_map/ppermute | solution.py:418
  65.6 8.8 %collective-permute-start.4 = (f32[8,256]{1,0:T(8,128)S(1)}, f32[8,256]{1,0:T(8,128)S(1)}, u32[]{:S(2)}, u32[]{:S(2)}) collective-permute-start(f32[8,256]{1,0:T(8,128)S(1)} %get-tuple-element.39.moment0_ref), channel_id=1, source_target_pairs={{0,4},{4,8},{8,12},{12,0},{1,5},{5,9},{9,13},{13,1},{2,6},{6,10},{... | collective-permute-start | bytes 24584 | tf_op jit(solution)/shard_map/ppermute | solution.py:418
  74.4 2.8 %collective-permute-done.w1_ref = bf16[3,224,256]{2,1,0:T(8,128)(2,1)S(1)} collective-permute-done((bf16[3,224,256]{2,1,0:T(8,128)(2,1)S(1)}, bf16[3,224,256]{2,1,0:T(8,128)(2,1)S(1)}, u32[]{:S(2)}, u32[]{:S(2)}) %collective-permute-start) | collective-permute-done | bytes 344096 | tf_op jit(solution)/shard_map/ppermute | solution.py:418
  77.2 12.7 %collective-permute-start.5 = (f32[8,256]{1,0:T(8,128)S(1)}, f32[8,256]{1,0:T(8,128)S(1)}, u32[]{:S(2)}, u32[]{:S(2)}) collective-permute-start(f32[8,256]{1,0:T(8,128)S(1)} %get-tuple-element.39.moment0_ref), channel_id=1, source_target_pairs={{0,8},{4,12},{8,0},{12,4},{1,9},{5,13},{9,1},{13,5},{2,10},{6,14},... | collective-permute-start | bytes 24584 | tf_op jit(solution)/shard_map/ppermute | solution.py:418
  90.0 3.1 %collective-permute-start.6 = (f32[8,256]{1,0:T(8,128)S(1)}, f32[8,256]{1,0:T(8,128)S(1)}, u32[]{:S(2)}, u32[]{:S(2)}) collective-permute-start(f32[8,256]{1,0:T(8,128)S(1)} %get-tuple-element.39.moment0_ref), channel_id=1, source_target_pairs={{0,12},{4,0},{8,4},{12,8},{1,13},{5,1},{9,5},{13,9},{2,14},{6,2},{... | collective-permute-start | bytes 24584 | tf_op jit(solution)/shard_map/ppermute | solution.py:418
  93.1 5.1 %collective-permute-done.6.moment3_ref = f32[8,256]{1,0:T(8,128)S(1)} collective-permute-done((f32[8,256]{1,0:T(8,128)S(1)}, f32[8,256]{1,0:T(8,128)S(1)}, u32[]{:S(2)}, u32[]{:S(2)}) %collective-permute-start.6) | collective-permute-done | bytes 8224 | tf_op jit(solution)/shard_map/ppermute | solution.py:418
  98.3 2.4 %shard_map.138 = (bf16[168,640]{1,0:T(8,128)(2,1)S(1)}, bf16[168,640]{1,0:T(8,128)(2,1)S(1)}, bf16[168,640]{1,0:T(8,128)(2,1)S(1)}, bf16[168,640]{1,0:T(8,128)(2...) custom-call(s32[5]{0:T(128)S(1)} %stack.23.place_ref, ...), custom_call_target="tpu_custom_call" | custom-call | tf_op jit(solution)/shard_map/pallas_call | solution.py:403
  100.7 3.4 %collective-permute-start.8 = (bf16[168,640]{1,0:T(8,128)(2,1)S(1)}, bf16[168,640]{1,0:T(8,128)(2,1)S(1)}, u32[]{:S(2)}, u32[]{:S(2)}) collective-permute-start(bf16[168,640]{1,0:T(8,128)(2,1)S(1)} %get-tuple-element.43), channel_id=1, source_target_pairs={{0,4},{4,8},{8,12},{12,0},{16,28},{20,16},{24,20},{28,24},{1,5},{5... | collective-permute-start | bytes 645128 | tf_op jit(solution)/shard_map/ppermute | solution.py:426
  104.1 5.8 %collective-permute-start.7 = (bf16[168,640]{1,0:T(8,128)(2,1)S(1)}, bf16[168,640]{1,0:T(8,128)(2,1)S(1)}, u32[]{:S(2)}, u32[]{:S(2)}) collective-permute-start(bf16[168,640]{1,0:T(8,128)(2,1)S(1)} %get-tuple-element.41), channel_id=1, source_target_pairs={{0,12},{4,0},{8,4},{12,8},{16,20},{20,24},{24,28},{28,16},{1,13},{... | collective-permute-start | bytes 645128 | tf_op jit(solution)/shard_map/ppermute | solution.py:426
  109.9 9.6 %collective-permute-done.8.b_ref = bf16[168,640]{1,0:T(8,128)(2,1)S(1)} collective-permute-done((bf16[168,640]{1,0:T(8,128)(2,1)S(1)}, bf16[168,640]{1,0:T(8,128)(2,1)S(1)}, u32[]{:S(2)}, u32[]{:S(2)}) %collective-permute-start.8) | collective-permute-done | bytes 215072 | tf_op jit(solution)/shard_map/ppermute | solution.py:426
  119.6 6.2 %collective-permute-start.9 = (bf16[168,640]{1,0:T(8,128)(2,1)S(1)}, bf16[168,640]{1,0:T(8,128)(2,1)S(1)}, u32[]{:S(2)}, u32[]{:S(2)}) collective-permute-start(bf16[168,640]{1,0:T(8,128)(2,1)S(1)} %shard_map.139), channel_id=1, source_target_pairs={{0,4},{4,8},{8,12},{12,0},{16,28},{20,16},{24,20},{28,24},{1,5},{5... | collective-permute-start | bytes 645128 | tf_op jit(solution)/shard_map/ppermute | solution.py:426
  125.8 7.6 %collective-permute-done.9.third_ref = bf16[168,640]{1,0:T(8,128)(2,1)S(1)} collective-permute-done((bf16[168,640]{1,0:T(8,128)(2,1)S(1)}, bf16[168,640]{1,0:T(8,128)(2,1)S(1)}, u32[]{:S(2)}, u32[]{:S(2)}) %collective-permute-start.9) | collective-permute-done | bytes 215072 | tf_op jit(solution)/shard_map/ppermute | solution.py:426
  133.7 34.3 %all-gather = bf16[704,640]{1,0:T(8,128)(2,1)S(1)} all-gather(bf16[176,640]{1,0:T(8,128)(2,1)S(1)} %shard_map.140), channel_id=2, replica_groups=mesh['y'=4,'zl'=4,'core'=2,'zh'=4,'x'=4] {'zh'}, dimensions={0}, use_global_device_ids=true | all-gather | bytes 1126400 | tf_op jit(solution)/shard_map/all_gather | solution.py:493
  169.6 4.5 %collective-permute-start.10 = (bf16[4,328,256]{2,1,0:T(8,128)(2,1)S(1)}, bf16[4,328,256]{2,1,0:T(8,128)(2,1)S(1)}, u32[]{:S(2)}, u32[]{:S(2)}) collective-permute-start(bf16[4,328,256]{2,1,0:T(8,128)(2,1)S(1)} %get-tuple-element.48), channel_id=1, source_target_pairs={{0,16},{16,0},{1,17},{17,1},{2,18},{18,2},{3,19},{19,3},{4,20},{20... | collective-permute-start | bytes 2015240 | tf_op jit(solution)/shard_map/ppermute | solution.py:500
  176.8 4.2 %all-to-all-start.2 = ((bf16[4,4,88,256]{3,2,1,0:T(8,128)(2,1)}), bf16[4,4,88,256]{3,2,1,0:T(8,128)(2,1)}, u32[]{:S(2)}, u32[]{:S(2)}) async-start(bf16[4,4,88,256]{3,2,1,0:T(8,128)(2,1)} %copy-done.11), calls=%async_computation.2 | async-start | bytes 1441792 | tf_op jit(solution)/shard_map/all_to_all | solution.py:413
  192.4 2.1 shard_map.144
  194.4 4.2 %all-to-all-start.3 = ((bf16[16,32,256]{2,1,0:T(8,128)(2,1)}), bf16[16,32,256]{2,1,0:T(8,128)(2,1)S(1)}, u32[]{:S(2)}, u32[]{:S(2)}) async-start(bf16[16,32,256]{2,1,0:T(8,128)(2,1)} %bitcast.9), calls=%async_computation.3 | async-start | bytes 524288 | tf_op jit(solution)/shard_map/all_to_all | solution.py:413
  198.6 4.5 %collective-permute-start.11 = (bf16[3,224,256]{2,1,0:T(8,128)(2,1)S(1)}, bf16[3,224,256]{2,1,0:T(8,128)(2,1)S(1)}, u32[]{:S(2)}, u32[]{:S(2)}) collective-permute-start(bf16[3,224,256]{2,1,0:T(8,128)(2,1)S(1)} %copy-done.23), channel_id=1, source_target_pairs={{0,3},{1,0},{2,1},{3,2},{4,7},{5,4},{6,5},{7,6},{8,11},{9,8},{10,9... | collective-permute-start | bytes 1032200 | tf_op jit(solution)/shard_map/ppermute | solution.py:418
  203.1 2.5 %collective-permute-start.12 = (bf16[3,224,256]{2,1,0:T(8,128)(2,1)S(1)}, bf16[3,224,256]{2,1,0:T(8,128)(2,1)S(1)}, u32[]{:S(2)}, u32[]{:S(2)}) collective-permute-start(bf16[3,224,256]{2,1,0:T(8,128)(2,1)S(1)} %copy-done.21), channel_id=1, source_target_pairs={{0,2},{1,3},{2,0},{3,1},{4,6},{5,7},{6,4},{7,5},{8,10},{9,11},{10,... | collective-permute-start | bytes 1032200 | tf_op jit(solution)/shard_map/ppermute | solution.py:418
  205.6 2.5 %collective-permute-start.13 = (bf16[3,224,256]{2,1,0:T(8,128)(2,1)S(1)}, bf16[3,224,256]{2,1,0:T(8,128)(2,1)S(1)}, u32[]{:S(2)}, u32[]{:S(2)}) collective-permute-start(bf16[3,224,256]{2,1,0:T(8,128)(2,1)S(1)} %copy-done.19), channel_id=1, source_target_pairs={{0,1},{1,2},{2,3},{3,0},{4,5},{5,6},{6,7},{7,4},{8,9},{9,10},{10,1... | collective-permute-start | bytes 1032200 | tf_op jit(solution)/shard_map/ppermute | solution.py:418
  208.1 3.9 %collective-permute-done.11.g1_ref = bf16[3,224,256]{2,1,0:T(8,128)(2,1)S(1)} collective-permute-done((bf16[3,224,256]{2,1,0:T(8,128)(2,1)S(1)}, bf16[3,224,256]{2,1,0:T(8,128)(2,1)S(1)}, u32[]{:S(2)}, u32[]{:S(2)}) %collective-permute-start.11) | collective-permute-done | bytes 344096 | tf_op jit(solution)/shard_map/ppermute | solution.py:418
  212.0 2.8 %collective-permute-done.12.g2_ref = bf16[3,224,256]{2,1,0:T(8,128)(2,1)S(1)} collective-permute-done((bf16[3,224,256]{2,1,0:T(8,128)(2,1)S(1)}, bf16[3,224,256]{2,1,0:T(8,128)(2,1)S(1)}, u32[]{:S(2)}, u32[]{:S(2)}) %collective-permute-start.12) | collective-permute-done | bytes 344096 | tf_op jit(solution)/shard_map/ppermute | solution.py:418
  214.8 9.5 %collective-permute-done.13.g3_ref = bf16[3,224,256]{2,1,0:T(8,128)(2,1)S(1)} collective-permute-done((bf16[3,224,256]{2,1,0:T(8,128)(2,1)S(1)}, bf16[3,224,256]{2,1,0:T(8,128)(2,1)S(1)}, u32[]{:S(2)}, u32[]{:S(2)}) %collective-permute-start.13) | collective-permute-done | bytes 344096 | tf_op jit(solution)/shard_map/ppermute | solution.py:418
  224.3 2.3 %shard_map.146 = (f32[256,896]{1,0:T(8,128)}, f32[256,896]{1,0:T(8,128)}) custom-call(s32[5]{0:T(128)S(1)} %stack.23.place_ref, bf16[3,224,256]{2,1,0:T(8,128)(2,1)S(1)} %copy-done.15, bf16[3,224,256]{2,1,0:T(8,128)(2,1)S(1)} %collective-permute-done.11.g1_ref, bf16[3,224,256]{2,1,0:T(8,128)(2,1)S(1)} %collective-permute-done.12.g2_ref, ...), custom_call_target="tpu_custom_call" | custom-call | tf_op jit(solution)/shard_map/pallas_call | solution.py:403
  (74 shorter events, 19.9 us)
Async XLA Ops:
  3.3 24.8 %all-to-all-start = ((bf16[16,32,512]{2,1,0:T(8,128)(2,1)}), bf16[16,32,512]{2,1,0:T(8,128)(2,1)S(1)}, u32[]{:S(2)}, u32[]{:S(2)}) async-start(bf16[16,32,512]{2,1,0:T(8,128)(2,1)} %bitcast.21), calls=%async_computation | async-start | bytes 1048576 | tf_op jit(solution)/shard_map/all_to_all | solution.py:413
  28.8 26.3 %copy-start.2 = (bf16[896,256]{1,0:T(8,128)(2,1)S(1)}, bf16[896,256]{1,0:T(8,128)(2,1)}, u32[]{:S(2)}) copy-start(bf16[896,256]{1,0:T(8,128)(2,1)} %down_hbm.3) | copy-start | bytes 1376260
  28.8 26.3 %copy-start.12 = (bf16[256,896]{1,0:T(8,128)(2,1)S(1)}, bf16[256,896]{1,0:T(8,128)(2,1)}, u32[]{:S(2)}) copy-start(bf16[256,896]{1,0:T(8,128)(2,1)} %gate_hbm.3) | copy-start | bytes 1376260
  28.8 26.3 %copy-start.13 = (bf16[256,896]{1,0:T(8,128)(2,1)S(1)}, bf16[256,896]{1,0:T(8,128)(2,1)}, u32[]{:S(2)}) copy-start(bf16[256,896]{1,0:T(8,128)(2,1)} %up_hbm.3) | copy-start | bytes 1376260
  28.9 64.2 %copy-start.24 = (f32[896]{0:T(1024)S(1)}, f32[896]{0:T(1024)}, u32[]{:S(2)}) copy-start(f32[896]{0:T(1024)} %param.13) | copy-start | bytes 10756
  28.9 64.2 %copy-start.25 = (f32[896]{0:T(1024)S(1)}, f32[896]{0:T(1024)}, u32[]{:S(2)}) copy-start(f32[896]{0:T(1024)} %param.14) | copy-start | bytes 10756
  50.4 47.9 %collective-permute-start.3 = (bf16[4,4,88,512]{3,2,1,0:T(8,128)(2,1)S(1)}, bf16[4,4,88,512]{3,2,1,0:T(8,128)(2,1)S(1)}, u32[]{:S(2)}, u32[]{:S(2)}) collective-permute-start(bf16[4,4,88,512]{3,2,1,0:T(8,128)(2,1)S(1)} %all_to_all.20.own_ref), channel_id=1, source_target_pairs={{0,16},{16,0},{1,17},{17,1},{2,18},{18,2},{3,19},{19,3},{4,20},{20... | collective-permute-start | bytes 4325384 | tf_op jit(solution)/shard_map/ppermute | solution.py:479
  57.1 110.9 %copy-start.3 = (bf16[3,224,256]{2,1,0:T(8,128)(2,1)}, bf16[3,224,256]{2,1,0:T(8,128)(2,1)S(1)}, u32[]{:S(2)}) copy-start(bf16[3,224,256]{2,1,0:T(8,128)(2,1)S(1)} %get-tuple-element.34.w0_ref) | copy-start | bytes 1032196
  57.1 20.1 %collective-permute-start = (bf16[3,224,256]{2,1,0:T(8,128)(2,1)S(1)}, bf16[3,224,256]{2,1,0:T(8,128)(2,1)S(1)}, u32[]{:S(2)}, u32[]{:S(2)}) collective-permute-start(bf16[3,224,256]{2,1,0:T(8,128)(2,1)S(1)} %get-tuple-element.35), channel_id=1, source_target_pairs={{0,1},{1,2},{2,3},{3,0},{4,5},{5,6},{6,7},{7,4},{8,9},{9,10},{10,1... | collective-permute-start | bytes 1032200 | tf_op jit(solution)/shard_map/ppermute | solution.py:418
  59.1 30.9 %collective-permute-start.1 = (bf16[3,224,256]{2,1,0:T(8,128)(2,1)S(1)}, bf16[3,224,256]{2,1,0:T(8,128)(2,1)S(1)}, u32[]{:S(2)}, u32[]{:S(2)}) collective-permute-start(bf16[3,224,256]{2,1,0:T(8,128)(2,1)S(1)} %get-tuple-element.36), channel_id=1, source_target_pairs={{0,2},{1,3},{2,0},{3,1},{4,6},{5,7},{6,4},{7,5},{8,10},{9,11},{10,... | collective-permute-start | bytes 1032200 | tf_op jit(solution)/shard_map/ppermute | solution.py:418
  62.7 30.4 %collective-permute-start.2 = (bf16[3,224,256]{2,1,0:T(8,128)(2,1)S(1)}, bf16[3,224,256]{2,1,0:T(8,128)(2,1)S(1)}, u32[]{:S(2)}, u32[]{:S(2)}) collective-permute-start(bf16[3,224,256]{2,1,0:T(8,128)(2,1)S(1)} %get-tuple-element.37), channel_id=1, source_target_pairs={{0,3},{1,0},{2,1},{3,2},{4,7},{5,4},{6,5},{7,6},{8,11},{9,8},{10,9... | collective-permute-start | bytes 1032200 | tf_op jit(solution)/shard_map/ppermute | solution.py:418
  65.6 27.6 %collective-permute-start.4 = (f32[8,256]{1,0:T(8,128)S(1)}, f32[8,256]{1,0:T(8,128)S(1)}, u32[]{:S(2)}, u32[]{:S(2)}) collective-permute-start(f32[8,256]{1,0:T(8,128)S(1)} %get-tuple-element.39.moment0_ref), channel_id=1, source_target_pairs={{0,4},{4,8},{8,12},{12,0},{1,5},{5,9},{9,13},{13,1},{2,6},{6,10},{... | collective-permute-start | bytes 24584 | tf_op jit(solution)/shard_map/ppermute | solution.py:418
  77.2 90.8 %copy-start.5 = (bf16[3,224,256]{2,1,0:T(8,128)(2,1)}, bf16[3,224,256]{2,1,0:T(8,128)(2,1)S(1)}, u32[]{:S(2)}) copy-start(bf16[3,224,256]{2,1,0:T(8,128)(2,1)S(1)} %collective-permute-done.w1_ref) | copy-start | bytes 1032196
  77.2 15.9 %collective-permute-start.5 = (f32[8,256]{1,0:T(8,128)S(1)}, f32[8,256]{1,0:T(8,128)S(1)}, u32[]{:S(2)}, u32[]{:S(2)}) collective-permute-start(f32[8,256]{1,0:T(8,128)S(1)} %get-tuple-element.39.moment0_ref), channel_id=1, source_target_pairs={{0,8},{4,12},{8,0},{12,4},{1,9},{5,13},{9,1},{13,5},{2,10},{6,14},... | collective-permute-start | bytes 24584 | tf_op jit(solution)/shard_map/ppermute | solution.py:418
  90.0 78.0 %copy-start.7 = (bf16[3,224,256]{2,1,0:T(8,128)(2,1)}, bf16[3,224,256]{2,1,0:T(8,128)(2,1)S(1)}, u32[]{:S(2)}) copy-start(bf16[3,224,256]{2,1,0:T(8,128)(2,1)S(1)} %collective-permute-done.1.w2_ref) | copy-start | bytes 1032196
  90.0 8.3 %collective-permute-start.6 = (f32[8,256]{1,0:T(8,128)S(1)}, f32[8,256]{1,0:T(8,128)S(1)}, u32[]{:S(2)}, u32[]{:S(2)}) collective-permute-start(f32[8,256]{1,0:T(8,128)S(1)} %get-tuple-element.39.moment0_ref), channel_id=1, source_target_pairs={{0,12},{4,0},{8,4},{12,8},{1,13},{5,1},{9,5},{13,9},{2,14},{6,2},{... | collective-permute-start | bytes 24584 | tf_op jit(solution)/shard_map/ppermute | solution.py:418
  93.1 74.9 %copy-start.9 = (bf16[3,224,256]{2,1,0:T(8,128)(2,1)}, bf16[3,224,256]{2,1,0:T(8,128)(2,1)S(1)}, u32[]{:S(2)}) copy-start(bf16[3,224,256]{2,1,0:T(8,128)(2,1)S(1)} %collective-permute-done.2.w3_ref) | copy-start | bytes 1032196
  100.7 18.8 %collective-permute-start.8 = (bf16[168,640]{1,0:T(8,128)(2,1)S(1)}, bf16[168,640]{1,0:T(8,128)(2,1)S(1)}, u32[]{:S(2)}, u32[]{:S(2)}) collective-permute-start(bf16[168,640]{1,0:T(8,128)(2,1)S(1)} %get-tuple-element.43), channel_id=1, source_target_pairs={{0,4},{4,8},{8,12},{12,0},{16,28},{20,16},{24,20},{28,24},{1,5},{5... | collective-permute-start | bytes 645128 | tf_op jit(solution)/shard_map/ppermute | solution.py:426
  104.1 21.7 %collective-permute-start.7 = (bf16[168,640]{1,0:T(8,128)(2,1)S(1)}, bf16[168,640]{1,0:T(8,128)(2,1)S(1)}, u32[]{:S(2)}, u32[]{:S(2)}) collective-permute-start(bf16[168,640]{1,0:T(8,128)(2,1)S(1)} %get-tuple-element.41), channel_id=1, source_target_pairs={{0,12},{4,0},{8,4},{12,8},{16,20},{20,24},{24,28},{28,16},{1,13},{... | collective-permute-start | bytes 645128 | tf_op jit(solution)/shard_map/ppermute | solution.py:426
  119.6 13.8 %collective-permute-start.9 = (bf16[168,640]{1,0:T(8,128)(2,1)S(1)}, bf16[168,640]{1,0:T(8,128)(2,1)S(1)}, u32[]{:S(2)}, u32[]{:S(2)}) collective-permute-start(bf16[168,640]{1,0:T(8,128)(2,1)S(1)} %shard_map.139), channel_id=1, source_target_pairs={{0,4},{4,8},{8,12},{12,0},{16,28},{20,16},{24,20},{28,24},{1,5},{5... | collective-permute-start | bytes 645128 | tf_op jit(solution)/shard_map/ppermute | solution.py:426
  169.6 6.2 %collective-permute-start.10 = (bf16[4,328,256]{2,1,0:T(8,128)(2,1)S(1)}, bf16[4,328,256]{2,1,0:T(8,128)(2,1)S(1)}, u32[]{:S(2)}, u32[]{:S(2)}) collective-permute-start(bf16[4,328,256]{2,1,0:T(8,128)(2,1)S(1)} %get-tuple-element.48), channel_id=1, source_target_pairs={{0,16},{16,0},{1,17},{17,1},{2,18},{18,2},{3,19},{19,3},{4,20},{20... | collective-permute-start | bytes 2015240 | tf_op jit(solution)/shard_map/ppermute | solution.py:500
  176.8 15.6 %all-to-all-start.2 = ((bf16[4,4,88,256]{3,2,1,0:T(8,128)(2,1)}), bf16[4,4,88,256]{3,2,1,0:T(8,128)(2,1)}, u32[]{:S(2)}, u32[]{:S(2)}) async-start(bf16[4,4,88,256]{3,2,1,0:T(8,128)(2,1)} %copy-done.11), calls=%async_computation.2 | async-start | bytes 1441792 | tf_op jit(solution)/shard_map/all_to_all | solution.py:413
  192.3 6.3 %copy-start.23 = (bf16[3,224,256]{2,1,0:T(8,128)(2,1)S(1)}, bf16[3,224,256]{2,1,0:T(8,128)(2,1)}, u32[]{:S(2)}) copy-start(bf16[3,224,256]{2,1,0:T(8,128)(2,1)} %copy-done.22) | copy-start | bytes 1032196
  192.3 10.8 %copy-start.21 = (bf16[3,224,256]{2,1,0:T(8,128)(2,1)S(1)}, bf16[3,224,256]{2,1,0:T(8,128)(2,1)}, u32[]{:S(2)}) copy-start(bf16[3,224,256]{2,1,0:T(8,128)(2,1)} %copy-done.20) | copy-start | bytes 1032196
  192.3 13.3 %copy-start.19 = (bf16[3,224,256]{2,1,0:T(8,128)(2,1)S(1)}, bf16[3,224,256]{2,1,0:T(8,128)(2,1)}, u32[]{:S(2)}) copy-start(bf16[3,224,256]{2,1,0:T(8,128)(2,1)} %copy-done.18) | copy-start | bytes 1032196
  192.3 32.0 %copy-start.15 = (bf16[3,224,256]{2,1,0:T(8,128)(2,1)S(1)}, bf16[3,224,256]{2,1,0:T(8,128)(2,1)}, u32[]{:S(2)}) copy-start(bf16[3,224,256]{2,1,0:T(8,128)(2,1)} %copy-done.14) | copy-start | bytes 1032196
  192.3 34.3 %copy-start.16 = (bf16[20,256]{1,0:T(8,128)(2,1)S(1)}, bf16[20,256]{1,0:T(8,128)(2,1)}, u32[]{:S(2)}) copy-start(bf16[20,256]{1,0:T(8,128)(2,1)} %cotangent_ref.1) | copy-start | bytes 30724
  192.4 34.3 %copy-start.17 = (f32[256]{0:T(256)S(1)}, f32[256]{0:T(256)}, u32[]{:S(2)}) copy-start(f32[256]{0:T(256)} %param.15) | copy-start | bytes 3076
  194.4 32.2 %all-to-all-start.3 = ((bf16[16,32,256]{2,1,0:T(8,128)(2,1)}), bf16[16,32,256]{2,1,0:T(8,128)(2,1)S(1)}, u32[]{:S(2)}, u32[]{:S(2)}) async-start(bf16[16,32,256]{2,1,0:T(8,128)(2,1)} %bitcast.9), calls=%async_computation.3 | async-start | bytes 524288 | tf_op jit(solution)/shard_map/all_to_all | solution.py:413
  198.6 13.3 %collective-permute-start.11 = (bf16[3,224,256]{2,1,0:T(8,128)(2,1)S(1)}, bf16[3,224,256]{2,1,0:T(8,128)(2,1)S(1)}, u32[]{:S(2)}, u32[]{:S(2)}) collective-permute-start(bf16[3,224,256]{2,1,0:T(8,128)(2,1)S(1)} %copy-done.23), channel_id=1, source_target_pairs={{0,3},{1,0},{2,1},{3,2},{4,7},{5,4},{6,5},{7,6},{8,11},{9,8},{10,9... | collective-permute-start | bytes 1032200 | tf_op jit(solution)/shard_map/ppermute | solution.py:418
  203.1 11.7 %collective-permute-start.12 = (bf16[3,224,256]{2,1,0:T(8,128)(2,1)S(1)}, bf16[3,224,256]{2,1,0:T(8,128)(2,1)S(1)}, u32[]{:S(2)}, u32[]{:S(2)}) collective-permute-start(bf16[3,224,256]{2,1,0:T(8,128)(2,1)S(1)} %copy-done.21), channel_id=1, source_target_pairs={{0,2},{1,3},{2,0},{3,1},{4,6},{5,7},{6,4},{7,5},{8,10},{9,11},{10,... | collective-permute-start | bytes 1032200 | tf_op jit(solution)/shard_map/ppermute | solution.py:418
  205.6 18.7 %collective-permute-start.13 = (bf16[3,224,256]{2,1,0:T(8,128)(2,1)S(1)}, bf16[3,224,256]{2,1,0:T(8,128)(2,1)S(1)}, u32[]{:S(2)}, u32[]{:S(2)}) collective-permute-start(bf16[3,224,256]{2,1,0:T(8,128)(2,1)S(1)} %copy-done.19), channel_id=1, source_target_pairs={{0,1},{1,2},{2,3},{3,0},{4,5},{5,6},{6,7},{7,4},{8,9},{9,10},{10,1... | collective-permute-start | bytes 1032200 | tf_op jit(solution)/shard_map/ppermute | solution.py:418
  (11 other events, 10.4 us)

commit v4 on v3

--- a/solution.py
+++ b/solution.py
@@ -64,54 +64,28 @@
 
 
 def pack_tokens(
-    down_hbm, gain_hbm, tokens_hbm, cotangent_hbm, gate_hbm, up_hbm, out_ref,
-    down_ref, gain_ref, tokens_ref, cotangent_ref, gate_ref, up_ref, sems,
+    down_hbm, gain_hbm, tokens_hbm, cotangent_hbm, out_ref, down_ref, gain_ref, tokens_ref, cotangent_ref, sems
 ):
     copies = fetched(
-        (
-            (down_hbm, down_ref), (gain_hbm, gain_ref), (tokens_hbm, tokens_ref), (cotangent_hbm, cotangent_ref),
-            (gate_hbm, gate_ref), (up_hbm, up_ref),
-        ),
-        sems,
-    )
-    rows, width = tokens_ref.shape
-
-    def moments(ref):
-        w = ref[...].astype(f32)
-        mean = jnp.sum(w, axis=0, keepdims=True) * (1.0 / w.shape[0])
-        off = w - mean
-        return mean, jnp.sum(off * off, axis=0, keepdims=True)
-
-    def single(x):
-        return [p.astype(f32) for p in pieces(x)]
-
+        ((down_hbm, down_ref), (gain_hbm, gain_ref), (tokens_hbm, tokens_ref), (cotangent_hbm, cotangent_ref)), sems
+    )
+    _, width = tokens_ref.shape
     copies[0].wait()
-    mean, square = moments(down_ref)
-    for c in copies[1:4]:
+    w = down_ref[...].astype(f32)
+    mean = jnp.sum(w, axis=0, keepdims=True) * (1.0 / w.shape[0])
+    off = w - mean
+    square = jnp.sum(off * off, axis=0, keepdims=True)
+    for c in copies[1:]:
         c.wait()
     scaled = (branch_scale * cotangent_ref[...].astype(f32)).astype(bf16)
-    gain = single(gain_ref[...])
-    left = jnp.concatenate([tokens_ref[...].astype(f32), *single(mean), gain[0]], axis=0).astype(bf16)
-    right = jnp.concatenate([scaled.astype(f32), *single(square), gain[1]], axis=0).astype(bf16)
-    wide = []
-    for c, ref in zip(copies[4:], (gate_ref, up_ref)):
-        c.wait()
-        wide.append(moments(ref))
-    blocks, lines = out_ref.shape[0], out_ref.shape[1]
-    share = gate_ref.shape[1] // blocks
-    for j in range(blocks):
-        sides = []
-        for side in range(2):
-            parts = []
-            for pair in wide:
-                row = pair[side][:, j * share : (j + 1) * share]
-                parts += single(jnp.concatenate([row, jnp.zeros((1, width - share), f32)], axis=1))
-            sides.append(jnp.concatenate([*parts, jnp.zeros((2, width), f32)], axis=0).astype(bf16))
-        for l in range(lines):
-            out_ref[j, l, 0 : rows + 4, 0:width] = left
-            out_ref[j, l, 0 : rows + 4, width : 2 * width] = right
-            out_ref[j, l, rows + 4 : rows + 12, 0:width] = sides[0]
-            out_ref[j, l, rows + 4 : rows + 12, width : 2 * width] = sides[1]
+    gain = pieces(gain_ref[...])
+    left = [tokens_ref[...], *pieces(mean), gain[0]]
+    right = [scaled, *pieces(square), gain[1]]
+    for side, parts in enumerate((left, right)):
+        block = jnp.concatenate([p.astype(f32) for p in parts], axis=0).astype(bf16)
+        for j in range(out_ref.shape[0]):
+            for l in range(out_ref.shape[1]):
+                out_ref[j, l, :, side * width : (side + 1) * width] = block
 
 
 def pack_weights(place_ref, gate_hbm, up_hbm, down_hbm, *refs):
@@ -130,9 +104,9 @@
         outs[k][...] = store_ref[lax.rem(place_ref[1] + k, blocks)]
 
 
-def repack_tokens(wide_count, tall_count, place_ref, in_ref, out_ref, moment_ref):
+def repack_tokens(tall_count, place_ref, in_ref, out_ref):
     blocks, lines, high, wide = in_ref.shape
-    rows = high - 12
+    rows = high - 4
     width = wide // 2
     for j in range(blocks):
         source = lax.rem(place_ref[1] + blocks - j, blocks)
@@ -149,16 +123,6 @@
             block = jnp.concatenate(parts, axis=0).astype(bf16)
             for y in range(out_ref.shape[0]):
                 out_ref[y, j, :, a : a + width] = block
-    line = place_ref[2]
-    own = [in_ref[j, line, rows + 4 : rows + 12, :].astype(f32) for j in range(blocks)]
-    found = []
-    for at in range(2):
-        moments = [
-            (joined(o[3 * at : 3 * at + 3, 0:width]), joined(o[3 * at : 3 * at + 3, width:])) for o in own
-        ]
-        found += merged(moments, wide_count)
-    block = jnp.concatenate([*found, jnp.zeros((4, width), f32)], axis=0)
-    moment_ref[...] = block
 
 
 def whole(own_ref, other_ref, j, at):
@@ -170,48 +134,37 @@
     return jnp.concatenate(halves, axis=0)
 
 
+def moments_of(w_ref, at):
+    blocks = [w[at].astype(f32) for w in w_ref]
+    mean = sum(jnp.sum(w, axis=1, keepdims=True) for w in blocks) * (1.0 / (len(blocks) * blocks[0].shape[1]))
+    square = sum(jnp.sum((w - mean) * (w - mean), axis=1, keepdims=True) for w in blocks)
+    return mean, square
+
+
 def forward(
-    wide_count, tall_count, place_ref, w0_ref, w1_ref, w2_ref, w3_ref, own_ref, other_ref,
-    moment0_ref, moment1_ref, moment2_ref, moment3_ref, gate_gain_ref, up_gain_ref,
-    kept_ref, first_ref, second_ref, third_ref,
-    cols_ref, rows_ref, row_ref, store_ref,
+    tall_count, place_ref, w0_ref, w1_ref, w2_ref, w3_ref, own_ref, other_ref,
+    kept_ref, first_ref, second_ref, third_ref, rows_ref, news_ref, store_ref,
 ):
     w_ref = (w0_ref, w1_ref, w2_ref, w3_ref)
     blocks = len(w_ref)
     _, share, width = w0_ref.shape
     parts = store_ref.shape[0]
     tall = share // parts
-    lane = lax.broadcasted_iota(jnp.int32, cols_ref.shape, 1)
-    cols = jnp.zeros(cols_ref.shape, f32)
-    row = 0.0
     lefts = [whole(own_ref, other_ref, j, 0) for j in range(blocks)]
     ones = jnp.ones((8, width), bf16)
-    for j in range(blocks):
-        row = row + nt(ones, lefts[j])
-    row_ref[...] = row
+    row = sum(nt(ones, left) for left in lefts)[0:1]
+    levels = []
     for at in range(2):
-        moments = [
-            (ref[2 * at : 2 * at + 1, :], ref[2 * at + 1 : 2 * at + 2, :])
-            for ref in (moment0_ref, moment1_ref, moment2_ref, moment3_ref)
-        ]
-        mean, square = merged(moments, wide_count)
-        mean = upright(mean, share)
-        scale = upright(lax.rsqrt(square + epsilon), share)
-        row_of = (gate_gain_ref, up_gain_ref)[at]
-        gain = sum(
-            jnp.where(place_ref[1] == j, row_of[:, j * share : (j + 1) * share], 0.0) for j in range(blocks)
-        )
-        gain = upright(gain, share)
-        gs = gain * scale
-        for k, v in ((3 * at, mean), (3 * at + 1, gs), (3 * at + 2, scale), (6 + at, gain)):
-            cols = jnp.where(lane == k, v, cols)
-        total = 0.0
-        for j in range(blocks):
-            total = total + nt(w_ref[j][at], lefts[j])
-        total = ((total - mean * row[0:1]) * gs).astype(bf16)
+        mean, square = moments_of(w_ref, at)
+        levels += [level(mean, 256), level(square, 256)]
+        total = sum(nt(w_ref[j][at], lefts[j]) for j in range(blocks))
+        total = (total - mean * row).astype(bf16)
         for q in range(parts):
             store_ref[q, at * tall : (at + 1) * tall, :] = total[q * tall : (q + 1) * tall]
-    cols_ref[...] = cols
+    rest = jnp.zeros((1, row.shape[1] - 512), f32)
+    lines = [row] + [jnp.concatenate([levels[2 * at], levels[2 * at + 1], rest], axis=1) for at in range(2)]
+    lines = [p.astype(f32) for line in lines for p in pieces(line)[0:2]]
+    news_ref[...] = jnp.concatenate([*lines, jnp.zeros((2, row.shape[1]), f32)], axis=0).astype(bf16)
     total = 0.0
     rows = own_ref.shape[2] - 8
     for j in range(blocks):
@@ -230,17 +183,57 @@
         store_ref[q, 2 * tall : 3 * tall, :] = total[q * tall : (q + 1) * tall]
     at, core = place_ref[0], place_ref[4]
     for ref, k in ((kept_ref, 0), (first_ref, 2), (second_ref, 3 - 2 * core), (third_ref, 1 + 2 * core)):
-        ref[...] = store_ref[lax.rem(at + k, parts)]
+        ref[0 : 3 * tall, :] = store_ref[lax.rem(at + k, parts)]
+    for ref in (first_ref, second_ref):
+        ref[3 * tall : 3 * tall + 8, :] = news_ref[...]
 
 
 def add_pair(a_ref, b_ref, out_ref):
-    out_ref[...] = (a_ref[...].astype(f32) + b_ref[...].astype(f32)).astype(bf16)
-
-
-def gating(kept_ref, second_ref, third_ref, row_ref, d_ref):
+    high = a_ref.shape[0]
+    out_ref[0:high, :] = (a_ref[...].astype(f32) + b_ref[0:high, :].astype(f32)).astype(bf16)
+    out_ref[high:, :] = b_ref[high:, :]
+
+
+def gating(
+    wide_count, place_ref, kept_ref, first_ref, second_ref, third_ref, news_ref, gate_gain_ref, up_gain_ref,
+    d_ref, cols_ref, row_ref,
+):
     tall = (d_ref.shape[0] - 8) // 3
-    total = kept_ref[...].astype(f32) + second_ref[...].astype(f32) + third_ref[...].astype(f32)
-    gate, up, dhidden = total[0:tall], total[tall : 2 * tall], total[2 * tall : 3 * tall]
+    share = cols_ref.shape[0]
+    high = 3 * tall
+    news = [news_ref[...].astype(f32)]
+    news += [ref[high : high + 8, :].astype(f32) for ref in (first_ref, second_ref, third_ref)]
+    rows = [n[0:1] + n[1:2] for n in news]
+    row = sum(rows)
+    row_ref[...] = jnp.broadcast_to(row, row_ref.shape)
+    lane = lax.broadcasted_iota(jnp.int32, cols_ref.shape, 1)
+    cols = jnp.zeros(cols_ref.shape, f32)
+    for at in range(2):
+        both = [n[2 * at + 2 : 2 * at + 3] + n[2 * at + 3 : 2 * at + 4] for n in news]
+        moments = [(b[:, 0:256], b[:, 256:512]) for b in both]
+        mean, square = merged(moments, wide_count)
+        gains = (gate_gain_ref, up_gain_ref)[at]
+        gain = sum(
+            jnp.where(place_ref[1] == j, gains[:, j * share : (j + 1) * share], 0.0)
+            for j in range(gains.shape[1] // share)
+        )
+        scale = upright(lax.rsqrt(square + epsilon), share)
+        gain = upright(gain, share)
+        found = [(3 * at, upright(mean, share)), (3 * at + 1, gain * scale), (3 * at + 2, scale), (6 + at, gain)]
+        found += [(8 + 4 * at + q, upright(m, share)) for q, (m, _) in enumerate(moments)]
+        for k, v in found:
+            cols = jnp.where(lane == k, v, cols)
+    cols_ref[...] = cols
+    mine = cols_ref[pl.ds(pl.multiple_of(place_ref[0] * tall, 8), tall), :]
+    total = kept_ref[...].astype(f32) + second_ref[0:high, :].astype(f32) + third_ref[0:high, :].astype(f32)
+    sums = []
+    for at in range(2):
+        x = total[at * tall : (at + 1) * tall] - mine[:, 3 * at : 3 * at + 1] * row
+        for q, r in enumerate(rows):
+            x = x + mine[:, 8 + 4 * at + q : 9 + 4 * at + q] * r
+        sums.append(mine[:, 3 * at + 1 : 3 * at + 2] * x)
+    gate, up = sums
+    dhidden = total[2 * tall : 3 * tall]
     sig = 1.0 / (1.0 + jnp.exp(-gate))
     act = gate * sig
     d_gate = (dhidden * up * sig * (1.0 + gate * (1.0 - sig))).astype(bf16)
@@ -254,8 +247,7 @@
     ]
     wide = d_ref.shape[1]
     dots = jnp.concatenate([*dots, jnp.zeros((1, wide - 256), f32)], axis=1)
-    extra = [*pieces(dots), *pieces(row_ref[0:1, :])]
-    extra = [p.astype(f32) for p in extra] + [jnp.zeros((2, wide), f32)]
+    extra = [p.astype(f32) for p in pieces(dots)] + [jnp.zeros((5, wide), f32)]
     d_ref[3 * tall : 3 * tall + 8, :] = jnp.concatenate(extra, axis=0).astype(bf16)
 
 
@@ -266,7 +258,7 @@
 
 
 def weight_grads(
-    width_all, d_ref, w0_ref, w1_ref, w2_ref, w3_ref, own_ref, other_ref, cols_ref,
+    width_all, d_ref, w0_ref, w1_ref, w2_ref, w3_ref, own_ref, other_ref, cols_ref, row_ref,
     g0_ref, g1_ref, g2_ref, g3_ref, dots_ref,
 ):
     w_ref = (w0_ref, w1_ref, w2_ref, w3_ref)
@@ -277,7 +269,7 @@
     tall = share // parts
     streams = [stacked(d_ref, at, tall) for at in range(3)]
     extra = [d_ref[q, 3 * tall : 3 * tall + 8, :].astype(f32) for q in range(parts)]
-    row = sum(joined(e[3:6]) for e in extra)
+    row = row_ref[0:1, :]
     dots_ref[...] = jnp.zeros(dots_ref.shape, f32)
     means, pulls = [], []
     for at in range(2):
@@ -446,14 +438,13 @@
         return flat.reshape(x.shape)
 
     (both,) = call(
-        pack_tokens, [((nx, nl, rows + 12, 2 * width), bf16)],
-        down_weight, down_gain.reshape(1, width), tokens, cotangent, gate_weight, up_weight,
-        far=6,
+        pack_tokens, [((nx, nl, rows + 4, 2 * width), bf16)],
+        down_weight, down_gain.reshape(1, width), tokens, cotangent,
+        far=4,
         grant=60,
         scratch=[
             pltpu.VMEM((hidden, width), bf16), pltpu.VMEM((1, width), f32),
-            pltpu.VMEM((rows, width), bf16), pltpu.VMEM((rows, width), bf16),
-            pltpu.VMEM((width, hidden), bf16), pltpu.VMEM((width, hidden), bf16), pltpu.SemaphoreType.DMA((6,)),
+            pltpu.VMEM((rows, width), bf16), pltpu.VMEM((rows, width), bf16), pltpu.SemaphoreType.DMA((4,)),
         ],
     )
     both = grid_exchange(both, ("x", "zl"))
@@ -470,26 +461,29 @@
     weights = [cut_weights[0]]
     for k in (1, 2, 3):
         weights.append(shift(cut_weights[k], "x", k))
-    both, moments = call(
-        functools.partial(repack_tokens, width, hidden),
-        [((ny, nx, nl * rows + 8, 2 * width), bf16), ((8, width), f32)], both, place=place,
+    (both,) = call(
+        functools.partial(repack_tokens, hidden), [((ny, nx, nl * rows + 8, 2 * width), bf16)], both, place=place
     )
     own = exchange(both, "y")
-    moments = [moments, *(shift(moments, "zh", k) for k in (1, 2, 3))]
     other = lax.ppermute(own, "core", swap)
-    piece = ((3 * tall, count), bf16)
-    kept, first, second, third, cols, rows_of, row = call(
-        functools.partial(forward, width * nx, hidden * nl),
-        [piece, piece, piece, piece, ((share, 128), f32), ((nx, 8, width), f32), ((8, count), f32)],
-        *weights, own, other, *moments, gate_gain.reshape(1, hidden), up_gain.reshape(1, hidden),
+    piece, sent = ((3 * tall, count), bf16), ((3 * tall + 8, count), bf16)
+    kept, first, second, third, rows_of, news = call(
+        functools.partial(forward, hidden * nl),
+        [piece, sent, sent, piece, ((nx, 8, width), f32), ((8, count), bf16)],
+        *weights, own, other,
         place=place,
         scratch=[pltpu.VMEM((nz, 3 * tall, count), bf16)],
     )
     first = apart(first, "zh", 1)
     second = apart(second, "zh", -1)
-    (third,) = call(add_pair, [piece], third, first)
+    (third,) = call(add_pair, [sent], third, first)
     third = apart(third, "zh", 1)
-    (d,) = call(gating, [((3 * tall + 8, count), bf16)], kept, second, third, row)
+    d, cols, row = call(
+        functools.partial(gating, width * nx),
+        [((3 * tall + 8, count), bf16), ((share, 128), f32), ((8, count), f32)],
+        kept, first, second, third, news, gate_gain.reshape(1, hidden), up_gain.reshape(1, hidden),
+        place=place,
+    )
     d = lax.all_gather(d, "zh")
 
     half = count // nc
@@ -500,22 +494,22 @@
     theirs = lax.ppermute(theirs, "core", swap)
     *grads, dots = call(
         functools.partial(weight_grads, width_all), [((3, share, width), bf16)] * nx + [((8, width), f32)],
-        d, *weights, own, other, cols,
+        d, *weights, own, other, cols, row,
     )
     (back,) = call(both_cores, [((ny, nx, nl * rows + 8, width), bf16)], mine, theirs, sums)
     back = exchange(back, "y")
-    sent = [grads[0], None, None, None]
+    met = [grads[0], None, None, None]
     for k in (2, 1, 3):
-        sent[k] = shift(grads[k], "x", -k)
+        met[k] = shift(grads[k], "x", -k)
     (back,) = call(whole_column, [((nl, nx, rows + 12, width), bf16)], back, dots, place=place)
     back = grid_exchange(back, ("zl", "x"))
-    grad_gate, grad_up = call(finish_wide, [((width, hidden), f32), ((width, hidden), f32)], *sent,
+    grad_gate, grad_up = call(finish_wide, [((width, hidden), f32), ((width, hidden), f32)], *met,
         place=place, scratch=[pltpu.VMEM((nx, share, width), f32)],
     )
     grad_tokens, grad_down, down_dgain, dots = call(
         functools.partial(finish_tall, hidden_all),
         [((rows, width), f32), ((nx, share, width), f32), ((1, width), f32), ((2, nx, width), f32)],
-        back, cotangent, *sent, down_weight.reshape(nx, share, width), rows_of, down_gain.reshape(1, width),
+        back, cotangent, *met, down_weight.reshape(nx, share, width), rows_of, down_gain.reshape(1, width),
         place=place,
     )
     dots = dots[:, :, :share].reshape(2, hidden)

time: 231 us -> 221 us (0.957)
  starting transfers between devices: 84.4 us -> 70.5 us
  waiting for transfers between devices: 60.5 us -> 67.9 us
  blocking collectives: 55.9 us -> 52 us
    ppermute x9 -> x6, starting transfers between devices: 42.5 us -> 17.9 us  [shift(): return lax.ppermute(x, axis, [(i, (i + by) % size) for i in range(size)])]
    ppermute x9 -> x6, waiting for transfers between devices: 24.1 us -> 30.1 us  [shift(): return lax.ppermute(x, axis, [(i, (i + by) % size) for i in range(size)])]
    ppermute x3, waiting for transfers between devices: 17.2 us -> 21.7 us  [apart(): return lax.ppermute(x, ('core', axis), pairs)]
    all_to_all x3, starting transfers between devices: 17.4 us -> 21.8 us  [exchange(): return lax.all_to_all(x, axis, split_axis=0, concat_axis=0, tiled=True)]
    ppermute x3, starting transfers between devices: 15.3 us -> 19.7 us  [apart(): return lax.ppermute(x, ('core', axis), pairs)]
    all_gather x1, blocking collectives: 34.3 us -> 30.4 us  [block(): d = lax.all_gather(d, 'zh')]
    all_to_all x3, waiting for transfers between devices: 17.4 us -> 14.4 us  [exchange(): return lax.all_to_all(x, axis, split_axis=0, concat_axis=0, tiled=True)]
  transfers between devices with their start and end apart: 17 -> 14, of which waited for: 10 -> 10; matrix products, arithmetic and copies ran while one was open for 0% -> 0% of each run, Pallas kernels for 3% -> 3%
where the time goes in v4:
time: 221 us; the launch traced here: 220 us
  starting transfers between devices  70.5 us (32%)
  waiting for transfers between devices  67.9 us (31%)
  blocking collectives  52 us (24%)
  Pallas kernels  18.4 us (8%)
  local copies, waits for them, and re-layouts  10.4 us (5%)
    all_gather x1, blocking collectives, block(): d = lax.all_gather(d, 'zh')  30.4 us
    ppermute x6, waiting for transfers between devices, shift(): return lax.ppermute(x, axis, [(i, (i + by) % size) for i in range(size)])  30.1 us
    all_to_all x3, starting transfers between devices, exchange(): return lax.all_to_all(x, axis, split_axis=0, concat_axis=0, tiled=True)  21.8 us
    ppermute x3, waiting for transfers between devices, apart(): return lax.ppermute(x, ('core', axis), pairs)  21.7 us
    all_to_all x1, blocking collectives, exchange(): return lax.all_to_all(x, axis, split_axis=0, concat_axis=0, tiled=True)  21.6 us
    ppermute x3, starting transfers between devices, apart(): return lax.ppermute(x, ('core', axis), pairs)  19.7 us
    pallas_call x12, Pallas kernels, call(): pl.pallas_call(body, out_shape=[jax.ShapeDtypeStruct(s, t) for s, t in ou...  18.4 us
    ppermute x6, starting transfers between devices, shift(): return lax.ppermute(x, axis, [(i, (i + by) % size) for i in range(size)])  17.9 us
  transfers between devices with their start and end apart: 14, of which 10 were waited for; matrix products, arithmetic and copies ran while one was open for 0% of the time, Pallas kernels for 3%

profile of v4, /device:TPU:1, one launch (start us, length us, event | category | flops | bytes accessed | tf_op | source)
XLA Modules:
  0.0 220.1 jit_solution(16337574053318338630)
XLA Ops:
  0.6 2.1 shard_map.136
  2.7 9.0 %all-to-all-start = ((bf16[16,24,512]{2,1,0:T(8,128)(2,1)}), bf16[16,24,512]{2,1,0:T(8,128)(2,1)S(1)}, u32[]{:S(2)}, u32[]{:S(2)}) async-start(bf16[16,24,512]{2,1,0:T(8,128)(2,1)} %bitcast.21), calls=%async_computation | async-start | bytes 786432 | tf_op jit(solution)/shard_map/all_to_all | solution.py:405
  11.8 12.9 %all-to-all-done = bf16[16,24,512]{2,1,0:T(8,128)(2,1)S(1)} async-done(((bf16[16,24,512]{2,1,0:T(8,128)(2,1)}), bf16[16,24,512]{2,1,0:T(8,128)(2,1)S(1)}, u32[]{:S(2)}, u32[]{:S(2)}) %all-to-all-start) | async-done | bytes 393248 | tf_op jit(solution)/shard_map/all_to_all | solution.py:405
  25.5 21.6 %all_to_all.20.own_ref = bf16[4,4,88,512]{3,2,1,0:T(8,128)(2,1)S(1)} all-to-all(bf16[4,4,88,512]{3,2,1,0:T(8,128)(2,1)S(1)} %shard_map.137), channel_id=1, replica_groups=mesh['y'=4,'zl'=4,'core'=2,'zh'=4,'x'=4] {'y'}, dimensions={0} | all-to-all | bytes 2883584 | tf_op jit(solution)/shard_map/all_to_all | solution.py:405
  47.0 4.7 %collective-permute-start.3 = (bf16[4,4,88,512]{3,2,1,0:T(8,128)(2,1)S(1)}, bf16[4,4,88,512]{3,2,1,0:T(8,128)(2,1)S(1)}, u32[]{:S(2)}, u32[]{:S(2)}) collective-permute-start(bf16[4,4,88,512]{3,2,1,0:T(8,128)(2,1)S(1)} %all_to_all.20.own_ref), channel_id=1, source_target_pairs={{0,16},{16,0},{1,17},{17,1},{2,18},{18,2},{3,19},{19,3},{4,20},{20... | collective-permute-start | bytes 4325384 | tf_op jit(solution)/shard_map/ppermute | solution.py:468
  51.8 1.9 shard_map.135
  53.7 1.9 collective-permute-start
  55.6 3.7 %collective-permute-start.1 = (bf16[3,224,256]{2,1,0:T(8,128)(2,1)S(1)}, bf16[3,224,256]{2,1,0:T(8,128)(2,1)S(1)}, u32[]{:S(2)}, u32[]{:S(2)}) collective-permute-start(bf16[3,224,256]{2,1,0:T(8,128)(2,1)S(1)} %get-tuple-element.36), channel_id=1, source_target_pairs={{0,2},{1,3},{2,0},{3,1},{4,6},{5,7},{6,4},{7,5},{8,10},{9,11},{10,... | collective-permute-start | bytes 1032200 | tf_op jit(solution)/shard_map/ppermute | solution.py:410
  59.3 2.8 %collective-permute-start.2 = (bf16[3,224,256]{2,1,0:T(8,128)(2,1)S(1)}, bf16[3,224,256]{2,1,0:T(8,128)(2,1)S(1)}, u32[]{:S(2)}, u32[]{:S(2)}) collective-permute-start(bf16[3,224,256]{2,1,0:T(8,128)(2,1)S(1)} %get-tuple-element.37), channel_id=1, source_target_pairs={{0,3},{1,0},{2,1},{3,2},{4,7},{5,4},{6,5},{7,6},{8,11},{9,8},{10,9... | collective-permute-start | bytes 1032200 | tf_op jit(solution)/shard_map/ppermute | solution.py:410
  62.1 11.6 %collective-permute-done.w1_ref = bf16[3,224,256]{2,1,0:T(8,128)(2,1)S(1)} collective-permute-done((bf16[3,224,256]{2,1,0:T(8,128)(2,1)S(1)}, bf16[3,224,256]{2,1,0:T(8,128)(2,1)S(1)}, u32[]{:S(2)}, u32[]{:S(2)}) %collective-permute-start) | collective-permute-done | bytes 344096 | tf_op jit(solution)/shard_map/ppermute | solution.py:410
  73.8 2.2 %collective-permute-done.2.w3_ref = bf16[3,224,256]{2,1,0:T(8,128)(2,1)S(1)} collective-permute-done((bf16[3,224,256]{2,1,0:T(8,128)(2,1)S(1)}, bf16[3,224,256]{2,1,0:T(8,128)(2,1)S(1)}, u32[]{:S(2)}, u32[]{:S(2)}) %collective-permute-start.2) | collective-permute-done | bytes 344096 | tf_op jit(solution)/shard_map/ppermute | solution.py:410
  76.1 2.6 %shard_map.138 = (bf16[168,640]{1,0:T(8,128)(2,1)S(1)}, bf16[176,640]{1,0:T(8,128)(2,1)S(1)}, bf16[176,640]{1,0:T(8,128)(2,1)S(1)}, bf16[168,640]{1,0:T(8,128)(2...) custom-call(s32[5]{0:T(128)S(1)} %stack.23.place_ref, bf16[3,224,256]{2,1,0:T(8,128)(2,1)S(1)} %get-tuple-element.34.w0_ref, ...), custom_call_target="tpu_custom_call" | custom-call | tf_op jit(solution)/shard_map/pallas_call | solution.py:395
  78.7 9.8 %collective-permute-start.4 = (bf16[176,640]{1,0:T(8,128)(2,1)S(1)}, bf16[176,640]{1,0:T(8,128)(2,1)S(1)}, u32[]{:S(2)}, u32[]{:S(2)}) collective-permute-start(bf16[176,640]{1,0:T(8,128)(2,1)S(1)} %get-tuple-element.39), channel_id=1, source_target_pairs={{0,4},{4,8},{8,12},{12,0},{16,28},{20,16},{24,20},{28,24},{1,5},{5... | collective-permute-start | bytes 675848 | tf_op jit(solution)/shard_map/ppermute | solution.py:418
  88.4 1.9 collective-permute-start.5
  90.4 13.1 %collective-permute-done.4.b_ref.first_ref = bf16[176,640]{1,0:T(8,128)(2,1)S(1)} collective-permute-done((bf16[176,640]{1,0:T(8,128)(2,1)S(1)}, bf16[176,640]{1,0:T(8,128)(2,1)S(1)}, u32[]{:S(2)}, u32[]{:S(2)}) %collective-permute-start.4) | collective-permute-done | bytes 225312 | tf_op jit(solution)/shard_map/ppermute | solution.py:418
  103.5 8.0 %collective-permute-start.6 = (bf16[176,640]{1,0:T(8,128)(2,1)S(1)}, bf16[176,640]{1,0:T(8,128)(2,1)S(1)}, u32[]{:S(2)}, u32[]{:S(2)}) collective-permute-start(bf16[176,640]{1,0:T(8,128)(2,1)S(1)} %shard_map.139), channel_id=1, source_target_pairs={{0,4},{4,8},{8,12},{12,0},{16,28},{20,16},{24,20},{28,24},{1,5},{5... | collective-permute-start | bytes 675848 | tf_op jit(solution)/shard_map/ppermute | solution.py:418
  111.6 8.6 %collective-permute-done.6.third_ref = bf16[176,640]{1,0:T(8,128)(2,1)S(1)} collective-permute-done((bf16[176,640]{1,0:T(8,128)(2,1)S(1)}, bf16[176,640]{1,0:T(8,128)(2,1)S(1)}, u32[]{:S(2)}, u32[]{:S(2)}) %collective-permute-start.6) | collective-permute-done | bytes 225312 | tf_op jit(solution)/shard_map/ppermute | solution.py:418
  120.2 1.6 shard_map.140
  121.8 30.4 %all-gather = bf16[704,640]{1,0:T(8,128)(2,1)S(1)} all-gather(bf16[176,640]{1,0:T(8,128)(2,1)S(1)} %get-tuple-element.43), channel_id=2, replica_groups=mesh['y'=4,'zl'=4,'core'=2,'zh'=4,'x'=4] {'zh'}, dimensions={0}, use_global_device_ids=true | all-gather | bytes 1126400 | tf_op jit(solution)/shard_map/all_gather | solution.py:487
  153.8 6.4 %collective-permute-start.7 = (bf16[4,328,256]{2,1,0:T(8,128)(2,1)S(1)}, bf16[4,328,256]{2,1,0:T(8,128)(2,1)S(1)}, u32[]{:S(2)}, u32[]{:S(2)}) collective-permute-start(bf16[4,328,256]{2,1,0:T(8,128)(2,1)S(1)} %get-tuple-element.47), channel_id=1, source_target_pairs={{0,16},{16,0},{1,17},{17,1},{2,18},{18,2},{3,19},{19,3},{4,20},{20... | collective-permute-start | bytes 2015240 | tf_op jit(solution)/shard_map/ppermute | solution.py:494
  160.2 1.7 collective-permute-done.7.theirs_ref
  162.9 6.8 %all-to-all-start.2 = ((bf16[4,4,88,256]{3,2,1,0:T(8,128)(2,1)}), bf16[4,4,88,256]{3,2,1,0:T(8,128)(2,1)}, u32[]{:S(2)}, u32[]{:S(2)}) async-start(bf16[4,4,88,256]{3,2,1,0:T(8,128)(2,1)} %copy-done.11), calls=%async_computation.2 | async-start | bytes 1441792 | tf_op jit(solution)/shard_map/all_to_all | solution.py:405
  181.0 2.1 shard_map.144
  183.0 5.9 %all-to-all-start.3 = ((bf16[16,32,256]{2,1,0:T(8,128)(2,1)}), bf16[16,32,256]{2,1,0:T(8,128)(2,1)S(1)}, u32[]{:S(2)}, u32[]{:S(2)}) async-start(bf16[16,32,256]{2,1,0:T(8,128)(2,1)} %bitcast.9), calls=%async_computation.3 | async-start | bytes 524288 | tf_op jit(solution)/shard_map/all_to_all | solution.py:405
  189.0 4.5 %collective-permute-start.8 = (bf16[3,224,256]{2,1,0:T(8,128)(2,1)S(1)}, bf16[3,224,256]{2,1,0:T(8,128)(2,1)S(1)}, u32[]{:S(2)}, u32[]{:S(2)}) collective-permute-start(bf16[3,224,256]{2,1,0:T(8,128)(2,1)S(1)} %copy-done.23), channel_id=1, source_target_pairs={{0,3},{1,0},{2,1},{3,2},{4,7},{5,4},{6,5},{7,6},{8,11},{9,8},{10,9... | collective-permute-start | bytes 1032200 | tf_op jit(solution)/shard_map/ppermute | solution.py:410
  193.5 2.5 %collective-permute-start.9 = (bf16[3,224,256]{2,1,0:T(8,128)(2,1)S(1)}, bf16[3,224,256]{2,1,0:T(8,128)(2,1)S(1)}, u32[]{:S(2)}, u32[]{:S(2)}) collective-permute-start(bf16[3,224,256]{2,1,0:T(8,128)(2,1)S(1)} %copy-done.21), channel_id=1, source_target_pairs={{0,2},{1,3},{2,0},{3,1},{4,6},{5,7},{6,4},{7,5},{8,10},{9,11},{10,... | collective-permute-start | bytes 1032200 | tf_op jit(solution)/shard_map/ppermute | solution.py:410
  196.0 2.5 %collective-permute-start.10 = (bf16[3,224,256]{2,1,0:T(8,128)(2,1)S(1)}, bf16[3,224,256]{2,1,0:T(8,128)(2,1)S(1)}, u32[]{:S(2)}, u32[]{:S(2)}) collective-permute-start(bf16[3,224,256]{2,1,0:T(8,128)(2,1)S(1)} %copy-done.19), channel_id=1, source_target_pairs={{0,1},{1,2},{2,3},{3,0},{4,5},{5,6},{6,7},{7,4},{8,9},{9,10},{10,1... | collective-permute-start | bytes 1032200 | tf_op jit(solution)/shard_map/ppermute | solution.py:410
  198.5 3.9 %collective-permute-done.8.g1_ref = bf16[3,224,256]{2,1,0:T(8,128)(2,1)S(1)} collective-permute-done((bf16[3,224,256]{2,1,0:T(8,128)(2,1)S(1)}, bf16[3,224,256]{2,1,0:T(8,128)(2,1)S(1)}, u32[]{:S(2)}, u32[]{:S(2)}) %collective-permute-start.8) | collective-permute-done | bytes 344096 | tf_op jit(solution)/shard_map/ppermute | solution.py:410
  202.4 2.8 %collective-permute-done.9.g2_ref = bf16[3,224,256]{2,1,0:T(8,128)(2,1)S(1)} collective-permute-done((bf16[3,224,256]{2,1,0:T(8,128)(2,1)S(1)}, bf16[3,224,256]{2,1,0:T(8,128)(2,1)S(1)}, u32[]{:S(2)}, u32[]{:S(2)}) %collective-permute-start.9) | collective-permute-done | bytes 344096 | tf_op jit(solution)/shard_map/ppermute | solution.py:410
  205.2 9.5 %collective-permute-done.10.g3_ref = bf16[3,224,256]{2,1,0:T(8,128)(2,1)S(1)} collective-permute-done((bf16[3,224,256]{2,1,0:T(8,128)(2,1)S(1)}, bf16[3,224,256]{2,1,0:T(8,128)(2,1)S(1)}, u32[]{:S(2)}, u32[]{:S(2)}) %collective-permute-start.10) | collective-permute-done | bytes 344096 | tf_op jit(solution)/shard_map/ppermute | solution.py:410
  214.7 2.3 %shard_map.146 = (f32[256,896]{1,0:T(8,128)}, f32[256,896]{1,0:T(8,128)}) custom-call(s32[5]{0:T(128)S(1)} %stack.23.place_ref, bf16[3,224,256]{2,1,0:T(8,128)(2,1)S(1)} %copy-done.13, bf16[3,224,256]{2,1,0:T(8,128)(2,1)S(1)} %collective-permute-done.8.g1_ref, bf16[3,224,256]{2,1,0:T(8,128)(2,1)S(1)} %collective-permute-done.9.g2_ref, ...), custom_call_target="tpu_custom_call" | custom-call | tf_op jit(solution)/shard_map/pallas_call | solution.py:395
  217.0 1.7 shard_map.145
  (68 shorter events, 15.9 us)
Async XLA Ops:
  2.7 22.0 %all-to-all-start = ((bf16[16,24,512]{2,1,0:T(8,128)(2,1)}), bf16[16,24,512]{2,1,0:T(8,128)(2,1)S(1)}, u32[]{:S(2)}, u32[]{:S(2)}) async-start(bf16[16,24,512]{2,1,0:T(8,128)(2,1)} %bitcast.21), calls=%async_computation | async-start | bytes 786432 | tf_op jit(solution)/shard_map/all_to_all | solution.py:405
  25.4 26.3 %copy-start.2 = (bf16[896,256]{1,0:T(8,128)(2,1)S(1)}, bf16[896,256]{1,0:T(8,128)(2,1)}, u32[]{:S(2)}) copy-start(bf16[896,256]{1,0:T(8,128)(2,1)} %down_hbm.3) | copy-start | bytes 1376260
  25.4 26.3 %copy-start.14 = (bf16[256,896]{1,0:T(8,128)(2,1)S(1)}, bf16[256,896]{1,0:T(8,128)(2,1)}, u32[]{:S(2)}) copy-start(bf16[256,896]{1,0:T(8,128)(2,1)} %gate_hbm.1) | copy-start | bytes 1376260
  25.4 26.3 %copy-start.15 = (bf16[256,896]{1,0:T(8,128)(2,1)S(1)}, bf16[256,896]{1,0:T(8,128)(2,1)}, u32[]{:S(2)}) copy-start(bf16[256,896]{1,0:T(8,128)(2,1)} %up_hbm.1) | copy-start | bytes 1376260
  47.0 29.0 %collective-permute-start.3 = (bf16[4,4,88,512]{3,2,1,0:T(8,128)(2,1)S(1)}, bf16[4,4,88,512]{3,2,1,0:T(8,128)(2,1)S(1)}, u32[]{:S(2)}, u32[]{:S(2)}) collective-permute-start(bf16[4,4,88,512]{3,2,1,0:T(8,128)(2,1)S(1)} %all_to_all.20.own_ref), channel_id=1, source_target_pairs={{0,16},{16,0},{1,17},{17,1},{2,18},{18,2},{3,19},{19,3},{4,20},{20... | collective-permute-start | bytes 4325384 | tf_op jit(solution)/shard_map/ppermute | solution.py:468
  53.7 98.6 %copy-start.3 = (bf16[3,224,256]{2,1,0:T(8,128)(2,1)}, bf16[3,224,256]{2,1,0:T(8,128)(2,1)S(1)}, u32[]{:S(2)}) copy-start(bf16[3,224,256]{2,1,0:T(8,128)(2,1)S(1)} %get-tuple-element.34.w0_ref) | copy-start | bytes 1032196
  53.7 20.1 %collective-permute-start = (bf16[3,224,256]{2,1,0:T(8,128)(2,1)S(1)}, bf16[3,224,256]{2,1,0:T(8,128)(2,1)S(1)}, u32[]{:S(2)}, u32[]{:S(2)}) collective-permute-start(bf16[3,224,256]{2,1,0:T(8,128)(2,1)S(1)} %get-tuple-element.35), channel_id=1, source_target_pairs={{0,1},{1,2},{2,3},{3,0},{4,5},{5,6},{6,7},{7,4},{8,9},{9,10},{10,1... | collective-permute-start | bytes 1032200 | tf_op jit(solution)/shard_map/ppermute | solution.py:410
  55.6 18.2 %collective-permute-start.1 = (bf16[3,224,256]{2,1,0:T(8,128)(2,1)S(1)}, bf16[3,224,256]{2,1,0:T(8,128)(2,1)S(1)}, u32[]{:S(2)}, u32[]{:S(2)}) collective-permute-start(bf16[3,224,256]{2,1,0:T(8,128)(2,1)S(1)} %get-tuple-element.36), channel_id=1, source_target_pairs={{0,2},{1,3},{2,0},{3,1},{4,6},{5,7},{6,4},{7,5},{8,10},{9,11},{10,... | collective-permute-start | bytes 1032200 | tf_op jit(solution)/shard_map/ppermute | solution.py:410
  59.3 16.7 %collective-permute-start.2 = (bf16[3,224,256]{2,1,0:T(8,128)(2,1)S(1)}, bf16[3,224,256]{2,1,0:T(8,128)(2,1)S(1)}, u32[]{:S(2)}, u32[]{:S(2)}) collective-permute-start(bf16[3,224,256]{2,1,0:T(8,128)(2,1)S(1)} %get-tuple-element.37), channel_id=1, source_target_pairs={{0,3},{1,0},{2,1},{3,2},{4,7},{5,4},{6,5},{7,6},{8,11},{9,8},{10,9... | collective-permute-start | bytes 1032200 | tf_op jit(solution)/shard_map/ppermute | solution.py:410
  73.8 78.5 %copy-start.5 = (bf16[3,224,256]{2,1,0:T(8,128)(2,1)}, bf16[3,224,256]{2,1,0:T(8,128)(2,1)S(1)}, u32[]{:S(2)}) copy-start(bf16[3,224,256]{2,1,0:T(8,128)(2,1)S(1)} %collective-permute-done.w1_ref) | copy-start | bytes 1032196
  73.8 78.5 %copy-start.7 = (bf16[3,224,256]{2,1,0:T(8,128)(2,1)}, bf16[3,224,256]{2,1,0:T(8,128)(2,1)S(1)}, u32[]{:S(2)}) copy-start(bf16[3,224,256]{2,1,0:T(8,128)(2,1)S(1)} %collective-permute-done.1.w2_ref) | copy-start | bytes 1032196
  76.0 76.2 %copy-start.9 = (bf16[3,224,256]{2,1,0:T(8,128)(2,1)}, bf16[3,224,256]{2,1,0:T(8,128)(2,1)S(1)}, u32[]{:S(2)}) copy-start(bf16[3,224,256]{2,1,0:T(8,128)(2,1)S(1)} %collective-permute-done.2.w3_ref) | copy-start | bytes 1032196
  76.0 35.5 %copy-start.24 = (f32[896]{0:T(1024)S(1)}, f32[896]{0:T(1024)}, u32[]{:S(2)}) copy-start(f32[896]{0:T(1024)} %param.13) | copy-start | bytes 10756
  76.0 35.5 %copy-start.25 = (f32[896]{0:T(1024)S(1)}, f32[896]{0:T(1024)}, u32[]{:S(2)}) copy-start(f32[896]{0:T(1024)} %param.14) | copy-start | bytes 10756
  78.7 24.8 %collective-permute-start.4 = (bf16[176,640]{1,0:T(8,128)(2,1)S(1)}, bf16[176,640]{1,0:T(8,128)(2,1)S(1)}, u32[]{:S(2)}, u32[]{:S(2)}) collective-permute-start(bf16[176,640]{1,0:T(8,128)(2,1)S(1)} %get-tuple-element.39), channel_id=1, source_target_pairs={{0,4},{4,8},{8,12},{12,0},{16,28},{20,16},{24,20},{28,24},{1,5},{5... | collective-permute-start | bytes 675848 | tf_op jit(solution)/shard_map/ppermute | solution.py:418
  88.4 23.2 %collective-permute-start.5 = (bf16[176,640]{1,0:T(8,128)(2,1)S(1)}, bf16[176,640]{1,0:T(8,128)(2,1)S(1)}, u32[]{:S(2)}, u32[]{:S(2)}) collective-permute-start(bf16[176,640]{1,0:T(8,128)(2,1)S(1)} %get-tuple-element.40), channel_id=1, source_target_pairs={{0,12},{4,0},{8,4},{12,8},{16,20},{20,24},{24,28},{28,16},{1,13},{... | collective-permute-start | bytes 675848 | tf_op jit(solution)/shard_map/ppermute | solution.py:418
  103.5 16.7 %collective-permute-start.6 = (bf16[176,640]{1,0:T(8,128)(2,1)S(1)}, bf16[176,640]{1,0:T(8,128)(2,1)S(1)}, u32[]{:S(2)}, u32[]{:S(2)}) collective-permute-start(bf16[176,640]{1,0:T(8,128)(2,1)S(1)} %shard_map.139), channel_id=1, source_target_pairs={{0,4},{4,8},{8,12},{12,0},{16,28},{20,16},{24,20},{28,24},{1,5},{5... | collective-permute-start | bytes 675848 | tf_op jit(solution)/shard_map/ppermute | solution.py:418
  152.3 1.5 copy-start
  153.8 8.1 %collective-permute-start.7 = (bf16[4,328,256]{2,1,0:T(8,128)(2,1)S(1)}, bf16[4,328,256]{2,1,0:T(8,128)(2,1)S(1)}, u32[]{:S(2)}, u32[]{:S(2)}) collective-permute-start(bf16[4,328,256]{2,1,0:T(8,128)(2,1)S(1)} %get-tuple-element.47), channel_id=1, source_target_pairs={{0,16},{16,0},{1,17},{17,1},{2,18},{18,2},{3,19},{19,3},{4,20},{20... | collective-permute-start | bytes 2015240 | tf_op jit(solution)/shard_map/ppermute | solution.py:494
  162.9 18.0 %all-to-all-start.2 = ((bf16[4,4,88,256]{3,2,1,0:T(8,128)(2,1)}), bf16[4,4,88,256]{3,2,1,0:T(8,128)(2,1)}, u32[]{:S(2)}, u32[]{:S(2)}) async-start(bf16[4,4,88,256]{3,2,1,0:T(8,128)(2,1)} %copy-done.11), calls=%async_computation.2 | async-start | bytes 1441792 | tf_op jit(solution)/shard_map/all_to_all | solution.py:405
  169.8 1.2 copy-start.1
  171.0 1.0 copy-start.4
  180.9 8.1 %copy-start.23 = (bf16[3,224,256]{2,1,0:T(8,128)(2,1)S(1)}, bf16[3,224,256]{2,1,0:T(8,128)(2,1)}, u32[]{:S(2)}) copy-start(bf16[3,224,256]{2,1,0:T(8,128)(2,1)} %copy-done.22) | copy-start | bytes 1032196
  180.9 12.6 %copy-start.21 = (bf16[3,224,256]{2,1,0:T(8,128)(2,1)S(1)}, bf16[3,224,256]{2,1,0:T(8,128)(2,1)}, u32[]{:S(2)}) copy-start(bf16[3,224,256]{2,1,0:T(8,128)(2,1)} %copy-done.20) | copy-start | bytes 1032196
  180.9 15.1 %copy-start.19 = (bf16[3,224,256]{2,1,0:T(8,128)(2,1)S(1)}, bf16[3,224,256]{2,1,0:T(8,128)(2,1)}, u32[]{:S(2)}) copy-start(bf16[3,224,256]{2,1,0:T(8,128)(2,1)} %copy-done.18) | copy-start | bytes 1032196
  180.9 33.7 %copy-start.13 = (bf16[3,224,256]{2,1,0:T(8,128)(2,1)S(1)}, bf16[3,224,256]{2,1,0:T(8,128)(2,1)}, u32[]{:S(2)}) copy-start(bf16[3,224,256]{2,1,0:T(8,128)(2,1)} %copy-done.12) | copy-start | bytes 1032196
  180.9 36.1 %copy-start.16 = (bf16[20,256]{1,0:T(8,128)(2,1)S(1)}, bf16[20,256]{1,0:T(8,128)(2,1)}, u32[]{:S(2)}) copy-start(bf16[20,256]{1,0:T(8,128)(2,1)} %cotangent_ref.1) | copy-start | bytes 30724
  180.9 36.0 %copy-start.17 = (f32[256]{0:T(256)S(1)}, f32[256]{0:T(256)}, u32[]{:S(2)}) copy-start(f32[256]{0:T(256)} %param.15) | copy-start | bytes 3076
  183.0 33.9 %all-to-all-start.3 = ((bf16[16,32,256]{2,1,0:T(8,128)(2,1)}), bf16[16,32,256]{2,1,0:T(8,128)(2,1)S(1)}, u32[]{:S(2)}, u32[]{:S(2)}) async-start(bf16[16,32,256]{2,1,0:T(8,128)(2,1)} %bitcast.9), calls=%async_computation.3 | async-start | bytes 524288 | tf_op jit(solution)/shard_map/all_to_all | solution.py:405
  189.0 13.3 %collective-permute-start.8 = (bf16[3,224,256]{2,1,0:T(8,128)(2,1)S(1)}, bf16[3,224,256]{2,1,0:T(8,128)(2,1)S(1)}, u32[]{:S(2)}, u32[]{:S(2)}) collective-permute-start(bf16[3,224,256]{2,1,0:T(8,128)(2,1)S(1)} %copy-done.23), channel_id=1, source_target_pairs={{0,3},{1,0},{2,1},{3,2},{4,7},{5,4},{6,5},{7,6},{8,11},{9,8},{10,9... | collective-permute-start | bytes 1032200 | tf_op jit(solution)/shard_map/ppermute | solution.py:410
  193.5 11.7 %collective-permute-start.9 = (bf16[3,224,256]{2,1,0:T(8,128)(2,1)S(1)}, bf16[3,224,256]{2,1,0:T(8,128)(2,1)S(1)}, u32[]{:S(2)}, u32[]{:S(2)}) collective-permute-start(bf16[3,224,256]{2,1,0:T(8,128)(2,1)S(1)} %copy-done.21), channel_id=1, source_target_pairs={{0,2},{1,3},{2,0},{3,1},{4,6},{5,7},{6,4},{7,5},{8,10},{9,11},{10,... | collective-permute-start | bytes 1032200 | tf_op jit(solution)/shard_map/ppermute | solution.py:410
  196.0 18.7 %collective-permute-start.10 = (bf16[3,224,256]{2,1,0:T(8,128)(2,1)S(1)}, bf16[3,224,256]{2,1,0:T(8,128)(2,1)S(1)}, u32[]{:S(2)}, u32[]{:S(2)}) collective-permute-start(bf16[3,224,256]{2,1,0:T(8,128)(2,1)S(1)} %copy-done.19), channel_id=1, source_target_pairs={{0,1},{1,2},{2,3},{3,0},{4,5},{5,6},{6,7},{7,4},{8,9},{9,10},{10,1... | collective-permute-start | bytes 1032200 | tf_op jit(solution)/shard_map/ppermute | solution.py:410
  (8 other events, 6.7 us)

commit v5 on v4

--- a/solution.py
+++ b/solution.py
@@ -125,12 +125,10 @@
                 out_ref[y, j, :, a : a + width] = block
 
 
-def whole(own_ref, other_ref, j, at):
-    rows = own_ref.shape[2] - 8
-    width = own_ref.shape[3] // 2
-    halves = [
-        ref[:, j, 0:rows, at * width : (at + 1) * width].reshape(-1, width) for ref in (own_ref, other_ref)
-    ]
+def whole(token_refs, j, at):
+    rows = token_refs[0].shape[2] - 8
+    width = token_refs[0].shape[3] // 2
+    halves = [ref[:, j, 0:rows, at * width : (at + 1) * width].reshape(-1, width) for ref in token_refs]
     return jnp.concatenate(halves, axis=0)
 
 
@@ -142,15 +140,16 @@
 
 
 def forward(
-    tall_count, place_ref, w0_ref, w1_ref, w2_ref, w3_ref, own_ref, other_ref,
-    kept_ref, first_ref, second_ref, third_ref, rows_ref, news_ref, store_ref,
+    tall_count, place_ref, w0_ref, w1_ref, w2_ref, w3_ref, *refs
 ):
+    token_refs = refs[:2]
+    kept_ref, first_ref, second_ref, third_ref, rows_ref, news_ref, store_ref = refs[2:]
     w_ref = (w0_ref, w1_ref, w2_ref, w3_ref)
     blocks = len(w_ref)
     _, share, width = w0_ref.shape
     parts = store_ref.shape[0]
     tall = share // parts
-    lefts = [whole(own_ref, other_ref, j, 0) for j in range(blocks)]
+    lefts = [whole(token_refs, j, 0) for j in range(blocks)]
     ones = jnp.ones((8, width), bf16)
     row = sum(nt(ones, left) for left in lefts)[0:1]
     levels = []
@@ -166,10 +165,10 @@
     lines = [p.astype(f32) for line in lines for p in pieces(line)[0:2]]
     news_ref[...] = jnp.concatenate([*lines, jnp.zeros((2, row.shape[1]), f32)], axis=0).astype(bf16)
     total = 0.0
-    rows = own_ref.shape[2] - 8
+    rows = token_refs[0].shape[2] - 8
     for j in range(blocks):
         lots = [
-            ref[y, j, rows : rows + 8, :].astype(f32) for ref in (own_ref, other_ref) for y in range(own_ref.shape[0])
+            ref[y, j, rows : rows + 8, :].astype(f32) for ref in token_refs for y in range(token_refs[0].shape[0])
         ]
         mean, square = merged([(joined(lot[:, 0:width]), joined(lot[:, width:])) for lot in lots], tall_count)
         scale = lax.rsqrt(square + epsilon)
@@ -177,7 +176,7 @@
         gs = gain * scale
         rows_ref[j] = jnp.concatenate([mean, gs, scale, jnp.zeros((5, width), f32)], axis=0)
         hat = ((w_ref[j][2].astype(f32) - mean) * gs).astype(bf16)
-        total = total + nt(hat, whole(own_ref, other_ref, j, 1))
+        total = total + nt(hat, whole(token_refs, j, 1))
     total = total.astype(bf16)
     for q in range(parts):
         store_ref[q, 2 * tall : 3 * tall, :] = total[q * tall : (q + 1) * tall]
@@ -206,24 +205,24 @@
     rows = [n[0:1] + n[1:2] for n in news]
     row = sum(rows)
     row_ref[...] = jnp.broadcast_to(row, row_ref.shape)
-    lane = lax.broadcasted_iota(jnp.int32, cols_ref.shape, 1)
-    cols = jnp.zeros(cols_ref.shape, f32)
+    wide = 256
+    lines = [None] * 16
     for at in range(2):
         both = [n[2 * at + 2 : 2 * at + 3] + n[2 * at + 3 : 2 * at + 4] for n in news]
-        moments = [(b[:, 0:256], b[:, 256:512]) for b in both]
+        moments = [(b[:, 0:wide], b[:, wide : 2 * wide]) for b in both]
         mean, square = merged(moments, wide_count)
         gains = (gate_gain_ref, up_gain_ref)[at]
         gain = sum(
             jnp.where(place_ref[1] == j, gains[:, j * share : (j + 1) * share], 0.0)
             for j in range(gains.shape[1] // share)
         )
-        scale = upright(lax.rsqrt(square + epsilon), share)
-        gain = upright(gain, share)
-        found = [(3 * at, upright(mean, share)), (3 * at + 1, gain * scale), (3 * at + 2, scale), (6 + at, gain)]
-        found += [(8 + 4 * at + q, upright(m, share)) for q, (m, _) in enumerate(moments)]
-        for k, v in found:
-            cols = jnp.where(lane == k, v, cols)
-    cols_ref[...] = cols
+        gain = jnp.concatenate([gain, jnp.zeros((1, wide - share), f32)], axis=1)
+        scale = lax.rsqrt(square + epsilon)
+        lines[3 * at : 3 * at + 3] = [mean, gain * scale, scale]
+        lines[6 + at] = gain
+        lines[8 + 4 * at : 12 + 4 * at] = [m for m, _ in moments]
+    lines.append(jnp.zeros((cols_ref.shape[1] - 16, wide), f32))
+    cols_ref[...] = jnp.concatenate(lines, axis=0).T[0:share]
     mine = cols_ref[pl.ds(pl.multiple_of(place_ref[0] * tall, 8), tall), :]
     total = kept_ref[...].astype(f32) + second_ref[0:high, :].astype(f32) + third_ref[0:high, :].astype(f32)
     sums = []
@@ -257,46 +256,46 @@
     )
 
 
-def weight_grads(
-    width_all, d_ref, w0_ref, w1_ref, w2_ref, w3_ref, own_ref, other_ref, cols_ref, row_ref,
-    g0_ref, g1_ref, g2_ref, g3_ref, dots_ref,
-):
+def weight_grads(width_all, d_ref, w0_ref, w1_ref, w2_ref, w3_ref, *refs):
+    token_refs = refs[:2]
+    cols_ref, row_ref, *grad_ref = refs[2:]
     w_ref = (w0_ref, w1_ref, w2_ref, w3_ref)
     blocks = len(w_ref)
-    _, share, _ = w0_ref.shape
-    grad_ref = (g0_ref, g1_ref, g2_ref, g3_ref)
+    _, share, width = w0_ref.shape
     parts = d_ref.shape[0]
     tall = share // parts
     streams = [stacked(d_ref, at, tall) for at in range(3)]
     extra = [d_ref[q, 3 * tall : 3 * tall + 8, :].astype(f32) for q in range(parts)]
     row = row_ref[0:1, :]
-    dots_ref[...] = jnp.zeros(dots_ref.shape, f32)
-    means, pulls = [], []
+    means, pulls, dots = [], [], []
     for at in range(2):
         means.append(jnp.sum(streams[at].astype(f32) * row, axis=1, keepdims=True) * (1.0 / width_all))
         dot = jnp.concatenate(
             [upright(joined(e[0:3, 128 * at : 128 * (at + 1)]), tall) for e in extra], axis=0
         )
-        dots_ref[at : at + 1, :] = level(dot / cols_ref[:, 6 + at : 7 + at], dots_ref.shape[1])
+        dots.append(level(dot / cols_ref[:, 6 + at : 7 + at], width))
         s = cols_ref[:, 3 * at + 2 : 3 * at + 3]
         pulls.append(s * s * dot)
-    for j in range(blocks):
-        left = whole(own_ref, other_ref, j, 0)
+    dots = [*spread(jnp.concatenate(dots, axis=0)), jnp.zeros((2, width), f32)]
+    dots = jnp.concatenate(dots, axis=0).astype(bf16)
+    for j in range(blocks):
+        left = whole(token_refs, j, 0)
         for at in range(2):
             p = nn(streams[at], left)
             cent = w_ref[j][at].astype(f32) - cols_ref[:, 3 * at : 3 * at + 1]
             grad = cols_ref[:, 3 * at + 1 : 3 * at + 2] * (p - means[at]) - cent * pulls[at]
-            grad_ref[j][at] = grad.astype(bf16)
-        grad_ref[j][2] = nn(streams[2], whole(own_ref, other_ref, j, 1)).astype(bf16)
+            grad_ref[j][at * share : (at + 1) * share, :] = grad.astype(bf16)
+        grad_ref[j][2 * share : 3 * share, :] = nn(streams[2], whole(token_refs, j, 1)).astype(bf16)
+        grad_ref[j][3 * share :, :] = dots
 
 
 def spread(sums):
     return [p.astype(f32) for k in range(2) for p in pieces(sums[k : k + 1, :])]
 
 
-def token_back(
-    d_ref, w0_ref, w1_ref, w2_ref, w3_ref, own_ref, other_ref, cols_ref, rows_ref, mine_ref, theirs_ref, sums_ref
-):
+def token_back(d_ref, w0_ref, w1_ref, w2_ref, w3_ref, *refs):
+    token_refs = refs[:2]
+    cols_ref, rows_ref, mine_ref, theirs_ref, sums_ref = refs[2:]
     w_ref = (w0_ref, w1_ref, w2_ref, w3_ref)
     blocks = len(w_ref)
     _, share, width = w0_ref.shape
@@ -310,7 +309,7 @@
             cent = w_ref[j][at].astype(f32) - cols_ref[:, 3 * at : 3 * at + 1]
             back = back + nn(streams[at], (cent * cols_ref[:, 3 * at + 1 : 3 * at + 2]).astype(bf16))
         mine_ref[j] = back[:half]
-        p = nn(hidden, whole(own_ref, other_ref, j, 1))
+        p = nn(hidden, whole(token_refs, j, 1))
         cent = w_ref[j][2].astype(f32) - rows_ref[j, 0:1, :]
         summed = jnp.sum(p, axis=0, keepdims=True)
         crossed = jnp.sum(p * cent, axis=0, keepdims=True)
@@ -335,27 +334,27 @@
             out_ref[k, j, rows : rows + 8, :] = extra
 
 
-def whole_column(place_ref, in_ref, dots_ref, out_ref):
+def whole_column(place_ref, in_ref, out_ref):
     lines, blocks, high, _ = in_ref.shape
-    dots = spread(dots_ref[...])
     cuts = out_ref.shape[0]
     rows = (high - 8) // cuts
     for j in range(blocks):
         lots = [in_ref[y, j].astype(f32) for y in range(lines)]
         back = sum(lot[0 : high - 8] for lot in lots)
         total = [sum(joined(lot[high - 8 + 3 * k : high - 5 + 3 * k]) for lot in lots) for k in range(2)]
-        extra = spread(jnp.concatenate(total, axis=0))
+        extra = [p.astype(f32) for t in total for p in pieces(t)[0:2]]
         for l in range(cuts):
             out_ref[l, lax.rem(place_ref[1] + blocks - j, blocks)] = jnp.concatenate(
-                [back[l * rows : (l + 1) * rows], *extra, *dots], axis=0
+                [back[l * rows : (l + 1) * rows], *extra], axis=0
             ).astype(bf16)
 
 
 def finish_wide(place_ref, g0_ref, g1_ref, g2_ref, g3_ref, gate_ref, up_ref, store_ref):
     g_ref = (g0_ref, g1_ref, g2_ref, g3_ref)
+    share = store_ref.shape[1]
     for at, ref in enumerate((gate_ref, up_ref)):
         for k, g in enumerate(g_ref):
-            store_ref[lax.rem(place_ref[1] + k, len(g_ref))] = g[at].astype(f32)
+            store_ref[lax.rem(place_ref[1] + k, len(g_ref))] = g[at * share : (at + 1) * share, :].astype(f32)
         ref[...] = store_ref[...].reshape(-1, store_ref.shape[2]).T
 
 
@@ -363,26 +362,25 @@
     hidden_all, place_ref, in_ref, cotangent_ref, g0_ref, g1_ref, g2_ref, g3_ref, down_ref, rows_ref, gain_ref,
     tokens_ref, grad_ref, dgain_ref, dots_ref,
 ):
-    lines, blocks, _, _ = in_ref.shape
+    lines, blocks, _, width = in_ref.shape
     rows = tokens_ref.shape[0]
     lots = [in_ref[l, j].astype(f32) for l in range(lines) for j in range(blocks)]
     total = sum(lots)
     tokens_ref[...] = cotangent_ref[...].astype(f32) + total[0:rows]
-    summed, crossed = (sum(joined(lot[rows + 3 * k : rows + 3 * k + 3]) for lot in lots) for k in range(2))
-    line = place_ref[2]
-    for j in range(blocks):
-        own = in_ref[line, j].astype(f32)
-        dots_ref[0:1, j, :] = joined(own[rows + 6 : rows + 9])
-        dots_ref[1:2, j, :] = joined(own[rows + 9 : rows + 12])
+    summed = total[rows : rows + 1] + total[rows + 1 : rows + 2]
+    crossed = total[rows + 2 : rows + 3] + total[rows + 3 : rows + 4]
     mine = rows_ref[0]
     mean, scale = mine[0:1, :], mine[2:3, :]
     gain = gain_ref[...]
     dgain_ref[...] = scale * crossed
     g_ref = (g0_ref, g1_ref, g2_ref, g3_ref)
+    share = down_ref.shape[1]
     for k, g in enumerate(g_ref):
         j = lax.rem(place_ref[1] + k, len(g_ref))
+        dots = g[3 * share :, :].astype(f32)
+        dots_ref[j] = jnp.concatenate([joined(dots[0:3]), joined(dots[3:6]), jnp.zeros((6, width), f32)], axis=0)
         cent = down_ref[j].astype(f32) - mean
-        grad_ref[j] = scale * gain * (g[2].astype(f32) - summed * (1.0 / hidden_all)) - (
+        grad_ref[j] = scale * gain * (g[2 * share : 3 * share, :].astype(f32) - summed * (1.0 / hidden_all)) - (
             scale * scale * scale * gain * crossed
         ) * cent
 
@@ -412,10 +410,13 @@
 
 def apart(x, axis, by):
     size = lax.axis_size(axis)
-    pairs = [
-        (core * size + i, core * size + (i + (by if core == 0 else -by)) % size) for core in (0, 1) for i in range(size)
-    ]
-    return lax.ppermute(x, ("core", axis), pairs)
+    outer = axis in BLK
+
+    def spot(core, i):
+        return i % size * 2 + core if outer else core * size + i % size
+
+    pairs = [(spot(core, i), spot(core, i + by * (1 - 2 * core))) for core in (0, 1) for i in range(size)]
+    return lax.ppermute(x, (axis, "core") if outer else ("core", axis), pairs)
 
 
 def block(tokens, cotangent, gate_weight, up_weight, down_weight, gate_gain, up_gain, down_gain):
@@ -458,9 +459,9 @@
             pltpu.SemaphoreType.DMA((3,)),
         ],
     )
-    weights = [cut_weights[0]]
-    for k in (1, 2, 3):
-        weights.append(shift(cut_weights[k], "x", k))
+    weights = [cut_weights[0], None, None, None]
+    for k in (2, 1, 3):
+        weights[k] = shift(cut_weights[k], "x", k)
     (both,) = call(
         functools.partial(repack_tokens, hidden), [((ny, nx, nl * rows + 8, 2 * width), bf16)], both, place=place
     )
@@ -492,8 +493,8 @@
         d, *weights, own, other, cols, rows_of,
     )
     theirs = lax.ppermute(theirs, "core", swap)
-    *grads, dots = call(
-        functools.partial(weight_grads, width_all), [((3, share, width), bf16)] * nx + [((8, width), f32)],
+    grads = call(
+        functools.partial(weight_grads, width_all), [((3 * share + 8, width), bf16)] * nx,
         d, *weights, own, other, cols, row,
     )
     (back,) = call(both_cores, [((ny, nx, nl * rows + 8, width), bf16)], mine, theirs, sums)
@@ -501,25 +502,24 @@
     met = [grads[0], None, None, None]
     for k in (2, 1, 3):
         met[k] = shift(grads[k], "x", -k)
-    (back,) = call(whole_column, [((nl, nx, rows + 12, width), bf16)], back, dots, place=place)
+    (back,) = call(whole_column, [((nl, nx, rows + 4, width), bf16)], back, place=place)
     back = grid_exchange(back, ("zl", "x"))
     grad_gate, grad_up = call(finish_wide, [((width, hidden), f32), ((width, hidden), f32)], *met,
         place=place, scratch=[pltpu.VMEM((nx, share, width), f32)],
     )
     grad_tokens, grad_down, down_dgain, dots = call(
         functools.partial(finish_tall, hidden_all),
-        [((rows, width), f32), ((nx, share, width), f32), ((1, width), f32), ((2, nx, width), f32)],
+        [((rows, width), f32), ((nx, share, width), f32), ((1, width), f32), ((nx, 8, width), f32)],
         back, cotangent, *met, down_weight.reshape(nx, share, width), rows_of, down_gain.reshape(1, width),
         place=place,
     )
-    dots = dots[:, :, :share].reshape(2, hidden)
     return (
         grad_tokens,
         grad_gate,
         grad_up,
         grad_down.reshape(hidden, width),
-        dots[0],
-        dots[1],
+        dots[:, 0, :share].reshape(hidden),
+        dots[:, 1, :share].reshape(hidden),
         down_dgain.reshape(width),
     )
 

time: 221 us -> 227 us (1.027)
  blocking collectives: 52 us -> 68.4 us
  starting transfers between devices: 70.5 us -> 62.5 us
    all_to_all x1 -> x2, blocking collectives: 21.6 us -> 35 us  [exchange(): return lax.all_to_all(x, axis, split_axis=0, concat_axis=0, tiled=True)]
    all_to_all x3 -> x2, starting transfers between devices: 21.8 us -> 13 us  [exchange(): return lax.all_to_all(x, axis, split_axis=0, concat_axis=0, tiled=True)]
    all_gather x1, blocking collectives: 30.4 us -> 33.4 us  [block(): d = lax.all_gather(d, 'zh')]
    all_to_all x3 -> x2, waiting for transfers between devices: 14.4 us -> 12.9 us  [exchange(): return lax.all_to_all(x, axis, split_axis=0, concat_axis=0, tiled=True)]
  transfers between devices with their start and end apart: 14 -> 13, of which waited for: 10 -> 9; matrix products, arithmetic and copies ran while one was open for 0% -> 0% of each run, Pallas kernels for 3% -> 3%
where the time goes in v5:
time: 227 us; the launch traced here: 226 us
  blocking collectives  68.4 us (30%)
  waiting for transfers between devices  65.8 us (29%)
  starting transfers between devices  62.5 us (28%)
  Pallas kernels  16.5 us (7%)
  local copies, waits for them, and re-layouts  12.1 us (5%)
    all_to_all x2, blocking collectives, exchange(): return lax.all_to_all(x, axis, split_axis=0, concat_axis=0, tiled=True)  35 us
    all_gather x1, blocking collectives, block(): d = lax.all_gather(d, 'zh')  33.4 us
    ppermute x6, waiting for transfers between devices, shift(): return lax.ppermute(x, axis, [(i, (i + by) % size) for i in range(size)])  29.6 us
    ppermute x3, waiting for transfers between devices, apart(): return lax.ppermute(x, (axis, 'core') if outer else ('core', axis), pairs)  21.7 us
    ppermute x3, starting transfers between devices, apart(): return lax.ppermute(x, (axis, 'core') if outer else ('core', axis), pairs)  19.7 us
    ppermute x6, starting transfers between devices, shift(): return lax.ppermute(x, axis, [(i, (i + by) % size) for i in range(size)])  17.9 us
    pallas_call x12, Pallas kernels, call(): pl.pallas_call(body, out_shape=[jax.ShapeDtypeStruct(s, t) for s, t in ou...  16.5 us
    all_to_all x2, starting transfers between devices, exchange(): return lax.all_to_all(x, axis, split_axis=0, concat_axis=0, tiled=True)  13 us
  transfers between devices with their start and end apart: 13, of which 9 were waited for; matrix products, arithmetic and copies ran while one was open for 0% of the time, Pallas kernels for 3%

profile of v5, /device:TPU:1, one launch (start us, length us, event | category | flops | bytes accessed | tf_op | source)
XLA Modules:
  0.0 226.3 jit_solution(6257598460087452946)
XLA Ops:
  0.6 2.1 shard_map.136
  2.7 9.0 %all-to-all-start = ((bf16[16,24,512]{2,1,0:T(8,128)(2,1)}), bf16[16,24,512]{2,1,0:T(8,128)(2,1)S(1)}, u32[]{:S(2)}, u32[]{:S(2)}) async-start(bf16[16,24,512]{2,1,0:T(8,128)(2,1)} %bitcast.22), calls=%async_computation | async-start | bytes 786432 | tf_op jit(solution)/shard_map/all_to_all | solution.py:403
  11.8 12.9 %all-to-all-done = bf16[16,24,512]{2,1,0:T(8,128)(2,1)S(1)} async-done(((bf16[16,24,512]{2,1,0:T(8,128)(2,1)}), bf16[16,24,512]{2,1,0:T(8,128)(2,1)S(1)}, u32[]{:S(2)}, u32[]{:S(2)}) %all-to-all-start) | async-done | bytes 393248 | tf_op jit(solution)/shard_map/all_to_all | solution.py:403
  25.5 21.6 %all_to_all.20.refs_0_ = bf16[4,4,88,512]{3,2,1,0:T(8,128)(2,1)S(1)} all-to-all(bf16[4,4,88,512]{3,2,1,0:T(8,128)(2,1)S(1)} %shard_map.137), channel_id=1, replica_groups=mesh['y'=4,'zl'=4,'core'=2,'zh'=4,'x'=4] {'y'}, dimensions={0} | all-to-all | bytes 2883584 | tf_op jit(solution)/shard_map/all_to_all | solution.py:403
  47.0 4.7 %collective-permute-start.3 = (bf16[4,4,88,512]{3,2,1,0:T(8,128)(2,1)S(1)}, bf16[4,4,88,512]{3,2,1,0:T(8,128)(2,1)S(1)}, u32[]{:S(2)}, u32[]{:S(2)}) collective-permute-start(bf16[4,4,88,512]{3,2,1,0:T(8,128)(2,1)S(1)} %all_to_all.20.refs_0_), channel_id=1, source_target_pairs={{0,16},{16,0},{1,17},{17,1},{2,18},{18,2},{3,19},{19,3},{4,20},{20... | collective-permute-start | bytes 4325384 | tf_op jit(solution)/shard_map/ppermute | solution.py:469
  51.8 1.9 shard_map.135
  53.7 1.9 collective-permute-start
  55.6 3.7 %collective-permute-start.1 = (bf16[3,224,256]{2,1,0:T(8,128)(2,1)S(1)}, bf16[3,224,256]{2,1,0:T(8,128)(2,1)S(1)}, u32[]{:S(2)}, u32[]{:S(2)}) collective-permute-start(bf16[3,224,256]{2,1,0:T(8,128)(2,1)S(1)} %get-tuple-element.35), channel_id=1, source_target_pairs={{0,2},{1,3},{2,0},{3,1},{4,6},{5,7},{6,4},{7,5},{8,10},{9,11},{10,... | collective-permute-start | bytes 1032200 | tf_op jit(solution)/shard_map/ppermute | solution.py:408
  59.3 2.8 %collective-permute-start.2 = (bf16[3,224,256]{2,1,0:T(8,128)(2,1)S(1)}, bf16[3,224,256]{2,1,0:T(8,128)(2,1)S(1)}, u32[]{:S(2)}, u32[]{:S(2)}) collective-permute-start(bf16[3,224,256]{2,1,0:T(8,128)(2,1)S(1)} %get-tuple-element.36), channel_id=1, source_target_pairs={{0,3},{1,0},{2,1},{3,2},{4,7},{5,4},{6,5},{7,6},{8,11},{9,8},{10,9... | collective-permute-start | bytes 1032200 | tf_op jit(solution)/shard_map/ppermute | solution.py:408
  62.1 11.6 %collective-permute-done.w1_ref = bf16[3,224,256]{2,1,0:T(8,128)(2,1)S(1)} collective-permute-done((bf16[3,224,256]{2,1,0:T(8,128)(2,1)S(1)}, bf16[3,224,256]{2,1,0:T(8,128)(2,1)S(1)}, u32[]{:S(2)}, u32[]{:S(2)}) %collective-permute-start) | collective-permute-done | bytes 344096 | tf_op jit(solution)/shard_map/ppermute | solution.py:408
  73.8 2.2 collective-permute-done.2.w3_ref
  76.1 2.7 %shard_map.138 = (bf16[168,640]{1,0:T(8,128)(2,1)S(1)}, bf16[176,640]{1,0:T(8,128)(2,1)S(1)}, bf16[176,640]{1,0:T(8,128)(2,1)S(1)}, bf16[168,640]{1,0:T(8,128)(2...) custom-call(s32[5]{0:T(128)S(1)} %stack.23.place_ref, bf16[3,224,256]{2,1,0:T(8,128)(2,1)S(1)} %get-tuple-element.33.w0_ref, ...), custom_call_target="tpu_custom_call" | custom-call | tf_op jit(solution)/shard_map/pallas_call | solution.py:393
  78.7 9.8 %collective-permute-start.4 = (bf16[176,640]{1,0:T(8,128)(2,1)S(1)}, bf16[176,640]{1,0:T(8,128)(2,1)S(1)}, u32[]{:S(2)}, u32[]{:S(2)}) collective-permute-start(bf16[176,640]{1,0:T(8,128)(2,1)S(1)} %get-tuple-element.38), channel_id=1, source_target_pairs={{0,4},{4,8},{8,12},{12,0},{16,28},{20,16},{24,20},{28,24},{1,5},{5... | collective-permute-start | bytes 675848 | tf_op jit(solution)/shard_map/ppermute | solution.py:419
  88.5 1.9 collective-permute-start.5
  90.4 13.1 %collective-permute-done.4.b_ref.first_ref = bf16[176,640]{1,0:T(8,128)(2,1)S(1)} collective-permute-done((bf16[176,640]{1,0:T(8,128)(2,1)S(1)}, bf16[176,640]{1,0:T(8,128)(2,1)S(1)}, u32[]{:S(2)}, u32[]{:S(2)}) %collective-permute-start.4) | collective-permute-done | bytes 225312 | tf_op jit(solution)/shard_map/ppermute | solution.py:419
  103.6 8.0 %collective-permute-start.6 = (bf16[176,640]{1,0:T(8,128)(2,1)S(1)}, bf16[176,640]{1,0:T(8,128)(2,1)S(1)}, u32[]{:S(2)}, u32[]{:S(2)}) collective-permute-start(bf16[176,640]{1,0:T(8,128)(2,1)S(1)} %shard_map.139), channel_id=1, source_target_pairs={{0,4},{4,8},{8,12},{12,0},{16,28},{20,16},{24,20},{28,24},{1,5},{5... | collective-permute-start | bytes 675848 | tf_op jit(solution)/shard_map/ppermute | solution.py:419
  111.7 8.6 %collective-permute-done.6.third_ref = bf16[176,640]{1,0:T(8,128)(2,1)S(1)} collective-permute-done((bf16[176,640]{1,0:T(8,128)(2,1)S(1)}, bf16[176,640]{1,0:T(8,128)(2,1)S(1)}, u32[]{:S(2)}, u32[]{:S(2)}) %collective-permute-start.6) | collective-permute-done | bytes 225312 | tf_op jit(solution)/shard_map/ppermute | solution.py:419
  121.4 33.4 %all-gather = bf16[704,640]{1,0:T(8,128)(2,1)S(1)} all-gather(bf16[176,640]{1,0:T(8,128)(2,1)S(1)} %get-tuple-element.42), channel_id=2, replica_groups=mesh['y'=4,'zl'=4,'core'=2,'zh'=4,'x'=4] {'zh'}, dimensions={0}, use_global_device_ids=true | all-gather | bytes 1126400 | tf_op jit(solution)/shard_map/all_gather | solution.py:488
  154.8 1.5 shard_map.141
  156.4 7.2 %collective-permute-start.7 = (bf16[4,328,256]{2,1,0:T(8,128)(2,1)S(1)}, bf16[4,328,256]{2,1,0:T(8,128)(2,1)S(1)}, u32[]{:S(2)}, u32[]{:S(2)}) collective-permute-start(bf16[4,328,256]{2,1,0:T(8,128)(2,1)S(1)} %get-tuple-element.46), channel_id=1, source_target_pairs={{0,16},{16,0},{1,17},{17,1},{2,18},{18,2},{3,19},{19,3},{4,20},{20... | collective-permute-start | bytes 2015240 | tf_op jit(solution)/shard_map/ppermute | solution.py:495
  163.6 1.7 collective-permute-done.7.theirs_ref
  165.5 13.4 %all_to_all.21.in_ref = bf16[4,4,88,256]{3,2,1,0:T(8,128)(2,1)S(1)} all-to-all(bf16[4,4,88,256]{3,2,1,0:T(8,128)(2,1)S(1)} %shard_map.142), channel_id=1, replica_groups=mesh['y'=4,'zl'=4,'core'=2,'zh'=4,'x'=4] {'y'}, dimensions={0} | all-to-all | bytes 1441792 | tf_op jit(solution)/shard_map/all_to_all | solution.py:403
  180.3 4.0 %all-to-all-start.3 = ((bf16[16,24,256]{2,1,0:T(8,128)(2,1)}), bf16[16,24,256]{2,1,0:T(8,128)(2,1)S(1)}, u32[]{:S(2)}, u32[]{:S(2)}) async-start(bf16[16,24,256]{2,1,0:T(8,128)(2,1)} %bitcast.19), calls=%async_computation.3 | async-start | bytes 393216 | tf_op jit(solution)/shard_map/all_to_all | solution.py:403
  184.3 1.2 copy-done.1
  191.0 1.6 shard_map.144
  192.5 4.5 %collective-permute-start.8 = (bf16[680,256]{1,0:T(8,128)(2,1)S(1)}, bf16[680,256]{1,0:T(8,128)(2,1)S(1)}, u32[]{:S(2)}, u32[]{:S(2)}) collective-permute-start(bf16[680,256]{1,0:T(8,128)(2,1)S(1)} %get-tuple-element.50), channel_id=1, source_target_pairs={{0,3},{1,0},{2,1},{3,2},{4,7},{5,4},{6,5},{7,6},{8,11},{9,8},{10,9... | collective-permute-start | bytes 1044488 | tf_op jit(solution)/shard_map/ppermute | solution.py:408
  197.0 2.5 %collective-permute-start.9 = (bf16[680,256]{1,0:T(8,128)(2,1)S(1)}, bf16[680,256]{1,0:T(8,128)(2,1)S(1)}, u32[]{:S(2)}, u32[]{:S(2)}) collective-permute-start(bf16[680,256]{1,0:T(8,128)(2,1)S(1)} %get-tuple-element.51), channel_id=1, source_target_pairs={{0,2},{1,3},{2,0},{3,1},{4,6},{5,7},{6,4},{7,5},{8,10},{9,11},{10,... | collective-permute-start | bytes 1044488 | tf_op jit(solution)/shard_map/ppermute | solution.py:408
  199.5 2.5 %collective-permute-start.10 = (bf16[680,256]{1,0:T(8,128)(2,1)S(1)}, bf16[680,256]{1,0:T(8,128)(2,1)S(1)}, u32[]{:S(2)}, u32[]{:S(2)}) collective-permute-start(bf16[680,256]{1,0:T(8,128)(2,1)S(1)} %get-tuple-element.52), channel_id=1, source_target_pairs={{0,1},{1,2},{2,3},{3,0},{4,5},{5,6},{6,7},{7,4},{8,9},{9,10},{10,1... | collective-permute-start | bytes 1044488 | tf_op jit(solution)/shard_map/ppermute | solution.py:408
  203.1 4.8 %collective-permute-done.9.g2_ref = bf16[680,256]{1,0:T(8,128)(2,1)S(1)} collective-permute-done((bf16[680,256]{1,0:T(8,128)(2,1)S(1)}, bf16[680,256]{1,0:T(8,128)(2,1)S(1)}, u32[]{:S(2)}, u32[]{:S(2)}) %collective-permute-start.9) | collective-permute-done | bytes 348192 | tf_op jit(solution)/shard_map/ppermute | solution.py:408
  207.8 9.9 %collective-permute-done.10.g3_ref = bf16[680,256]{1,0:T(8,128)(2,1)S(1)} collective-permute-done((bf16[680,256]{1,0:T(8,128)(2,1)S(1)}, bf16[680,256]{1,0:T(8,128)(2,1)S(1)}, u32[]{:S(2)}, u32[]{:S(2)}) %collective-permute-start.10) | collective-permute-done | bytes 348192 | tf_op jit(solution)/shard_map/ppermute | solution.py:408
  217.7 2.3 %shard_map.146 = (f32[256,896]{1,0:T(8,128)}, f32[256,896]{1,0:T(8,128)}) custom-call(s32[5]{0:T(128)S(1)} %stack.23.place_ref, bf16[680,256]{1,0:T(8,128)(2,1)S(1)} %get-tuple-element.49.g0_ref, bf16[680,256]{1,0:T(8,128)(2,1)S(1)} %collective-permute-done.8.g1_ref, bf16[680,256]{1,0:T(8,128)(2,1)S(1)} %collective-permute-done.9.g2_ref, ...), custom_call_target="tpu_custom_call" | custom-call | tf_op jit(solution)/shard_map/pallas_call | solution.py:393
  223.2 1.7 shard_map.145
  (67 shorter events, 14.7 us)
Async XLA Ops:
  2.7 22.0 %all-to-all-start = ((bf16[16,24,512]{2,1,0:T(8,128)(2,1)}), bf16[16,24,512]{2,1,0:T(8,128)(2,1)S(1)}, u32[]{:S(2)}, u32[]{:S(2)}) async-start(bf16[16,24,512]{2,1,0:T(8,128)(2,1)} %bitcast.22), calls=%async_computation | async-start | bytes 786432 | tf_op jit(solution)/shard_map/all_to_all | solution.py:403
  25.4 26.3 %copy-start.2 = (bf16[896,256]{1,0:T(8,128)(2,1)S(1)}, bf16[896,256]{1,0:T(8,128)(2,1)}, u32[]{:S(2)}) copy-start(bf16[896,256]{1,0:T(8,128)(2,1)} %down_hbm.3) | copy-start | bytes 1376260
  25.4 26.3 %copy-start.14 = (bf16[256,896]{1,0:T(8,128)(2,1)S(1)}, bf16[256,896]{1,0:T(8,128)(2,1)}, u32[]{:S(2)}) copy-start(bf16[256,896]{1,0:T(8,128)(2,1)} %gate_hbm.1) | copy-start | bytes 1376260
  25.4 26.3 %copy-start.15 = (bf16[256,896]{1,0:T(8,128)(2,1)S(1)}, bf16[256,896]{1,0:T(8,128)(2,1)}, u32[]{:S(2)}) copy-start(bf16[256,896]{1,0:T(8,128)(2,1)} %up_hbm.1) | copy-start | bytes 1376260
  47.0 29.0 %collective-permute-start.3 = (bf16[4,4,88,512]{3,2,1,0:T(8,128)(2,1)S(1)}, bf16[4,4,88,512]{3,2,1,0:T(8,128)(2,1)S(1)}, u32[]{:S(2)}, u32[]{:S(2)}) collective-permute-start(bf16[4,4,88,512]{3,2,1,0:T(8,128)(2,1)S(1)} %all_to_all.20.refs_0_), channel_id=1, source_target_pairs={{0,16},{16,0},{1,17},{17,1},{2,18},{18,2},{3,19},{19,3},{4,20},{20... | collective-permute-start | bytes 4325384 | tf_op jit(solution)/shard_map/ppermute | solution.py:469
  53.7 101.1 %copy-start.3 = (bf16[3,224,256]{2,1,0:T(8,128)(2,1)}, bf16[3,224,256]{2,1,0:T(8,128)(2,1)S(1)}, u32[]{:S(2)}) copy-start(bf16[3,224,256]{2,1,0:T(8,128)(2,1)S(1)} %get-tuple-element.33.w0_ref) | copy-start | bytes 1032196
  53.7 20.1 %collective-permute-start = (bf16[3,224,256]{2,1,0:T(8,128)(2,1)S(1)}, bf16[3,224,256]{2,1,0:T(8,128)(2,1)S(1)}, u32[]{:S(2)}, u32[]{:S(2)}) collective-permute-start(bf16[3,224,256]{2,1,0:T(8,128)(2,1)S(1)} %get-tuple-element.34), channel_id=1, source_target_pairs={{0,1},{1,2},{2,3},{3,0},{4,5},{5,6},{6,7},{7,4},{8,9},{9,10},{10,1... | collective-permute-start | bytes 1032200 | tf_op jit(solution)/shard_map/ppermute | solution.py:408
  55.6 18.2 %collective-permute-start.1 = (bf16[3,224,256]{2,1,0:T(8,128)(2,1)S(1)}, bf16[3,224,256]{2,1,0:T(8,128)(2,1)S(1)}, u32[]{:S(2)}, u32[]{:S(2)}) collective-permute-start(bf16[3,224,256]{2,1,0:T(8,128)(2,1)S(1)} %get-tuple-element.35), channel_id=1, source_target_pairs={{0,2},{1,3},{2,0},{3,1},{4,6},{5,7},{6,4},{7,5},{8,10},{9,11},{10,... | collective-permute-start | bytes 1032200 | tf_op jit(solution)/shard_map/ppermute | solution.py:408
  59.3 16.7 %collective-permute-start.2 = (bf16[3,224,256]{2,1,0:T(8,128)(2,1)S(1)}, bf16[3,224,256]{2,1,0:T(8,128)(2,1)S(1)}, u32[]{:S(2)}, u32[]{:S(2)}) collective-permute-start(bf16[3,224,256]{2,1,0:T(8,128)(2,1)S(1)} %get-tuple-element.36), channel_id=1, source_target_pairs={{0,3},{1,0},{2,1},{3,2},{4,7},{5,4},{6,5},{7,6},{8,11},{9,8},{10,9... | collective-permute-start | bytes 1032200 | tf_op jit(solution)/shard_map/ppermute | solution.py:408
  73.8 81.0 %copy-start.5 = (bf16[3,224,256]{2,1,0:T(8,128)(2,1)}, bf16[3,224,256]{2,1,0:T(8,128)(2,1)S(1)}, u32[]{:S(2)}) copy-start(bf16[3,224,256]{2,1,0:T(8,128)(2,1)S(1)} %collective-permute-done.w1_ref) | copy-start | bytes 1032196
  73.8 81.0 %copy-start.7 = (bf16[3,224,256]{2,1,0:T(8,128)(2,1)}, bf16[3,224,256]{2,1,0:T(8,128)(2,1)S(1)}, u32[]{:S(2)}) copy-start(bf16[3,224,256]{2,1,0:T(8,128)(2,1)S(1)} %collective-permute-done.1.w2_ref) | copy-start | bytes 1032196
  76.0 78.8 %copy-start.9 = (bf16[3,224,256]{2,1,0:T(8,128)(2,1)}, bf16[3,224,256]{2,1,0:T(8,128)(2,1)S(1)}, u32[]{:S(2)}) copy-start(bf16[3,224,256]{2,1,0:T(8,128)(2,1)S(1)} %collective-permute-done.2.w3_ref) | copy-start | bytes 1032196
  76.0 35.6 %copy-start.24 = (f32[896]{0:T(1024)S(1)}, f32[896]{0:T(1024)}, u32[]{:S(2)}) copy-start(f32[896]{0:T(1024)} %param.13) | copy-start | bytes 10756
  76.0 35.6 %copy-start.25 = (f32[896]{0:T(1024)S(1)}, f32[896]{0:T(1024)}, u32[]{:S(2)}) copy-start(f32[896]{0:T(1024)} %param.14) | copy-start | bytes 10756
  78.7 77.6 %copy-start.18 = (f32[4,8,256]{2,1,0:T(8,128)}, f32[4,8,256]{2,1,0:T(8,128)S(1)}, u32[]{:S(2)}) copy-start(f32[4,8,256]{2,1,0:T(8,128)S(1)} %get-tuple-element.44.refs_3_.rows_ref) | copy-start | bytes 98308
  78.7 24.8 %collective-permute-start.4 = (bf16[176,640]{1,0:T(8,128)(2,1)S(1)}, bf16[176,640]{1,0:T(8,128)(2,1)S(1)}, u32[]{:S(2)}, u32[]{:S(2)}) collective-permute-start(bf16[176,640]{1,0:T(8,128)(2,1)S(1)} %get-tuple-element.38), channel_id=1, source_target_pairs={{0,4},{4,8},{8,12},{12,0},{16,28},{20,16},{24,20},{28,24},{1,5},{5... | collective-permute-start | bytes 675848 | tf_op jit(solution)/shard_map/ppermute | solution.py:419
  88.5 23.2 %collective-permute-start.5 = (bf16[176,640]{1,0:T(8,128)(2,1)S(1)}, bf16[176,640]{1,0:T(8,128)(2,1)S(1)}, u32[]{:S(2)}, u32[]{:S(2)}) collective-permute-start(bf16[176,640]{1,0:T(8,128)(2,1)S(1)} %get-tuple-element.39), channel_id=1, source_target_pairs={{0,12},{4,0},{8,4},{12,8},{16,20},{20,24},{24,28},{28,16},{1,13},{... | collective-permute-start | bytes 675848 | tf_op jit(solution)/shard_map/ppermute | solution.py:419
  103.6 16.6 %collective-permute-start.6 = (bf16[176,640]{1,0:T(8,128)(2,1)S(1)}, bf16[176,640]{1,0:T(8,128)(2,1)S(1)}, u32[]{:S(2)}, u32[]{:S(2)}) collective-permute-start(bf16[176,640]{1,0:T(8,128)(2,1)S(1)} %shard_map.139), channel_id=1, source_target_pairs={{0,4},{4,8},{8,12},{12,0},{16,28},{20,16},{24,20},{28,24},{1,5},{5... | collective-permute-start | bytes 675848 | tf_op jit(solution)/shard_map/ppermute | solution.py:419
  121.4 33.4 %copy-start.21 = (f32[8,640]{1,0:T(8,128)}, f32[8,640]{1,0:T(8,128)S(1)}, u32[]{:S(2)}) copy-start(f32[8,640]{1,0:T(8,128)S(1)} %get-tuple-element.48.refs_3_) | copy-start | bytes 61444
  121.4 35.0 %copy-start.16 = (f32[224,128]{1,0:T(8,128)}, f32[224,128]{1,0:T(8,128)S(1)}, u32[]{:S(2)}) copy-start(f32[224,128]{1,0:T(8,128)S(1)} %get-tuple-element.43.refs_2_) | copy-start | bytes 344068
  154.8 1.6 copy-start
  156.4 8.9 %collective-permute-start.7 = (bf16[4,328,256]{2,1,0:T(8,128)(2,1)S(1)}, bf16[4,328,256]{2,1,0:T(8,128)(2,1)S(1)}, u32[]{:S(2)}, u32[]{:S(2)}) collective-permute-start(bf16[4,328,256]{2,1,0:T(8,128)(2,1)S(1)} %get-tuple-element.46), channel_id=1, source_target_pairs={{0,16},{16,0},{1,17},{17,1},{2,18},{18,2},{3,19},{19,3},{4,20},{20... | collective-permute-start | bytes 2015240 | tf_op jit(solution)/shard_map/ppermute | solution.py:495
  180.3 40.5 %all-to-all-start.3 = ((bf16[16,24,256]{2,1,0:T(8,128)(2,1)}), bf16[16,24,256]{2,1,0:T(8,128)(2,1)S(1)}, u32[]{:S(2)}, u32[]{:S(2)}) async-start(bf16[16,24,256]{2,1,0:T(8,128)(2,1)} %bitcast.19), calls=%async_computation.3 | async-start | bytes 393216 | tf_op jit(solution)/shard_map/all_to_all | solution.py:403
  184.3 1.2 copy-start.1
  185.4 1.0 copy-start.4
  186.4 1.0 copy-start.6
  187.4 1.0 copy-start.8
  191.0 29.8 %copy-start.20 = (bf16[20,256]{1,0:T(8,128)(2,1)S(1)}, bf16[20,256]{1,0:T(8,128)(2,1)}, u32[]{:S(2)}) copy-start(bf16[20,256]{1,0:T(8,128)(2,1)} %cotangent_ref.1) | copy-start | bytes 30724
  192.5 10.5 %collective-permute-start.8 = (bf16[680,256]{1,0:T(8,128)(2,1)S(1)}, bf16[680,256]{1,0:T(8,128)(2,1)S(1)}, u32[]{:S(2)}, u32[]{:S(2)}) collective-permute-start(bf16[680,256]{1,0:T(8,128)(2,1)S(1)} %get-tuple-element.50), channel_id=1, source_target_pairs={{0,3},{1,0},{2,1},{3,2},{4,7},{5,4},{6,5},{7,6},{8,11},{9,8},{10,9... | collective-permute-start | bytes 1044488 | tf_op jit(solution)/shard_map/ppermute | solution.py:408
  197.0 10.8 %collective-permute-start.9 = (bf16[680,256]{1,0:T(8,128)(2,1)S(1)}, bf16[680,256]{1,0:T(8,128)(2,1)S(1)}, u32[]{:S(2)}, u32[]{:S(2)}) collective-permute-start(bf16[680,256]{1,0:T(8,128)(2,1)S(1)} %get-tuple-element.51), channel_id=1, source_target_pairs={{0,2},{1,3},{2,0},{3,1},{4,6},{5,7},{6,4},{7,5},{8,10},{9,11},{10,... | collective-permute-start | bytes 1044488 | tf_op jit(solution)/shard_map/ppermute | solution.py:408
  199.5 18.2 %collective-permute-start.10 = (bf16[680,256]{1,0:T(8,128)(2,1)S(1)}, bf16[680,256]{1,0:T(8,128)(2,1)S(1)}, u32[]{:S(2)}, u32[]{:S(2)}) collective-permute-start(bf16[680,256]{1,0:T(8,128)(2,1)S(1)} %get-tuple-element.52), channel_id=1, source_target_pairs={{0,1},{1,2},{2,3},{3,0},{4,5},{5,6},{6,7},{7,4},{8,9},{9,10},{10,1... | collective-permute-start | bytes 1044488 | tf_op jit(solution)/shard_map/ppermute | solution.py:408
  220.8 1.0 copy-start.12
  (7 other events, 5.5 us)

commit v6 on v5

--- a/solution.py
+++ b/solution.py
@@ -139,11 +139,24 @@
     return mean, square
 
 
+def weight_moments(w0_ref, w1_ref, w2_ref, w3_ref, mean_ref, line_ref):
+    lane = lax.broadcasted_iota(jnp.int32, mean_ref.shape, 1)
+    means = jnp.zeros(mean_ref.shape, f32)
+    for at in range(2):
+        mean, square = moments_of((w0_ref, w1_ref, w2_ref, w3_ref), at)
+        means = jnp.where(lane == at, mean, means)
+        width = line_ref.shape[1] // 2
+        line_ref[at : at + 1, 0:width] = level(mean, width)
+        line_ref[at : at + 1, width : 2 * width] = level(square, width)
+    mean_ref[...] = means
+
+
 def forward(
     tall_count, place_ref, w0_ref, w1_ref, w2_ref, w3_ref, *refs
 ):
     token_refs = refs[:2]
-    kept_ref, first_ref, second_ref, third_ref, rows_ref, news_ref, store_ref = refs[2:]
+    mean_ref, line_ref = refs[2:4]
+    kept_ref, first_ref, second_ref, third_ref, rows_ref, news_ref, store_ref = refs[4:]
     w_ref = (w0_ref, w1_ref, w2_ref, w3_ref)
     blocks = len(w_ref)
     _, share, width = w0_ref.shape
@@ -152,16 +165,14 @@
     lefts = [whole(token_refs, j, 0) for j in range(blocks)]
     ones = jnp.ones((8, width), bf16)
     row = sum(nt(ones, left) for left in lefts)[0:1]
-    levels = []
     for at in range(2):
-        mean, square = moments_of(w_ref, at)
-        levels += [level(mean, 256), level(square, 256)]
+        mean = mean_ref[:, at : at + 1]
         total = sum(nt(w_ref[j][at], lefts[j]) for j in range(blocks))
         total = (total - mean * row).astype(bf16)
         for q in range(parts):
             store_ref[q, at * tall : (at + 1) * tall, :] = total[q * tall : (q + 1) * tall]
     rest = jnp.zeros((1, row.shape[1] - 512), f32)
-    lines = [row] + [jnp.concatenate([levels[2 * at], levels[2 * at + 1], rest], axis=1) for at in range(2)]
+    lines = [row] + [jnp.concatenate([line_ref[at : at + 1, :], rest], axis=1) for at in range(2)]
     lines = [p.astype(f32) for line in lines for p in pieces(line)[0:2]]
     news_ref[...] = jnp.concatenate([*lines, jnp.zeros((2, row.shape[1]), f32)], axis=0).astype(bf16)
     total = 0.0
@@ -467,11 +478,12 @@
     )
     own = exchange(both, "y")
     other = lax.ppermute(own, "core", swap)
+    means, lines = call(weight_moments, [((share, 128), f32), ((2, 512), f32)], *weights)
     piece, sent = ((3 * tall, count), bf16), ((3 * tall + 8, count), bf16)
     kept, first, second, third, rows_of, news = call(
         functools.partial(forward, hidden * nl),
         [piece, sent, sent, piece, ((nx, 8, width), f32), ((8, count), bf16)],
-        *weights, own, other,
+        *weights, own, other, means, lines,
         place=place,
         scratch=[pltpu.VMEM((nz, 3 * tall, count), bf16)],
     )

time: 227 us -> 226 us (level)
    unnamed x52 -> x46, local copies, waits for them, and re-layouts: 10.6 us -> 8.71 us
    pallas_call x12 -> x13, Pallas kernels: 16.5 us -> 16.9 us  [call(): pl.pallas_call(body, out_shape=[jax.ShapeDtypeStruct(s, t) for s, t in ou...]
where the time goes in v6:
time: 226 us; the launch traced here: 225 us
  blocking collectives  67.9 us (30%)
  waiting for transfers between devices  65.9 us (29%)
  starting transfers between devices  63.2 us (28%)
  Pallas kernels  16.9 us (7%)
  local copies, waits for them, and re-layouts  10.2 us (5%)
    all_to_all x2, blocking collectives, exchange(): return lax.all_to_all(x, axis, split_axis=0, concat_axis=0, tiled=True)  35 us
    all_gather x1, blocking collectives, block(): d = lax.all_gather(d, 'zh')  32.9 us
    ppermute x6, waiting for transfers between devices, shift(): return lax.ppermute(x, axis, [(i, (i + by) % size) for i in range(size)])  29.7 us
    ppermute x3, waiting for transfers between devices, apart(): return lax.ppermute(x, (axis, 'core') if outer else ('core', axis), pairs)  21.7 us
    ppermute x3, starting transfers between devices, apart(): return lax.ppermute(x, (axis, 'core') if outer else ('core', axis), pairs)  19.7 us
    ppermute x6, starting transfers between devices, shift(): return lax.ppermute(x, axis, [(i, (i + by) % size) for i in range(size)])  17.9 us
    pallas_call x13, Pallas kernels, call(): pl.pallas_call(body, out_shape=[jax.ShapeDtypeStruct(s, t) for s, t in ou...  16.9 us
    all_to_all x2, waiting for transfers between devices, exchange(): return lax.all_to_all(x, axis, split_axis=0, concat_axis=0, tiled=True)  12.9 us
  transfers between devices with their start and end apart: 13, of which 9 were waited for; matrix products, arithmetic and copies ran while one was open for 0% of the time, Pallas kernels for 3%

profile of v6, /device:TPU:1, one launch (start us, length us, event | category | flops | bytes accessed | tf_op | source)
XLA Modules:
  0.0 225.1 jit_solution(1950421800044071238)
XLA Ops:
  0.6 2.1 shard_map.136
  2.7 9.0 %all-to-all-start = ((bf16[16,24,512]{2,1,0:T(8,128)(2,1)}), bf16[16,24,512]{2,1,0:T(8,128)(2,1)S(1)}, u32[]{:S(2)}, u32[]{:S(2)}) async-start(bf16[16,24,512]{2,1,0:T(8,128)(2,1)} %bitcast.22), calls=%async_computation | async-start | bytes 786432 | tf_op jit(solution)/shard_map/all_to_all | solution.py:414
  11.8 12.9 %all-to-all-done = bf16[16,24,512]{2,1,0:T(8,128)(2,1)S(1)} async-done(((bf16[16,24,512]{2,1,0:T(8,128)(2,1)}), bf16[16,24,512]{2,1,0:T(8,128)(2,1)S(1)}, u32[]{:S(2)}, u32[]{:S(2)}) %all-to-all-start) | async-done | bytes 393248 | tf_op jit(solution)/shard_map/all_to_all | solution.py:414
  25.5 21.6 %all_to_all.20.refs_0_ = bf16[4,4,88,512]{3,2,1,0:T(8,128)(2,1)S(1)} all-to-all(bf16[4,4,88,512]{3,2,1,0:T(8,128)(2,1)S(1)} %shard_map.137), channel_id=1, replica_groups=mesh['y'=4,'zl'=4,'core'=2,'zh'=4,'x'=4] {'y'}, dimensions={0} | all-to-all | bytes 2883584 | tf_op jit(solution)/shard_map/all_to_all | solution.py:414
  47.0 4.7 %collective-permute-start.3 = (bf16[4,4,88,512]{3,2,1,0:T(8,128)(2,1)S(1)}, bf16[4,4,88,512]{3,2,1,0:T(8,128)(2,1)S(1)}, u32[]{:S(2)}, u32[]{:S(2)}) collective-permute-start(bf16[4,4,88,512]{3,2,1,0:T(8,128)(2,1)S(1)} %all_to_all.20.refs_0_), channel_id=1, source_target_pairs={{0,16},{16,0},{1,17},{17,1},{2,18},{18,2},{3,19},{19,3},{4,20},{20... | collective-permute-start | bytes 4325384 | tf_op jit(solution)/shard_map/ppermute | solution.py:480
  51.8 1.9 shard_map.135
  53.7 1.9 collective-permute-start
  55.6 3.7 %collective-permute-start.1 = (bf16[3,224,256]{2,1,0:T(8,128)(2,1)S(1)}, bf16[3,224,256]{2,1,0:T(8,128)(2,1)S(1)}, u32[]{:S(2)}, u32[]{:S(2)}) collective-permute-start(bf16[3,224,256]{2,1,0:T(8,128)(2,1)S(1)} %get-tuple-element.37), channel_id=1, source_target_pairs={{0,2},{1,3},{2,0},{3,1},{4,6},{5,7},{6,4},{7,5},{8,10},{9,11},{10,... | collective-permute-start | bytes 1032200 | tf_op jit(solution)/shard_map/ppermute | solution.py:419
  59.3 2.8 %collective-permute-start.2 = (bf16[3,224,256]{2,1,0:T(8,128)(2,1)S(1)}, bf16[3,224,256]{2,1,0:T(8,128)(2,1)S(1)}, u32[]{:S(2)}, u32[]{:S(2)}) collective-permute-start(bf16[3,224,256]{2,1,0:T(8,128)(2,1)S(1)} %get-tuple-element.38), channel_id=1, source_target_pairs={{0,3},{1,0},{2,1},{3,2},{4,7},{5,4},{6,5},{7,6},{8,11},{9,8},{10,9... | collective-permute-start | bytes 1032200 | tf_op jit(solution)/shard_map/ppermute | solution.py:419
  62.1 11.6 %collective-permute-done.w1_ref = bf16[3,224,256]{2,1,0:T(8,128)(2,1)S(1)} collective-permute-done((bf16[3,224,256]{2,1,0:T(8,128)(2,1)S(1)}, bf16[3,224,256]{2,1,0:T(8,128)(2,1)S(1)}, u32[]{:S(2)}, u32[]{:S(2)}) %collective-permute-start) | collective-permute-done | bytes 344096 | tf_op jit(solution)/shard_map/ppermute | solution.py:419
  73.8 2.2 collective-permute-done.2.w3_ref
  76.8 2.4 %shard_map.139 = (bf16[168,640]{1,0:T(8,128)(2,1)S(1)}, bf16[176,640]{1,0:T(8,128)(2,1)S(1)}, bf16[176,640]{1,0:T(8,128)(2,1)S(1)}, bf16[168,640]{1,0:T(8,128)(2...) custom-call(s32[5]{0:T(128)S(1)} %stack.23.place_ref, bf16[3,224,256]{2,1,0:T(8,128)(2,1)S(1)} %get-tuple-element.35.w0_ref, ...), custom_call_target="tpu_custom_call" | custom-call | tf_op jit(solution)/shard_map/pallas_call | solution.py:404
  79.2 9.8 %collective-permute-start.4 = (bf16[176,640]{1,0:T(8,128)(2,1)S(1)}, bf16[176,640]{1,0:T(8,128)(2,1)S(1)}, u32[]{:S(2)}, u32[]{:S(2)}) collective-permute-start(bf16[176,640]{1,0:T(8,128)(2,1)S(1)} %get-tuple-element.42), channel_id=1, source_target_pairs={{0,4},{4,8},{8,12},{12,0},{16,28},{20,16},{24,20},{28,24},{1,5},{5... | collective-permute-start | bytes 675848 | tf_op jit(solution)/shard_map/ppermute | solution.py:430
  88.9 1.9 collective-permute-start.5
  90.9 13.1 %collective-permute-done.4.b_ref.first_ref = bf16[176,640]{1,0:T(8,128)(2,1)S(1)} collective-permute-done((bf16[176,640]{1,0:T(8,128)(2,1)S(1)}, bf16[176,640]{1,0:T(8,128)(2,1)S(1)}, u32[]{:S(2)}, u32[]{:S(2)}) %collective-permute-start.4) | collective-permute-done | bytes 225312 | tf_op jit(solution)/shard_map/ppermute | solution.py:430
  104.0 8.0 %collective-permute-start.6 = (bf16[176,640]{1,0:T(8,128)(2,1)S(1)}, bf16[176,640]{1,0:T(8,128)(2,1)S(1)}, u32[]{:S(2)}, u32[]{:S(2)}) collective-permute-start(bf16[176,640]{1,0:T(8,128)(2,1)S(1)} %shard_map.140), channel_id=1, source_target_pairs={{0,4},{4,8},{8,12},{12,0},{16,28},{20,16},{24,20},{28,24},{1,5},{5... | collective-permute-start | bytes 675848 | tf_op jit(solution)/shard_map/ppermute | solution.py:430
  112.1 8.6 %collective-permute-done.6.third_ref = bf16[176,640]{1,0:T(8,128)(2,1)S(1)} collective-permute-done((bf16[176,640]{1,0:T(8,128)(2,1)S(1)}, bf16[176,640]{1,0:T(8,128)(2,1)S(1)}, u32[]{:S(2)}, u32[]{:S(2)}) %collective-permute-start.6) | collective-permute-done | bytes 225312 | tf_op jit(solution)/shard_map/ppermute | solution.py:430
  121.8 32.9 %all-gather = bf16[704,640]{1,0:T(8,128)(2,1)S(1)} all-gather(bf16[176,640]{1,0:T(8,128)(2,1)S(1)} %get-tuple-element.46), channel_id=2, replica_groups=mesh['y'=4,'zl'=4,'core'=2,'zh'=4,'x'=4] {'zh'}, dimensions={0}, use_global_device_ids=true | all-gather | bytes 1126400 | tf_op jit(solution)/shard_map/all_gather | solution.py:500
  154.8 1.5 shard_map.142
  156.3 8.3 %collective-permute-start.7 = (bf16[4,328,256]{2,1,0:T(8,128)(2,1)S(1)}, bf16[4,328,256]{2,1,0:T(8,128)(2,1)S(1)}, u32[]{:S(2)}, u32[]{:S(2)}) collective-permute-start(bf16[4,328,256]{2,1,0:T(8,128)(2,1)S(1)} %get-tuple-element.50), channel_id=1, source_target_pairs={{0,16},{16,0},{1,17},{17,1},{2,18},{18,2},{3,19},{19,3},{4,20},{20... | collective-permute-start | bytes 2015240 | tf_op jit(solution)/shard_map/ppermute | solution.py:507
  164.6 1.7 collective-permute-done.7.theirs_ref
  166.5 13.4 %all_to_all.21.in_ref = bf16[4,4,88,256]{3,2,1,0:T(8,128)(2,1)S(1)} all-to-all(bf16[4,4,88,256]{3,2,1,0:T(8,128)(2,1)S(1)} %shard_map.143), channel_id=1, replica_groups=mesh['y'=4,'zl'=4,'core'=2,'zh'=4,'x'=4] {'y'}, dimensions={0} | all-to-all | bytes 1441792 | tf_op jit(solution)/shard_map/all_to_all | solution.py:414
  181.3 3.5 %all-to-all-start.3 = ((bf16[16,24,256]{2,1,0:T(8,128)(2,1)}), bf16[16,24,256]{2,1,0:T(8,128)(2,1)S(1)}, u32[]{:S(2)}, u32[]{:S(2)}) async-start(bf16[16,24,256]{2,1,0:T(8,128)(2,1)} %bitcast.19), calls=%async_computation.3 | async-start | bytes 393216 | tf_op jit(solution)/shard_map/all_to_all | solution.py:414
  184.8 1.2 copy-done.1
  189.7 1.6 shard_map.145
  191.3 4.5 %collective-permute-start.8 = (bf16[680,256]{1,0:T(8,128)(2,1)S(1)}, bf16[680,256]{1,0:T(8,128)(2,1)S(1)}, u32[]{:S(2)}, u32[]{:S(2)}) collective-permute-start(bf16[680,256]{1,0:T(8,128)(2,1)S(1)} %get-tuple-element.54), channel_id=1, source_target_pairs={{0,3},{1,0},{2,1},{3,2},{4,7},{5,4},{6,5},{7,6},{8,11},{9,8},{10,9... | collective-permute-start | bytes 1044488 | tf_op jit(solution)/shard_map/ppermute | solution.py:419
  195.8 2.5 %collective-permute-start.9 = (bf16[680,256]{1,0:T(8,128)(2,1)S(1)}, bf16[680,256]{1,0:T(8,128)(2,1)S(1)}, u32[]{:S(2)}, u32[]{:S(2)}) collective-permute-start(bf16[680,256]{1,0:T(8,128)(2,1)S(1)} %get-tuple-element.55), channel_id=1, source_target_pairs={{0,2},{1,3},{2,0},{3,1},{4,6},{5,7},{6,4},{7,5},{8,10},{9,11},{10,... | collective-permute-start | bytes 1044488 | tf_op jit(solution)/shard_map/ppermute | solution.py:419
  198.3 2.5 %collective-permute-start.10 = (bf16[680,256]{1,0:T(8,128)(2,1)S(1)}, bf16[680,256]{1,0:T(8,128)(2,1)S(1)}, u32[]{:S(2)}, u32[]{:S(2)}) collective-permute-start(bf16[680,256]{1,0:T(8,128)(2,1)S(1)} %get-tuple-element.56), channel_id=1, source_target_pairs={{0,1},{1,2},{2,3},{3,0},{4,5},{5,6},{6,7},{7,4},{8,9},{9,10},{10,1... | collective-permute-start | bytes 1044488 | tf_op jit(solution)/shard_map/ppermute | solution.py:419
  201.7 5.0 %collective-permute-done.9.g2_ref = bf16[680,256]{1,0:T(8,128)(2,1)S(1)} collective-permute-done((bf16[680,256]{1,0:T(8,128)(2,1)S(1)}, bf16[680,256]{1,0:T(8,128)(2,1)S(1)}, u32[]{:S(2)}, u32[]{:S(2)}) %collective-permute-start.9) | collective-permute-done | bytes 348192 | tf_op jit(solution)/shard_map/ppermute | solution.py:419
  206.7 9.9 %collective-permute-done.10.g3_ref = bf16[680,256]{1,0:T(8,128)(2,1)S(1)} collective-permute-done((bf16[680,256]{1,0:T(8,128)(2,1)S(1)}, bf16[680,256]{1,0:T(8,128)(2,1)S(1)}, u32[]{:S(2)}, u32[]{:S(2)}) %collective-permute-start.10) | collective-permute-done | bytes 348192 | tf_op jit(solution)/shard_map/ppermute | solution.py:419
  216.6 2.3 %shard_map.147 = (f32[256,896]{1,0:T(8,128)}, f32[256,896]{1,0:T(8,128)}) custom-call(s32[5]{0:T(128)S(1)} %stack.23.place_ref, bf16[680,256]{1,0:T(8,128)(2,1)S(1)} %get-tuple-element.53.g0_ref, bf16[680,256]{1,0:T(8,128)(2,1)S(1)} %collective-permute-done.8.g1_ref, bf16[680,256]{1,0:T(8,128)(2,1)S(1)} %collective-permute-done.9.g2_ref, ...), custom_call_target="tpu_custom_call" | custom-call | tf_op jit(solution)/shard_map/pallas_call | solution.py:404
  222.0 1.7 shard_map.146
  (62 shorter events, 13.4 us)
Async XLA Ops:
  2.7 22.0 %all-to-all-start = ((bf16[16,24,512]{2,1,0:T(8,128)(2,1)}), bf16[16,24,512]{2,1,0:T(8,128)(2,1)S(1)}, u32[]{:S(2)}, u32[]{:S(2)}) async-start(bf16[16,24,512]{2,1,0:T(8,128)(2,1)} %bitcast.22), calls=%async_computation | async-start | bytes 786432 | tf_op jit(solution)/shard_map/all_to_all | solution.py:414
  25.4 26.3 %copy-start.8 = (bf16[896,256]{1,0:T(8,128)(2,1)S(1)}, bf16[896,256]{1,0:T(8,128)(2,1)}, u32[]{:S(2)}) copy-start(bf16[896,256]{1,0:T(8,128)(2,1)} %down_hbm.3) | copy-start | bytes 1376260
  25.4 26.3 %copy-start.13 = (bf16[256,896]{1,0:T(8,128)(2,1)S(1)}, bf16[256,896]{1,0:T(8,128)(2,1)}, u32[]{:S(2)}) copy-start(bf16[256,896]{1,0:T(8,128)(2,1)} %gate_hbm.1) | copy-start | bytes 1376260
  25.4 26.3 %copy-start.14 = (bf16[256,896]{1,0:T(8,128)(2,1)S(1)}, bf16[256,896]{1,0:T(8,128)(2,1)}, u32[]{:S(2)}) copy-start(bf16[256,896]{1,0:T(8,128)(2,1)} %up_hbm.1) | copy-start | bytes 1376260
  47.0 29.8 %collective-permute-start.3 = (bf16[4,4,88,512]{3,2,1,0:T(8,128)(2,1)S(1)}, bf16[4,4,88,512]{3,2,1,0:T(8,128)(2,1)S(1)}, u32[]{:S(2)}, u32[]{:S(2)}) collective-permute-start(bf16[4,4,88,512]{3,2,1,0:T(8,128)(2,1)S(1)} %all_to_all.20.refs_0_), channel_id=1, source_target_pairs={{0,16},{16,0},{1,17},{17,1},{2,18},{18,2},{3,19},{19,3},{4,20},{20... | collective-permute-start | bytes 4325384 | tf_op jit(solution)/shard_map/ppermute | solution.py:480
  53.7 20.1 %collective-permute-start = (bf16[3,224,256]{2,1,0:T(8,128)(2,1)S(1)}, bf16[3,224,256]{2,1,0:T(8,128)(2,1)S(1)}, u32[]{:S(2)}, u32[]{:S(2)}) collective-permute-start(bf16[3,224,256]{2,1,0:T(8,128)(2,1)S(1)} %get-tuple-element.36), channel_id=1, source_target_pairs={{0,1},{1,2},{2,3},{3,0},{4,5},{5,6},{6,7},{7,4},{8,9},{9,10},{10,1... | collective-permute-start | bytes 1032200 | tf_op jit(solution)/shard_map/ppermute | solution.py:419
  55.6 18.2 %collective-permute-start.1 = (bf16[3,224,256]{2,1,0:T(8,128)(2,1)S(1)}, bf16[3,224,256]{2,1,0:T(8,128)(2,1)S(1)}, u32[]{:S(2)}, u32[]{:S(2)}) collective-permute-start(bf16[3,224,256]{2,1,0:T(8,128)(2,1)S(1)} %get-tuple-element.37), channel_id=1, source_target_pairs={{0,2},{1,3},{2,0},{3,1},{4,6},{5,7},{6,4},{7,5},{8,10},{9,11},{10,... | collective-permute-start | bytes 1032200 | tf_op jit(solution)/shard_map/ppermute | solution.py:419
  59.3 16.7 %collective-permute-start.2 = (bf16[3,224,256]{2,1,0:T(8,128)(2,1)S(1)}, bf16[3,224,256]{2,1,0:T(8,128)(2,1)S(1)}, u32[]{:S(2)}, u32[]{:S(2)}) collective-permute-start(bf16[3,224,256]{2,1,0:T(8,128)(2,1)S(1)} %get-tuple-element.38), channel_id=1, source_target_pairs={{0,3},{1,0},{2,1},{3,2},{4,7},{5,4},{6,5},{7,6},{8,11},{9,8},{10,9... | collective-permute-start | bytes 1032200 | tf_op jit(solution)/shard_map/ppermute | solution.py:419
  73.8 81.0 %copy-start.2 = (bf16[3,224,256]{2,1,0:T(8,128)(2,1)}, bf16[3,224,256]{2,1,0:T(8,128)(2,1)S(1)}, u32[]{:S(2)}) copy-start(bf16[3,224,256]{2,1,0:T(8,128)(2,1)S(1)} %collective-permute-done.w1_ref) | copy-start | bytes 1032196
  73.8 81.0 %copy-start.4 = (bf16[3,224,256]{2,1,0:T(8,128)(2,1)}, bf16[3,224,256]{2,1,0:T(8,128)(2,1)S(1)}, u32[]{:S(2)}) copy-start(bf16[3,224,256]{2,1,0:T(8,128)(2,1)S(1)} %collective-permute-done.1.w2_ref) | copy-start | bytes 1032196
  76.0 78.8 %copy-start.6 = (bf16[3,224,256]{2,1,0:T(8,128)(2,1)}, bf16[3,224,256]{2,1,0:T(8,128)(2,1)S(1)}, u32[]{:S(2)}) copy-start(bf16[3,224,256]{2,1,0:T(8,128)(2,1)S(1)} %collective-permute-done.2.w3_ref) | copy-start | bytes 1032196
  76.8 35.3 %copy-start.21 = (f32[896]{0:T(1024)S(1)}, f32[896]{0:T(1024)}, u32[]{:S(2)}) copy-start(f32[896]{0:T(1024)} %param.13) | copy-start | bytes 10756
  76.8 35.3 %copy-start.22 = (f32[896]{0:T(1024)S(1)}, f32[896]{0:T(1024)}, u32[]{:S(2)}) copy-start(f32[896]{0:T(1024)} %param.14) | copy-start | bytes 10756
  79.2 77.1 %copy-start.15 = (f32[4,8,256]{2,1,0:T(8,128)}, f32[4,8,256]{2,1,0:T(8,128)S(1)}, u32[]{:S(2)}) copy-start(f32[4,8,256]{2,1,0:T(8,128)S(1)} %get-tuple-element.48.refs_3_.rows_ref) | copy-start | bytes 98308
  79.2 24.8 %collective-permute-start.4 = (bf16[176,640]{1,0:T(8,128)(2,1)S(1)}, bf16[176,640]{1,0:T(8,128)(2,1)S(1)}, u32[]{:S(2)}, u32[]{:S(2)}) collective-permute-start(bf16[176,640]{1,0:T(8,128)(2,1)S(1)} %get-tuple-element.42), channel_id=1, source_target_pairs={{0,4},{4,8},{8,12},{12,0},{16,28},{20,16},{24,20},{28,24},{1,5},{5... | collective-permute-start | bytes 675848 | tf_op jit(solution)/shard_map/ppermute | solution.py:430
  88.9 23.2 %collective-permute-start.5 = (bf16[176,640]{1,0:T(8,128)(2,1)S(1)}, bf16[176,640]{1,0:T(8,128)(2,1)S(1)}, u32[]{:S(2)}, u32[]{:S(2)}) collective-permute-start(bf16[176,640]{1,0:T(8,128)(2,1)S(1)} %get-tuple-element.43), channel_id=1, source_target_pairs={{0,12},{4,0},{8,4},{12,8},{16,20},{20,24},{24,28},{28,16},{1,13},{... | collective-permute-start | bytes 675848 | tf_op jit(solution)/shard_map/ppermute | solution.py:430
  104.0 16.6 %collective-permute-start.6 = (bf16[176,640]{1,0:T(8,128)(2,1)S(1)}, bf16[176,640]{1,0:T(8,128)(2,1)S(1)}, u32[]{:S(2)}, u32[]{:S(2)}) collective-permute-start(bf16[176,640]{1,0:T(8,128)(2,1)S(1)} %shard_map.140), channel_id=1, source_target_pairs={{0,4},{4,8},{8,12},{12,0},{16,28},{20,16},{24,20},{28,24},{1,5},{5... | collective-permute-start | bytes 675848 | tf_op jit(solution)/shard_map/ppermute | solution.py:430
  121.8 32.9 %copy-start.18 = (f32[8,640]{1,0:T(8,128)}, f32[8,640]{1,0:T(8,128)S(1)}, u32[]{:S(2)}) copy-start(f32[8,640]{1,0:T(8,128)S(1)} %get-tuple-element.52.refs_3_) | copy-start | bytes 61444
  154.8 1.5 copy-start
  156.3 10.0 %collective-permute-start.7 = (bf16[4,328,256]{2,1,0:T(8,128)(2,1)S(1)}, bf16[4,328,256]{2,1,0:T(8,128)(2,1)S(1)}, u32[]{:S(2)}, u32[]{:S(2)}) collective-permute-start(bf16[4,328,256]{2,1,0:T(8,128)(2,1)S(1)} %get-tuple-element.50), channel_id=1, source_target_pairs={{0,16},{16,0},{1,17},{17,1},{2,18},{18,2},{3,19},{19,3},{4,20},{20... | collective-permute-start | bytes 2015240 | tf_op jit(solution)/shard_map/ppermute | solution.py:507
  181.3 38.3 %all-to-all-start.3 = ((bf16[16,24,256]{2,1,0:T(8,128)(2,1)}), bf16[16,24,256]{2,1,0:T(8,128)(2,1)S(1)}, u32[]{:S(2)}, u32[]{:S(2)}) async-start(bf16[16,24,256]{2,1,0:T(8,128)(2,1)} %bitcast.19), calls=%async_computation.3 | async-start | bytes 393216 | tf_op jit(solution)/shard_map/all_to_all | solution.py:414
  184.8 1.2 copy-start.1
  186.0 1.0 copy-start.3
  187.0 1.0 copy-start.5
  187.9 1.0 copy-start.7
  189.7 30.0 %copy-start.17 = (bf16[20,256]{1,0:T(8,128)(2,1)S(1)}, bf16[20,256]{1,0:T(8,128)(2,1)}, u32[]{:S(2)}) copy-start(bf16[20,256]{1,0:T(8,128)(2,1)} %cotangent_ref.1) | copy-start | bytes 30724
  191.3 28.4 %copy-start.9 = (bf16[896,256]{1,0:T(8,128)(2,1)S(1)}, bf16[896,256]{1,0:T(8,128)(2,1)}, u32[]{:S(2)}) copy-start(bf16[896,256]{1,0:T(8,128)(2,1)} %down_hbm.3) | copy-start | bytes 1376260
  191.3 10.4 %collective-permute-start.8 = (bf16[680,256]{1,0:T(8,128)(2,1)S(1)}, bf16[680,256]{1,0:T(8,128)(2,1)S(1)}, u32[]{:S(2)}, u32[]{:S(2)}) collective-permute-start(bf16[680,256]{1,0:T(8,128)(2,1)S(1)} %get-tuple-element.54), channel_id=1, source_target_pairs={{0,3},{1,0},{2,1},{3,2},{4,7},{5,4},{6,5},{7,6},{8,11},{9,8},{10,9... | collective-permute-start | bytes 1044488 | tf_op jit(solution)/shard_map/ppermute | solution.py:419
  195.8 10.9 %collective-permute-start.9 = (bf16[680,256]{1,0:T(8,128)(2,1)S(1)}, bf16[680,256]{1,0:T(8,128)(2,1)S(1)}, u32[]{:S(2)}, u32[]{:S(2)}) collective-permute-start(bf16[680,256]{1,0:T(8,128)(2,1)S(1)} %get-tuple-element.55), channel_id=1, source_target_pairs={{0,2},{1,3},{2,0},{3,1},{4,6},{5,7},{6,4},{7,5},{8,10},{9,11},{10,... | collective-permute-start | bytes 1044488 | tf_op jit(solution)/shard_map/ppermute | solution.py:419
  198.3 18.3 %collective-permute-start.10 = (bf16[680,256]{1,0:T(8,128)(2,1)S(1)}, bf16[680,256]{1,0:T(8,128)(2,1)S(1)}, u32[]{:S(2)}, u32[]{:S(2)}) collective-permute-start(bf16[680,256]{1,0:T(8,128)(2,1)S(1)} %get-tuple-element.56), channel_id=1, source_target_pairs={{0,1},{1,2},{2,3},{3,0},{4,5},{5,6},{6,7},{7,4},{8,9},{9,10},{10,1... | collective-permute-start | bytes 1044488 | tf_op jit(solution)/shard_map/ppermute | solution.py:419
  219.6 1.0 copy-start.11
  220.6 0.8 copy-start.16
  (4 other events, 2.8 us)

commit v7 on v6

--- a/solution.py
+++ b/solution.py
@@ -66,16 +66,26 @@
 def pack_tokens(
     down_hbm, gain_hbm, tokens_hbm, cotangent_hbm, out_ref, down_ref, gain_ref, tokens_ref, cotangent_ref, sems
 ):
+    cuts = sems.shape[0] - 3
+    high = down_ref.shape[0] // cuts
+    spans = [slice(i * high, (i + 1) * high) for i in range(cuts)]
     copies = fetched(
-        ((down_hbm, down_ref), (gain_hbm, gain_ref), (tokens_hbm, tokens_ref), (cotangent_hbm, cotangent_ref)), sems
+        [
+            *((down_hbm.at[at], down_ref.at[at]) for at in spans),
+            (gain_hbm, gain_ref), (tokens_hbm, tokens_ref), (cotangent_hbm, cotangent_ref),
+        ],
+        sems,
     )
     _, width = tokens_ref.shape
-    copies[0].wait()
-    w = down_ref[...].astype(f32)
-    mean = jnp.sum(w, axis=0, keepdims=True) * (1.0 / w.shape[0])
-    off = w - mean
-    square = jnp.sum(off * off, axis=0, keepdims=True)
-    for c in copies[1:]:
+    moments = []
+    for c, at in zip(copies, spans):
+        c.wait()
+        w = down_ref[at, :].astype(f32)
+        mean = jnp.sum(w, axis=0, keepdims=True) * (1.0 / high)
+        off = w - mean
+        moments.append((mean, jnp.sum(off * off, axis=0, keepdims=True)))
+    mean, square = merged(moments, high)
+    for c in copies[cuts:]:
         c.wait()
     scaled = (branch_scale * cotangent_ref[...].astype(f32)).astype(bf16)
     gain = pieces(gain_ref[...])
@@ -456,7 +466,7 @@
         grant=60,
         scratch=[
             pltpu.VMEM((hidden, width), bf16), pltpu.VMEM((1, width), f32),
-            pltpu.VMEM((rows, width), bf16), pltpu.VMEM((rows, width), bf16), pltpu.SemaphoreType.DMA((4,)),
+            pltpu.VMEM((rows, width), bf16), pltpu.VMEM((rows, width), bf16), pltpu.SemaphoreType.DMA((7,)),
         ],
     )
     both = grid_exchange(both, ("x", "zl"))

time: 226 us -> 225 us (level)
  no operation moved by 1% of the time
where the time goes in v7:
time: 225 us; the launch traced here: 224 us
  blocking collectives  67.8 us (30%)
  waiting for transfers between devices  65.9 us (29%)
  starting transfers between devices  62.6 us (28%)
  Pallas kernels  16.9 us (8%)
  local copies, waits for them, and re-layouts  10.2 us (5%)
    all_to_all x2, blocking collectives, exchange(): return lax.all_to_all(x, axis, split_axis=0, concat_axis=0, tiled=True)  35 us
    all_gather x1, blocking collectives, block(): d = lax.all_gather(d, 'zh')  32.9 us
    ppermute x6, waiting for transfers between devices, shift(): return lax.ppermute(x, axis, [(i, (i + by) % size) for i in range(size)])  29.6 us
    ppermute x3, waiting for transfers between devices, apart(): return lax.ppermute(x, (axis, 'core') if outer else ('core', axis), pairs)  21.7 us
    ppermute x3, starting transfers between devices, apart(): return lax.ppermute(x, (axis, 'core') if outer else ('core', axis), pairs)  19.7 us
    ppermute x6, starting transfers between devices, shift(): return lax.ppermute(x, axis, [(i, (i + by) % size) for i in range(size)])  18 us
    pallas_call x13, Pallas kernels, call(): pl.pallas_call(body, out_shape=[jax.ShapeDtypeStruct(s, t) for s, t in ou...  16.9 us
    all_to_all x2, waiting for transfers between devices, exchange(): return lax.all_to_all(x, axis, split_axis=0, concat_axis=0, tiled=True)  12.9 us
  transfers between devices with their start and end apart: 13, of which 9 were waited for; matrix products, arithmetic and copies ran while one was open for 0% of the time, Pallas kernels for 3%

profile of v7, /device:TPU:1, one launch (start us, length us, event | category | flops | bytes accessed | tf_op | source)
XLA Modules:
  0.0 224.4 jit_solution(18347663375470585901)
XLA Ops:
  0.6 2.0 shard_map.136
  2.7 9.0 %all-to-all-start = ((bf16[16,24,512]{2,1,0:T(8,128)(2,1)}), bf16[16,24,512]{2,1,0:T(8,128)(2,1)S(1)}, u32[]{:S(2)}, u32[]{:S(2)}) async-start(bf16[16,24,512]{2,1,0:T(8,128)(2,1)} %bitcast.22), calls=%async_computation | async-start | bytes 786432 | tf_op jit(solution)/shard_map/all_to_all | solution.py:424
  11.8 12.9 %all-to-all-done = bf16[16,24,512]{2,1,0:T(8,128)(2,1)S(1)} async-done(((bf16[16,24,512]{2,1,0:T(8,128)(2,1)}), bf16[16,24,512]{2,1,0:T(8,128)(2,1)S(1)}, u32[]{:S(2)}, u32[]{:S(2)}) %all-to-all-start) | async-done | bytes 393248 | tf_op jit(solution)/shard_map/all_to_all | solution.py:424
  25.4 21.6 %all_to_all.20.refs_0_ = bf16[4,4,88,512]{3,2,1,0:T(8,128)(2,1)S(1)} all-to-all(bf16[4,4,88,512]{3,2,1,0:T(8,128)(2,1)S(1)} %shard_map.137), channel_id=1, replica_groups=mesh['y'=4,'zl'=4,'core'=2,'zh'=4,'x'=4] {'y'}, dimensions={0} | all-to-all | bytes 2883584 | tf_op jit(solution)/shard_map/all_to_all | solution.py:424
  47.0 4.7 %collective-permute-start.3 = (bf16[4,4,88,512]{3,2,1,0:T(8,128)(2,1)S(1)}, bf16[4,4,88,512]{3,2,1,0:T(8,128)(2,1)S(1)}, u32[]{:S(2)}, u32[]{:S(2)}) collective-permute-start(bf16[4,4,88,512]{3,2,1,0:T(8,128)(2,1)S(1)} %all_to_all.20.refs_0_), channel_id=1, source_target_pairs={{0,16},{16,0},{1,17},{17,1},{2,18},{18,2},{3,19},{19,3},{4,20},{20... | collective-permute-start | bytes 4325384 | tf_op jit(solution)/shard_map/ppermute | solution.py:490
  51.7 1.9 shard_map.135
  53.7 1.9 collective-permute-start
  55.6 3.7 %collective-permute-start.1 = (bf16[3,224,256]{2,1,0:T(8,128)(2,1)S(1)}, bf16[3,224,256]{2,1,0:T(8,128)(2,1)S(1)}, u32[]{:S(2)}, u32[]{:S(2)}) collective-permute-start(bf16[3,224,256]{2,1,0:T(8,128)(2,1)S(1)} %get-tuple-element.37), channel_id=1, source_target_pairs={{0,2},{1,3},{2,0},{3,1},{4,6},{5,7},{6,4},{7,5},{8,10},{9,11},{10,... | collective-permute-start | bytes 1032200 | tf_op jit(solution)/shard_map/ppermute | solution.py:429
  59.2 2.8 %collective-permute-start.2 = (bf16[3,224,256]{2,1,0:T(8,128)(2,1)S(1)}, bf16[3,224,256]{2,1,0:T(8,128)(2,1)S(1)}, u32[]{:S(2)}, u32[]{:S(2)}) collective-permute-start(bf16[3,224,256]{2,1,0:T(8,128)(2,1)S(1)} %get-tuple-element.38), channel_id=1, source_target_pairs={{0,3},{1,0},{2,1},{3,2},{4,7},{5,4},{6,5},{7,6},{8,11},{9,8},{10,9... | collective-permute-start | bytes 1032200 | tf_op jit(solution)/shard_map/ppermute | solution.py:429
  62.1 11.6 %collective-permute-done.w1_ref = bf16[3,224,256]{2,1,0:T(8,128)(2,1)S(1)} collective-permute-done((bf16[3,224,256]{2,1,0:T(8,128)(2,1)S(1)}, bf16[3,224,256]{2,1,0:T(8,128)(2,1)S(1)}, u32[]{:S(2)}, u32[]{:S(2)}) %collective-permute-start) | collective-permute-done | bytes 344096 | tf_op jit(solution)/shard_map/ppermute | solution.py:429
  73.7 2.2 %collective-permute-done.2.w3_ref = bf16[3,224,256]{2,1,0:T(8,128)(2,1)S(1)} collective-permute-done((bf16[3,224,256]{2,1,0:T(8,128)(2,1)S(1)}, bf16[3,224,256]{2,1,0:T(8,128)(2,1)S(1)}, u32[]{:S(2)}, u32[]{:S(2)}) %collective-permute-start.2) | collective-permute-done | bytes 344096 | tf_op jit(solution)/shard_map/ppermute | solution.py:429
  76.8 2.4 %shard_map.139 = (bf16[168,640]{1,0:T(8,128)(2,1)S(1)}, bf16[176,640]{1,0:T(8,128)(2,1)S(1)}, bf16[176,640]{1,0:T(8,128)(2,1)S(1)}, bf16[168,640]{1,0:T(8,128)(2...) custom-call(s32[5]{0:T(128)S(1)} %stack.23.place_ref, bf16[3,224,256]{2,1,0:T(8,128)(2,1)S(1)} %get-tuple-element.35.w0_ref, ...), custom_call_target="tpu_custom_call" | custom-call | tf_op jit(solution)/shard_map/pallas_call | solution.py:414
  79.1 9.8 %collective-permute-start.4 = (bf16[176,640]{1,0:T(8,128)(2,1)S(1)}, bf16[176,640]{1,0:T(8,128)(2,1)S(1)}, u32[]{:S(2)}, u32[]{:S(2)}) collective-permute-start(bf16[176,640]{1,0:T(8,128)(2,1)S(1)} %get-tuple-element.42), channel_id=1, source_target_pairs={{0,4},{4,8},{8,12},{12,0},{16,28},{20,16},{24,20},{28,24},{1,5},{5... | collective-permute-start | bytes 675848 | tf_op jit(solution)/shard_map/ppermute | solution.py:440
  88.9 1.9 collective-permute-start.5
  90.8 13.1 %collective-permute-done.4.b_ref.first_ref = bf16[176,640]{1,0:T(8,128)(2,1)S(1)} collective-permute-done((bf16[176,640]{1,0:T(8,128)(2,1)S(1)}, bf16[176,640]{1,0:T(8,128)(2,1)S(1)}, u32[]{:S(2)}, u32[]{:S(2)}) %collective-permute-start.4) | collective-permute-done | bytes 225312 | tf_op jit(solution)/shard_map/ppermute | solution.py:440
  104.0 8.0 %collective-permute-start.6 = (bf16[176,640]{1,0:T(8,128)(2,1)S(1)}, bf16[176,640]{1,0:T(8,128)(2,1)S(1)}, u32[]{:S(2)}, u32[]{:S(2)}) collective-permute-start(bf16[176,640]{1,0:T(8,128)(2,1)S(1)} %shard_map.140), channel_id=1, source_target_pairs={{0,4},{4,8},{8,12},{12,0},{16,28},{20,16},{24,20},{28,24},{1,5},{5... | collective-permute-start | bytes 675848 | tf_op jit(solution)/shard_map/ppermute | solution.py:440
  112.1 8.6 %collective-permute-done.6.third_ref = bf16[176,640]{1,0:T(8,128)(2,1)S(1)} collective-permute-done((bf16[176,640]{1,0:T(8,128)(2,1)S(1)}, bf16[176,640]{1,0:T(8,128)(2,1)S(1)}, u32[]{:S(2)}, u32[]{:S(2)}) %collective-permute-start.6) | collective-permute-done | bytes 225312 | tf_op jit(solution)/shard_map/ppermute | solution.py:440
  121.8 32.9 %all-gather = bf16[704,640]{1,0:T(8,128)(2,1)S(1)} all-gather(bf16[176,640]{1,0:T(8,128)(2,1)S(1)} %get-tuple-element.46), channel_id=2, replica_groups=mesh['y'=4,'zl'=4,'core'=2,'zh'=4,'x'=4] {'zh'}, dimensions={0}, use_global_device_ids=true | all-gather | bytes 1126400 | tf_op jit(solution)/shard_map/all_gather | solution.py:510
  154.7 1.5 shard_map.142
  156.2 7.4 %collective-permute-start.7 = (bf16[4,328,256]{2,1,0:T(8,128)(2,1)S(1)}, bf16[4,328,256]{2,1,0:T(8,128)(2,1)S(1)}, u32[]{:S(2)}, u32[]{:S(2)}) collective-permute-start(bf16[4,328,256]{2,1,0:T(8,128)(2,1)S(1)} %get-tuple-element.50), channel_id=1, source_target_pairs={{0,16},{16,0},{1,17},{17,1},{2,18},{18,2},{3,19},{19,3},{4,20},{20... | collective-permute-start | bytes 2015240 | tf_op jit(solution)/shard_map/ppermute | solution.py:517
  163.7 1.7 collective-permute-done.7.theirs_ref
  165.5 13.4 %all_to_all.21.in_ref = bf16[4,4,88,256]{3,2,1,0:T(8,128)(2,1)S(1)} all-to-all(bf16[4,4,88,256]{3,2,1,0:T(8,128)(2,1)S(1)} %shard_map.143), channel_id=1, replica_groups=mesh['y'=4,'zl'=4,'core'=2,'zh'=4,'x'=4] {'y'}, dimensions={0} | all-to-all | bytes 1441792 | tf_op jit(solution)/shard_map/all_to_all | solution.py:424
  180.3 3.7 %all-to-all-start.3 = ((bf16[16,24,256]{2,1,0:T(8,128)(2,1)}), bf16[16,24,256]{2,1,0:T(8,128)(2,1)S(1)}, u32[]{:S(2)}, u32[]{:S(2)}) async-start(bf16[16,24,256]{2,1,0:T(8,128)(2,1)} %bitcast.19), calls=%async_computation.3 | async-start | bytes 393216 | tf_op jit(solution)/shard_map/all_to_all | solution.py:424
  184.1 1.2 copy-done.1
  188.9 1.6 shard_map.145
  190.5 4.6 %collective-permute-start.8 = (bf16[680,256]{1,0:T(8,128)(2,1)S(1)}, bf16[680,256]{1,0:T(8,128)(2,1)S(1)}, u32[]{:S(2)}, u32[]{:S(2)}) collective-permute-start(bf16[680,256]{1,0:T(8,128)(2,1)S(1)} %get-tuple-element.54), channel_id=1, source_target_pairs={{0,3},{1,0},{2,1},{3,2},{4,7},{5,4},{6,5},{7,6},{8,11},{9,8},{10,9... | collective-permute-start | bytes 1044488 | tf_op jit(solution)/shard_map/ppermute | solution.py:429
  195.1 2.5 %collective-permute-start.9 = (bf16[680,256]{1,0:T(8,128)(2,1)S(1)}, bf16[680,256]{1,0:T(8,128)(2,1)S(1)}, u32[]{:S(2)}, u32[]{:S(2)}) collective-permute-start(bf16[680,256]{1,0:T(8,128)(2,1)S(1)} %get-tuple-element.55), channel_id=1, source_target_pairs={{0,2},{1,3},{2,0},{3,1},{4,6},{5,7},{6,4},{7,5},{8,10},{9,11},{10,... | collective-permute-start | bytes 1044488 | tf_op jit(solution)/shard_map/ppermute | solution.py:429
  197.6 2.5 %collective-permute-start.10 = (bf16[680,256]{1,0:T(8,128)(2,1)S(1)}, bf16[680,256]{1,0:T(8,128)(2,1)S(1)}, u32[]{:S(2)}, u32[]{:S(2)}) collective-permute-start(bf16[680,256]{1,0:T(8,128)(2,1)S(1)} %get-tuple-element.56), channel_id=1, source_target_pairs={{0,1},{1,2},{2,3},{3,0},{4,5},{5,6},{6,7},{7,4},{8,9},{9,10},{10,1... | collective-permute-start | bytes 1044488 | tf_op jit(solution)/shard_map/ppermute | solution.py:429
  201.1 4.8 %collective-permute-done.9.g2_ref = bf16[680,256]{1,0:T(8,128)(2,1)S(1)} collective-permute-done((bf16[680,256]{1,0:T(8,128)(2,1)S(1)}, bf16[680,256]{1,0:T(8,128)(2,1)S(1)}, u32[]{:S(2)}, u32[]{:S(2)}) %collective-permute-start.9) | collective-permute-done | bytes 348192 | tf_op jit(solution)/shard_map/ppermute | solution.py:429
  205.9 9.9 %collective-permute-done.10.g3_ref = bf16[680,256]{1,0:T(8,128)(2,1)S(1)} collective-permute-done((bf16[680,256]{1,0:T(8,128)(2,1)S(1)}, bf16[680,256]{1,0:T(8,128)(2,1)S(1)}, u32[]{:S(2)}, u32[]{:S(2)}) %collective-permute-start.10) | collective-permute-done | bytes 348192 | tf_op jit(solution)/shard_map/ppermute | solution.py:429
  215.8 2.3 %shard_map.147 = (f32[256,896]{1,0:T(8,128)}, f32[256,896]{1,0:T(8,128)}) custom-call(s32[5]{0:T(128)S(1)} %stack.23.place_ref, bf16[680,256]{1,0:T(8,128)(2,1)S(1)} %get-tuple-element.53.g0_ref, bf16[680,256]{1,0:T(8,128)(2,1)S(1)} %collective-permute-done.8.g1_ref, bf16[680,256]{1,0:T(8,128)(2,1)S(1)} %collective-permute-done.9.g2_ref, ...), custom_call_target="tpu_custom_call" | custom-call | tf_op jit(solution)/shard_map/pallas_call | solution.py:414
  221.3 1.7 shard_map.146
  (62 shorter events, 13.5 us)
Async XLA Ops:
  2.7 22.0 %all-to-all-start = ((bf16[16,24,512]{2,1,0:T(8,128)(2,1)}), bf16[16,24,512]{2,1,0:T(8,128)(2,1)S(1)}, u32[]{:S(2)}, u32[]{:S(2)}) async-start(bf16[16,24,512]{2,1,0:T(8,128)(2,1)} %bitcast.22), calls=%async_computation | async-start | bytes 786432 | tf_op jit(solution)/shard_map/all_to_all | solution.py:424
  25.4 26.3 %copy-start.8 = (bf16[896,256]{1,0:T(8,128)(2,1)S(1)}, bf16[896,256]{1,0:T(8,128)(2,1)}, u32[]{:S(2)}) copy-start(bf16[896,256]{1,0:T(8,128)(2,1)} %down_hbm.3) | copy-start | bytes 1376260
  25.4 26.3 %copy-start.13 = (bf16[256,896]{1,0:T(8,128)(2,1)S(1)}, bf16[256,896]{1,0:T(8,128)(2,1)}, u32[]{:S(2)}) copy-start(bf16[256,896]{1,0:T(8,128)(2,1)} %gate_hbm.1) | copy-start | bytes 1376260
  25.4 26.3 %copy-start.14 = (bf16[256,896]{1,0:T(8,128)(2,1)S(1)}, bf16[256,896]{1,0:T(8,128)(2,1)}, u32[]{:S(2)}) copy-start(bf16[256,896]{1,0:T(8,128)(2,1)} %up_hbm.1) | copy-start | bytes 1376260
  47.0 29.8 %collective-permute-start.3 = (bf16[4,4,88,512]{3,2,1,0:T(8,128)(2,1)S(1)}, bf16[4,4,88,512]{3,2,1,0:T(8,128)(2,1)S(1)}, u32[]{:S(2)}, u32[]{:S(2)}) collective-permute-start(bf16[4,4,88,512]{3,2,1,0:T(8,128)(2,1)S(1)} %all_to_all.20.refs_0_), channel_id=1, source_target_pairs={{0,16},{16,0},{1,17},{17,1},{2,18},{18,2},{3,19},{19,3},{4,20},{20... | collective-permute-start | bytes 4325384 | tf_op jit(solution)/shard_map/ppermute | solution.py:490
  53.7 20.1 %collective-permute-start = (bf16[3,224,256]{2,1,0:T(8,128)(2,1)S(1)}, bf16[3,224,256]{2,1,0:T(8,128)(2,1)S(1)}, u32[]{:S(2)}, u32[]{:S(2)}) collective-permute-start(bf16[3,224,256]{2,1,0:T(8,128)(2,1)S(1)} %get-tuple-element.36), channel_id=1, source_target_pairs={{0,1},{1,2},{2,3},{3,0},{4,5},{5,6},{6,7},{7,4},{8,9},{9,10},{10,1... | collective-permute-start | bytes 1032200 | tf_op jit(solution)/shard_map/ppermute | solution.py:429
  55.6 18.2 %collective-permute-start.1 = (bf16[3,224,256]{2,1,0:T(8,128)(2,1)S(1)}, bf16[3,224,256]{2,1,0:T(8,128)(2,1)S(1)}, u32[]{:S(2)}, u32[]{:S(2)}) collective-permute-start(bf16[3,224,256]{2,1,0:T(8,128)(2,1)S(1)} %get-tuple-element.37), channel_id=1, source_target_pairs={{0,2},{1,3},{2,0},{3,1},{4,6},{5,7},{6,4},{7,5},{8,10},{9,11},{10,... | collective-permute-start | bytes 1032200 | tf_op jit(solution)/shard_map/ppermute | solution.py:429
  59.2 16.7 %collective-permute-start.2 = (bf16[3,224,256]{2,1,0:T(8,128)(2,1)S(1)}, bf16[3,224,256]{2,1,0:T(8,128)(2,1)S(1)}, u32[]{:S(2)}, u32[]{:S(2)}) collective-permute-start(bf16[3,224,256]{2,1,0:T(8,128)(2,1)S(1)} %get-tuple-element.38), channel_id=1, source_target_pairs={{0,3},{1,0},{2,1},{3,2},{4,7},{5,4},{6,5},{7,6},{8,11},{9,8},{10,9... | collective-permute-start | bytes 1032200 | tf_op jit(solution)/shard_map/ppermute | solution.py:429
  73.7 81.0 %copy-start.2 = (bf16[3,224,256]{2,1,0:T(8,128)(2,1)}, bf16[3,224,256]{2,1,0:T(8,128)(2,1)S(1)}, u32[]{:S(2)}) copy-start(bf16[3,224,256]{2,1,0:T(8,128)(2,1)S(1)} %collective-permute-done.w1_ref) | copy-start | bytes 1032196
  73.7 80.9 %copy-start.4 = (bf16[3,224,256]{2,1,0:T(8,128)(2,1)}, bf16[3,224,256]{2,1,0:T(8,128)(2,1)S(1)}, u32[]{:S(2)}) copy-start(bf16[3,224,256]{2,1,0:T(8,128)(2,1)S(1)} %collective-permute-done.1.w2_ref) | copy-start | bytes 1032196
  76.0 78.7 %copy-start.6 = (bf16[3,224,256]{2,1,0:T(8,128)(2,1)}, bf16[3,224,256]{2,1,0:T(8,128)(2,1)S(1)}, u32[]{:S(2)}) copy-start(bf16[3,224,256]{2,1,0:T(8,128)(2,1)S(1)} %collective-permute-done.2.w3_ref) | copy-start | bytes 1032196
  76.7 35.3 %copy-start.21 = (f32[896]{0:T(1024)S(1)}, f32[896]{0:T(1024)}, u32[]{:S(2)}) copy-start(f32[896]{0:T(1024)} %param.13) | copy-start | bytes 10756
  76.8 35.3 %copy-start.22 = (f32[896]{0:T(1024)S(1)}, f32[896]{0:T(1024)}, u32[]{:S(2)}) copy-start(f32[896]{0:T(1024)} %param.14) | copy-start | bytes 10756
  79.1 77.1 %copy-start.15 = (f32[4,8,256]{2,1,0:T(8,128)}, f32[4,8,256]{2,1,0:T(8,128)S(1)}, u32[]{:S(2)}) copy-start(f32[4,8,256]{2,1,0:T(8,128)S(1)} %get-tuple-element.48.refs_3_.rows_ref) | copy-start | bytes 98308
  79.1 24.8 %collective-permute-start.4 = (bf16[176,640]{1,0:T(8,128)(2,1)S(1)}, bf16[176,640]{1,0:T(8,128)(2,1)S(1)}, u32[]{:S(2)}, u32[]{:S(2)}) collective-permute-start(bf16[176,640]{1,0:T(8,128)(2,1)S(1)} %get-tuple-element.42), channel_id=1, source_target_pairs={{0,4},{4,8},{8,12},{12,0},{16,28},{20,16},{24,20},{28,24},{1,5},{5... | collective-permute-start | bytes 675848 | tf_op jit(solution)/shard_map/ppermute | solution.py:440
  88.9 23.2 %collective-permute-start.5 = (bf16[176,640]{1,0:T(8,128)(2,1)S(1)}, bf16[176,640]{1,0:T(8,128)(2,1)S(1)}, u32[]{:S(2)}, u32[]{:S(2)}) collective-permute-start(bf16[176,640]{1,0:T(8,128)(2,1)S(1)} %get-tuple-element.43), channel_id=1, source_target_pairs={{0,12},{4,0},{8,4},{12,8},{16,20},{20,24},{24,28},{28,16},{1,13},{... | collective-permute-start | bytes 675848 | tf_op jit(solution)/shard_map/ppermute | solution.py:440
  104.0 16.7 %collective-permute-start.6 = (bf16[176,640]{1,0:T(8,128)(2,1)S(1)}, bf16[176,640]{1,0:T(8,128)(2,1)S(1)}, u32[]{:S(2)}, u32[]{:S(2)}) collective-permute-start(bf16[176,640]{1,0:T(8,128)(2,1)S(1)} %shard_map.140), channel_id=1, source_target_pairs={{0,4},{4,8},{8,12},{12,0},{16,28},{20,16},{24,20},{28,24},{1,5},{5... | collective-permute-start | bytes 675848 | tf_op jit(solution)/shard_map/ppermute | solution.py:440
  121.8 32.9 %copy-start.18 = (f32[8,640]{1,0:T(8,128)}, f32[8,640]{1,0:T(8,128)S(1)}, u32[]{:S(2)}) copy-start(f32[8,640]{1,0:T(8,128)S(1)} %get-tuple-element.52.refs_3_) | copy-start | bytes 61444
  154.7 1.5 copy-start
  156.2 9.2 %collective-permute-start.7 = (bf16[4,328,256]{2,1,0:T(8,128)(2,1)S(1)}, bf16[4,328,256]{2,1,0:T(8,128)(2,1)S(1)}, u32[]{:S(2)}, u32[]{:S(2)}) collective-permute-start(bf16[4,328,256]{2,1,0:T(8,128)(2,1)S(1)} %get-tuple-element.50), channel_id=1, source_target_pairs={{0,16},{16,0},{1,17},{17,1},{2,18},{18,2},{3,19},{19,3},{4,20},{20... | collective-permute-start | bytes 2015240 | tf_op jit(solution)/shard_map/ppermute | solution.py:517
  180.3 38.5 %all-to-all-start.3 = ((bf16[16,24,256]{2,1,0:T(8,128)(2,1)}), bf16[16,24,256]{2,1,0:T(8,128)(2,1)S(1)}, u32[]{:S(2)}, u32[]{:S(2)}) async-start(bf16[16,24,256]{2,1,0:T(8,128)(2,1)} %bitcast.19), calls=%async_computation.3 | async-start | bytes 393216 | tf_op jit(solution)/shard_map/all_to_all | solution.py:424
  184.1 1.2 copy-start.1
  185.2 1.0 copy-start.3
  186.2 1.0 copy-start.5
  187.2 1.0 copy-start.7
  188.9 30.0 %copy-start.17 = (bf16[20,256]{1,0:T(8,128)(2,1)S(1)}, bf16[20,256]{1,0:T(8,128)(2,1)}, u32[]{:S(2)}) copy-start(bf16[20,256]{1,0:T(8,128)(2,1)} %cotangent_ref.1) | copy-start | bytes 30724
  190.5 28.4 %copy-start.9 = (bf16[896,256]{1,0:T(8,128)(2,1)S(1)}, bf16[896,256]{1,0:T(8,128)(2,1)}, u32[]{:S(2)}) copy-start(bf16[896,256]{1,0:T(8,128)(2,1)} %down_hbm.3) | copy-start | bytes 1376260
  190.5 10.6 %collective-permute-start.8 = (bf16[680,256]{1,0:T(8,128)(2,1)S(1)}, bf16[680,256]{1,0:T(8,128)(2,1)S(1)}, u32[]{:S(2)}, u32[]{:S(2)}) collective-permute-start(bf16[680,256]{1,0:T(8,128)(2,1)S(1)} %get-tuple-element.54), channel_id=1, source_target_pairs={{0,3},{1,0},{2,1},{3,2},{4,7},{5,4},{6,5},{7,6},{8,11},{9,8},{10,9... | collective-permute-start | bytes 1044488 | tf_op jit(solution)/shard_map/ppermute | solution.py:429
  195.1 10.8 %collective-permute-start.9 = (bf16[680,256]{1,0:T(8,128)(2,1)S(1)}, bf16[680,256]{1,0:T(8,128)(2,1)S(1)}, u32[]{:S(2)}, u32[]{:S(2)}) collective-permute-start(bf16[680,256]{1,0:T(8,128)(2,1)S(1)} %get-tuple-element.55), channel_id=1, source_target_pairs={{0,2},{1,3},{2,0},{3,1},{4,6},{5,7},{6,4},{7,5},{8,10},{9,11},{10,... | collective-permute-start | bytes 1044488 | tf_op jit(solution)/shard_map/ppermute | solution.py:429
  197.6 18.2 %collective-permute-start.10 = (bf16[680,256]{1,0:T(8,128)(2,1)S(1)}, bf16[680,256]{1,0:T(8,128)(2,1)S(1)}, u32[]{:S(2)}, u32[]{:S(2)}) collective-permute-start(bf16[680,256]{1,0:T(8,128)(2,1)S(1)} %get-tuple-element.56), channel_id=1, source_target_pairs={{0,1},{1,2},{2,3},{3,0},{4,5},{5,6},{6,7},{7,4},{8,9},{9,10},{10,1... | collective-permute-start | bytes 1044488 | tf_op jit(solution)/shard_map/ppermute | solution.py:429
  218.9 1.0 copy-start.11
  219.8 0.8 copy-start.16
  (4 other events, 2.8 us)
